TPU v7x, 32 devices: a whole 2x2x4 slice. The times are simulated.
32 devices in a mesh: dp: 8 (over z, y), expert: 4 (over x, core).
Axes of the slice: x: 2, y: 2, z: 4, core: 2. Of those that a mesh axis runs over, the one named last changes fastest.
Arguments:
- expert_grads: bfloat16 [8, 4, 1024, 896], P('dp', 'expert'), may hold values from -768 to 768
- round_offsets: int32 [8, 4, 1024], P('dp', 'expert'), may hold values from 0 to 1073741823
- slot_expert: int32 [4], replicated, may hold values from 0 to 3, each once
- master_weight: float32 [4, 1024, 896], P('expert', 'dp'), may hold values from -0.1875 to 0.1875
Outputs:
- mean_grad: float32 [4, 1024, 896], P('expert', 'dp')
- new_weight: float32 [4, 1024, 896], P('expert', 'dp')
- block_step: float32 [4, 8], P('expert', 'dp')
Inputs may be any that keep to these rules, and one draw needn't show every extreme that they name: `slot_expert`: each of 0 to 3 appears once.
All inputs are finite; a program needn't handle non-finite values.
Results may differ from a plain program's by a relative error of at most 0.0003.
Values may be sent and summed in bfloat16 or wider, within the bound.
No kernel may reach another device: no remote copies, remote signals or barrier semaphores. Data moves between devices by JAX's collectives and lax.ppermute only.
A program may use at most 64 MiB of HBM per device.

v0:
```python
import functools
import itertools

import jax
import jax.numpy as jnp
from jax import lax
from jax.experimental import pallas as pl
from jax.experimental.pallas import tpu as pltpu
from jax.sharding import PartitionSpec as P

level_bits = 6
low_power = -30
high_power = 30
learn_rate = 0.05
field_base = 32768
count_shift = 64
square = 4


def power_steps(maxima):
    powers = jnp.array([2.0**exponent for exponent in range(low_power, high_power)], jnp.float32)
    reached = maxima[..., None] >= powers
    doubled = jnp.prod(jnp.where(reached, jnp.float32(2.0), jnp.float32(1.0)), axis=-1)
    return 2.0 ** (low_power - level_bits) * doubled


def dither(element_code):
    mixed = element_code * 747796405 + 1013904223
    mixed = jnp.bitwise_xor(mixed, jnp.right_shift(mixed, 13))
    mixed = mixed * 1103515245
    mixed = jnp.bitwise_xor(mixed, jnp.right_shift(mixed, 16))
    return jnp.bitwise_and(jnp.right_shift(mixed, 12), 255).astype(jnp.float32) / 256.0


def quantize(values, inverse_step, offsets):
    columns = lax.broadcasted_iota(jnp.int32, (1, values.shape[-1]), 1)
    element_code = offsets[..., None] + columns
    scaled = values.astype(jnp.float32) * inverse_step
    floor_part = jnp.floor(scaled)
    return floor_part + jnp.floor(scaled - floor_part + dither(element_code))


def apply_update(mean_grad, master_weight):
    return mean_grad, master_weight - learn_rate * mean_grad


def general_body(expert_grads, round_offsets, slot_expert, master_weight):
    dp_count = lax.axis_size("dp")
    local_grads = expert_grads[0]
    slot_count, row_count, hidden = local_grads.shape
    block_rows = row_count // dp_count
    shaped = local_grads.reshape(slot_count, dp_count, block_rows, hidden)
    maxima = lax.pmax(jnp.max(jnp.abs(shaped), axis=(2, 3)).astype(jnp.float32), "dp")
    all_steps = power_steps(maxima)
    counts = quantize(
        shaped,
        (1.0 / all_steps)[:, :, None, None],
        round_offsets[0].reshape(slot_count, dp_count, block_rows),
    ).astype(jnp.int32).reshape(slot_count, row_count, hidden)
    half = hidden // 2
    words = (counts[:, :, :half] + count_shift) * field_base + (counts[:, :, half:] + count_shift)
    summed = lax.psum_scatter(words, "dp", scatter_dimension=1, tiled=True)
    upper = jnp.right_shift(summed, 15) - count_shift * dp_count
    lower = jnp.bitwise_and(summed, field_base - 1) - count_shift * dp_count
    totals = jnp.concatenate([upper, lower], axis=2)
    step_sizes = lax.dynamic_slice_in_dim(all_steps, lax.axis_index("dp"), 1, 1)
    mean_slot = totals.astype(jnp.float32) * (step_sizes / dp_count)[..., None]
    gathered = lax.all_gather(mean_slot, "expert", axis=0, tiled=True)
    gathered_steps = lax.all_gather(step_sizes, "expert", axis=0, tiled=True)
    wanted = lax.axis_index("expert") * slot_count + lax.broadcasted_iota(
        jnp.int32, (slot_count, 1), 0
    )
    positions = lax.broadcasted_iota(jnp.int32, (1, slot_expert.shape[0]), 1)
    holder = jnp.sum(jnp.where(slot_expert[None, :] == wanted, positions, 0), axis=1)
    mean_grad, new_weight = apply_update(gathered[holder], master_weight)
    return mean_grad, new_weight, gathered_steps[holder]


def flips(count, mask):
    return [(index, index ^ mask) for index in range(count)]


def power_of_two(exponent):
    result = jnp.ones(exponent.shape, jnp.float32)
    size = jnp.abs(exponent)
    for bit in range(6):
        factor = jnp.where(exponent < 0, jnp.float32(2.0 ** -(2**bit)), jnp.float32(2.0 ** (2**bit)))
        result = result * jnp.where((size >> bit) & 1 == 1, factor, jnp.float32(1.0))
    return result


def sum_kernel(far, rows, *refs):
    notes, raws, out, codes = refs[:square], refs[square : 2 * square], refs[-2], refs[-1]
    target = lax.axis_index("dp") ^ (far * square)
    counts = notes[0][2:3, :]
    for note in notes[1:]:
        counts = jnp.maximum(counts, note[2:3, :])
    lanes = lax.broadcasted_iota(jnp.int32, counts.shape, 1)
    reached = jnp.where(lanes == target, counts, 0).astype(jnp.float32)
    exponent = jnp.max(reached, axis=1, keepdims=True).astype(jnp.int32) + (low_power - level_bits)
    inverse_step = power_of_two(-exponent)
    seeds = jnp.concatenate([note[far : far + 1, :] for note in notes] * 2)
    codes[...] = jnp.transpose(seeds) * 747796405 + 1013904223
    height, width = 16, raws[0].shape[1]
    columns = lax.broadcasted_iota(jnp.int32, (1, width), 1) * 747796405

    def step(index, carry):
        span = pl.ds(pl.multiple_of(index * height, height), height)
        total = jnp.zeros((height, width), jnp.float32)
        for near in range(square):
            mixed = codes[span, near : near + 1] + columns
            mixed = jnp.bitwise_xor(mixed, jnp.right_shift(mixed, 13))
            mixed = mixed * 1103515245
            mixed = jnp.bitwise_xor(mixed, jnp.right_shift(mixed, 16))
            noise = jnp.bitwise_and(jnp.right_shift(mixed, 12), 255).astype(jnp.float32) * (1.0 / 256.0)
            scaled = raws[near][span, :].astype(jnp.float32) * inverse_step
            floor_part = jnp.floor(scaled)
            total = total + (floor_part + jnp.floor(scaled - floor_part + noise))
        out[span, :] = total.astype(jnp.bfloat16)
        return carry

    lax.fori_loop(0, rows // height, step, 0)
    if out.shape[0] > rows:
        tail = (out.shape[0] - rows, width)
        out[rows:, :] = jnp.broadcast_to(power_of_two(exponent), tail).astype(jnp.bfloat16)


def sum_counts(far, notes, raws, extra):
    rows, width = raws[0].shape
    whole = pl.BlockSpec(memory_space=pltpu.VMEM)
    return pl.pallas_call(
        functools.partial(sum_kernel, far, rows),
        out_shape=jax.ShapeDtypeStruct((rows + extra, width), jnp.bfloat16),
        in_specs=[whole] * (2 * square),
        out_specs=whole,
        scratch_shapes=[pltpu.VMEM((rows, 2 * square), jnp.int32)],
        cost_estimate=pl.CostEstimate(
            flops=20 * square * rows * width,
            bytes_accessed=2 * (square + 1) * rows * width,
            transcendentals=0,
        ),
        compiler_params=pltpu.CompilerParams(vmem_limit_bytes=8 * 2**20),
        name="sum_far" if far else "sum_near",
    )(*notes, *raws)


def staged_body(expert_grads, round_offsets, slot_expert, master_weight):
    dp_count = lax.axis_size("dp")
    expert_count = lax.axis_size("expert")
    row_count, hidden = expert_grads.shape[2:]
    block_rows = row_count // dp_count
    me = lax.axis_index("dp")
    place = lax.axis_index("expert")
    blocks = expert_grads[0, 0].reshape(dp_count, block_rows, hidden)
    offsets = round_offsets[0, 0].reshape(dp_count, block_rows)

    def pick(array, index):
        return lax.dynamic_index_in_dim(array, index, 0, keepdims=False)

    after = jnp.arange(expert_count)[None, :] > jnp.arange(expert_count)[:, None]
    weights = jnp.array([6, 2, 1, 0], jnp.int32)[:, None]
    lower = (slot_expert[:, None] > slot_expert[None, :]) & after
    branch = jnp.sum(jnp.where(lower, weights, 0))
    peaks = jnp.max(jnp.abs(blocks), axis=(1, 2)).astype(jnp.float32)
    twin = lax.ppermute(peaks, "dp", flips(dp_count, square))
    powers = jnp.array([2.0**power for power in range(low_power, high_power)], jnp.float32)
    reached = jnp.maximum(peaks, twin)[:, None] >= powers
    counts = jnp.sum(reached.astype(jnp.int32), axis=1)
    counts = jnp.pad(counts, (0, block_rows - dp_count))

    raw, notes = [[], []], []
    for near in range(square):
        picked = [(me ^ near) ^ (far * square) for far in range(2)]
        seeds = [pick(offsets, target) for target in picked]
        note = jnp.concatenate([jnp.stack(seeds + [counts]), jnp.zeros((5, block_rows), jnp.int32)])
        rows = [pick(blocks, target) for target in picked]
        if near:
            pairs = flips(dp_count, near)
            note = lax.ppermute(note, "dp", pairs)
            for far in range(2):
                rows[far] = lax.ppermute(rows[far], "dp", pairs)
        notes.append(note)
        for far in range(2):
            raw[far].append(rows[far])

    holder_of = [
        jnp.sum(jnp.where(slot_expert == (place ^ flip), jnp.arange(expert_count), 0))
        for flip in range(expert_count)
    ]
    own = sum_counts(0, notes, raw[0], 0)
    beside = lax.ppermute(own, "expert", flips(expert_count, 1))
    across_wants = jnp.where(holder_of[2] == place, own, beside)
    across = lax.ppermute(across_wants, "expert", flips(expert_count, 2))
    message = sum_counts(1, notes, raw[1], 8)

    def route(order):
        pairs = [
            (block * expert_count + slot, (block ^ square) * expert_count + order[slot])
            for block in range(dp_count)
            for slot in range(expert_count)
        ]
        return lambda parts: lax.ppermute(parts, ("dp", "expert"), pairs)

    orders = itertools.permutations(range(expert_count))
    arrived = lax.switch(branch, [route(order) for order in orders], message)
    mine = holder_of[0]
    near_sum = jnp.where(mine == place, own, jnp.where(mine == (place ^ 1), beside, across))
    totals = near_sum.astype(jnp.float32) + arrived[:block_rows].astype(jnp.float32)
    step = arrived[block_rows, 0].astype(jnp.float32)
    mean_grad, new_weight = apply_update((totals * (step / dp_count))[None], master_weight)
    return mean_grad, new_weight, step.reshape(1, 1)


def solution(mesh):
    staged = mesh.shape["dp"] == 2 * square and mesh.shape["expert"] == 4
    return jax.shard_map(
        staged_body if staged else general_body,
        mesh=mesh,
        in_specs=(
            P("dp", "expert", None, None),
            P("dp", "expert", None),
            P(),
            P("expert", "dp", None),
        ),
        out_specs=(P("expert", "dp", None), P("expert", "dp", None), P("expert", "dp")),
        check_vma=False,
    )
```

profile of v0, /device:TPU:0, one launch (start us, length us, event | category | flops | bytes accessed | tf_op | source)
XLA Modules:
  0.0 67.2 jit_solution(11574031036932028321)
XLA Ops:
  0.7 1.9 %dynamic-slice_bitcast_fusion.4 = (bf16[128,896]{1,0:T(8,128)(2,1)S(1)}, bf16[128,896]{1,0:T(8,128)(2,1)S(1)}, bf16[128,896]{1,0:T(8,128)(2,1)S(1)}, bf16[128,89...) fusion(bf16[8,128,896]{2,1,0:T(8,128)(2,1)} %bitcast.27, ...), kind=kLoop, calls=%fused_computation.9 | loop fusion | bytes 3670048 | tf_op jit(solution)/shard_map/jit(dynamic_index_in_dim)/squeeze | solution.py:158
  2.6 3.1 %collective-permute-start.28 = (bf16[128,896]{1,0:T(8,128)(2,1)S(1)}, bf16[128,896]{1,0:T(8,128)(2,1)S(1)}, u32[]{:S(2)}, u32[]{:S(2)}) collective-permute-start(bf16[128,896]{1,0:T(8,128)(2,1)S(1)} %get-tuple-element.62), channel_id=1, source_target_pairs={{0,4},{4,0},{8,12},{12,8},{16,20},{20,16},{24,28},{28,24},{1,5},{5... | collective-permute-start | bytes 688136 | tf_op jit(solution)/shard_map/ppermute | solution.py:181
  5.6 1.6 %collective-permute-start.29 = (bf16[128,896]{1,0:T(8,128)(2,1)S(1)}, bf16[128,896]{1,0:T(8,128)(2,1)S(1)}, u32[]{:S(2)}, u32[]{:S(2)}) collective-permute-start(bf16[128,896]{1,0:T(8,128)(2,1)S(1)} %get-tuple-element.61), channel_id=1, source_target_pairs={{0,8},{4,12},{8,0},{12,4},{16,24},{20,28},{24,16},{28,20},{1,9},{5... | collective-permute-start | bytes 688136 | tf_op jit(solution)/shard_map/ppermute | solution.py:181
  7.8 3.0 %collective-permute-start.24 = (f32[8]{0:T(128)S(1)}, f32[8]{0:T(128)S(1)}, u32[]{:S(2)}, u32[]{:S(2)}) collective-permute-start(f32[8]{0:T(128)S(1)} %convert_element_type.16), channel_id=1, source_target_pairs={{0,16},{4,20},{8,24},{12,28},{16,0},{20,4},{24,8},{28,12},{1,17},{... | collective-permute-start | bytes 104 | tf_op jit(solution)/shard_map/ppermute | solution.py:165
  10.9 5.8 %collective-permute-done.24 = f32[8]{0:T(128)S(1)} collective-permute-done((f32[8]{0:T(128)S(1)}, f32[8]{0:T(128)S(1)}, u32[]{:S(2)}, u32[]{:S(2)}) %collective-permute-start.24) | collective-permute-done | bytes 64 | tf_op jit(solution)/shard_map/ppermute | solution.py:165
  17.0 0.5 collective-permute-start.25
  17.6 3.5 %collective-permute-start.26 = (s32[8,128]{1,0:T(8,128)S(1)}, s32[8,128]{1,0:T(8,128)S(1)}, u32[]{:S(2)}, u32[]{:S(2)}) collective-permute-start(s32[8,128]{1,0:T(8,128)S(1)} %get-tuple-element.74), channel_id=1, source_target_pairs={{0,8},{4,12},{8,0},{12,4},{16,24},{20,28},{24,16},{28,20},{1,9},{5... | collective-permute-start | bytes 12296 | tf_op jit(solution)/shard_map/ppermute | solution.py:179
  21.0 3.0 %collective-permute-start.27 = (s32[8,128]{1,0:T(8,128)S(1)}, s32[8,128]{1,0:T(8,128)S(1)}, u32[]{:S(2)}, u32[]{:S(2)}) collective-permute-start(s32[8,128]{1,0:T(8,128)S(1)} %get-tuple-element.72), channel_id=1, source_target_pairs={{0,12},{4,8},{8,4},{12,0},{16,28},{20,24},{24,20},{28,16},{1,13},{... | collective-permute-start | bytes 12296 | tf_op jit(solution)/shard_map/ppermute | solution.py:179
  24.1 1.6 %collective-permute-done.27.refs_3_ = s32[8,128]{1,0:T(8,128)S(1)} collective-permute-done((s32[8,128]{1,0:T(8,128)S(1)}, s32[8,128]{1,0:T(8,128)S(1)}, u32[]{:S(2)}, u32[]{:S(2)}) %collective-permute-start.27) | collective-permute-done | bytes 4128 | tf_op jit(solution)/shard_map/ppermute | solution.py:179
  25.7 1.7 %sum_near.1 = bf16[128,896]{1,0:T(8,128)(2,1)S(1)} custom-call(s32[8,128]{1,0:T(8,128)S(1)} %get-tuple-element.75.refs_0_, s32[8,128]{1,0:T(8,128)S(1)} %collective-permute-done.25.refs_1_, s32[8,128]{1,0:T(8,128)S(1)} %collective-permute-done.26.refs_2_, s32[8,128]{1,0:T(8,128)S(1)} %collective-permute-done.27.refs_3_, ...), custom_call_target="tpu_custom_call" | custom-call | flops 9175040 | bytes 1146880 | tf_op jit(solution)/shard_map/sum_near/pallas_call | solution.py:131
  27.4 1.6 %collective-permute-start.33 = (bf16[128,896]{1,0:T(8,128)(2,1)S(1)}, bf16[128,896]{1,0:T(8,128)(2,1)S(1)}, u32[]{:S(2)}, u32[]{:S(2)}) collective-permute-start(bf16[128,896]{1,0:T(8,128)(2,1)S(1)} %get-tuple-element.59), channel_id=1, source_target_pairs={{0,4},{4,0},{8,12},{12,8},{16,20},{20,16},{24,28},{28,24},{1,5},{5... | collective-permute-start | bytes 688136 | tf_op jit(solution)/shard_map/ppermute | solution.py:181
  29.0 2.0 %collective-permute-start.34 = (bf16[128,896]{1,0:T(8,128)(2,1)S(1)}, bf16[128,896]{1,0:T(8,128)(2,1)S(1)}, u32[]{:S(2)}, u32[]{:S(2)}) collective-permute-start(bf16[128,896]{1,0:T(8,128)(2,1)S(1)} %get-tuple-element.58), channel_id=1, source_target_pairs={{0,8},{4,12},{8,0},{12,4},{16,24},{20,28},{24,16},{28,20},{1,9},{5... | collective-permute-start | bytes 688136 | tf_op jit(solution)/shard_map/ppermute | solution.py:181
  31.0 1.0 %collective-permute-start.35 = (bf16[128,896]{1,0:T(8,128)(2,1)S(1)}, bf16[128,896]{1,0:T(8,128)(2,1)S(1)}, u32[]{:S(2)}, u32[]{:S(2)}) collective-permute-start(bf16[128,896]{1,0:T(8,128)(2,1)S(1)} %get-tuple-element.57), channel_id=1, source_target_pairs={{0,12},{4,8},{8,4},{12,0},{16,28},{20,24},{24,20},{28,16},{1,13},{... | collective-permute-start | bytes 688136 | tf_op jit(solution)/shard_map/ppermute | solution.py:181
  31.9 0.6 fusion.6
  33.3 1.6 %collective-permute-start.32 = (bf16[128,896]{1,0:T(8,128)(2,1)S(1)}, bf16[128,896]{1,0:T(8,128)(2,1)S(1)}, u32[]{:S(2)}, u32[]{:S(2)}) collective-permute-start(bf16[128,896]{1,0:T(8,128)(2,1)S(1)} %broadcast_select_fusion), channel_id=1, source_target_pairs={{0,2},{1,3},{2,0},{3,1},{4,6},{5,7},{6,4},{7,5},{8,10},{9,11},{10,... | collective-permute-start | bytes 688136 | tf_op jit(solution)/shard_map/ppermute | solution.py:193
  36.1 0.7 %select_reduce_fusion = s32[]{:T(128)} fusion(s32[4]{0:T(128)S(1)} %copy-done.4, s32[4]{0:T(128)S(1)} %copy-done.2), kind=kLoop, calls=%fused_computation.32 | loop fusion | flops 79 | bytes 36 | tf_op jit(solution)/shard_map/reduce_sum | solution.py:163
  37.5 5.2 %collective-permute-done.35.refs_7_ = bf16[128,896]{1,0:T(8,128)(2,1)S(1)} collective-permute-done((bf16[128,896]{1,0:T(8,128)(2,1)S(1)}, bf16[128,896]{1,0:T(8,128)(2,1)S(1)}, u32[]{:S(2)}, u32[]{:S(2)}) %collective-permute-start.35) | collective-permute-done | bytes 229408 | tf_op jit(solution)/shard_map/ppermute | solution.py:181
  42.8 1.7 %sum_far.1 = bf16[136,896]{1,0:T(8,128)(2,1)S(1)} custom-call(s32[8,128]{1,0:T(8,128)S(1)} %get-tuple-element.75.refs_0_, s32[8,128]{1,0:T(8,128)S(1)} %collective-permute-done.25.refs_1_, s32[8,128]{1,0:T(8,128)S(1)} %collective-permute-done.26.refs_2_, s32[8,128]{1,0:T(8,128)S(1)} %collective-permute-done.27.refs_3_, ...), custom_call_target="tpu_custom_call" | custom-call | flops 9175040 | bytes 1146880 | tf_op jit(solution)/shard_map/sum_far/pallas_call | solution.py:131
  44.5 15.5 %conditional.1 = (bf16[136,896]{1,0:T(8,128)(2,1)}) conditional(s32[]{:T(128)} %clamp.3, bf16[136,896]{1,0:T(8,128)(2,1)S(1)} %sum_far.1, bf16[136,896]{1,0:T(8,128)(2,1)S(1)} %sum_far.1, bf16[136,896]{1,0:T(8,128)(2,1)S(1)} %sum_far.1, bf16[136,896]{1,0:T(8,128)(2,1)S(1)} %sum_far.1, ...), branch_computations={%region_6.7_spmd, %region_7.8_spmd, %region_8.9_spmd, %region_9.10... | conditional | bytes 974896 | solution.py:205
  44.5 1.5 %collective-permute-start.20 = (bf16[136,896]{1,0:T(8,128)(2,1)S(1)}, bf16[136,896]{1,0:T(8,128)(2,1)}, u32[]{:S(2)}, u32[]{:S(2)}) collective-permute-start(bf16[136,896]{1,0:T(8,128)(2,1)S(1)} %param.20), channel_id=1, source_target_pairs={{0,19},{1,17},{2,16},{3,18},{4,23},{5,21},{6,20},{7,22},{8,27},{9,... | collective-permute-start | bytes 731144 | tf_op jit(solution)/shard_map/cond/branch_20_fun/ppermute | solution.py:202
  46.0 13.9 %collective-permute-done.20 = bf16[136,896]{1,0:T(8,128)(2,1)} collective-permute-done((bf16[136,896]{1,0:T(8,128)(2,1)S(1)}, bf16[136,896]{1,0:T(8,128)(2,1)}, u32[]{:S(2)}, u32[]{:S(2)}) %collective-permute-start.20) | collective-permute-done | bytes 243744 | tf_op jit(solution)/shard_map/cond/branch_20_fun/ppermute | solution.py:202
  59.9 1.2 %slice.9 = bf16[1,1]{1,0:T(2,128)(2,1)} slice(bf16[136,896]{1,0:T(8,128)(2,1)} %get-tuple-element.76), slice={[128:129], [0:1]} | slice | bytes 4 | tf_op jit(solution)/shard_map/slice | solution.py:209
  62.4 1.9 %bitcast_subtract_fusion = (f32[1,128,896]{2,1,0:T(8,128)}, bf16[128,896]{1,0:T(8,128)(2,1)S(1)}) fusion(f32[1,128,896]{2,1,0:T(8,128)S(1)} %copy-done.1, f32[]{:T(128)} %bitcast.12, bf16[136,896]{1,0:T(8,128)(2,1)} %get-tuple-element.76, bf16[128,896]{1,0:T(8,128)(2,1)S(1)} %sum_near.1, bf16[128,896]{1,0:T(8,128)(2,1)S(1)} %collective-permute-done.31, ...), kind=kLoop, calls=%fused_computation.1 | loop fusion | flops 917504 | bytes 2064390 | tf_op jit(solution)/shard_map/sub | solution.py:44
  64.3 1.8 %fusion = f32[1,128,896]{2,1,0:T(8,128)} fusion(bf16[128,896]{1,0:T(8,128)(2,1)S(1)} %get-tuple-element.55, f32[]{:T(128)} %bitcast.12, bf16[136,896]{1,0:T(8,128)(2,1)} %get-tuple-element.76), kind=kLoop, calls=%fused_computation.3 | loop fusion | flops 458752 | bytes 917508 | tf_op jit(solution)/shard_map/broadcast_in_dim | solution.py:210
  (34 shorter events, 1.1 us)
Async XLA Ops:
  0.7 6.6 %copy-start = (bf16[1,1,1024,896]{3,2,1,0:T(8,128)(2,1)S(1)}, bf16[1,1,1024,896]{3,2,1,0:T(8,128)(2,1)}, u32[]{:S(2)}) copy-start(bf16[1,1,1024,896]{3,2,1,0:T(8,128)(2,1)} %param.30) | copy-start | bytes 5505028
  2.5 8.3 %copy-start.3 = (s32[1,1,1024]{2,1,0:T(1,128)S(1)}, s32[1,1,1024]{2,1,0:T(1,128)}, u32[]{:S(2)}) copy-start(s32[1,1,1024]{2,1,0:T(1,128)} %param.31) | copy-start | bytes 12292
  2.6 14.2 %copy-start.5 = (f32[60]{0:T(128)S(1)}, f32[60]{0:T(128)}, u32[]{:S(2)}) copy-start(f32[60]{0:T(128)} %constant.72.clone) | copy-start | bytes 724
  2.6 29.4 %copy-start.2 = (s32[4]{0:T(128)S(1)}, s32[4]{0:T(128)}, u32[]{:S(2)}) copy-start(s32[4]{0:T(128)} %param.32) | copy-start | bytes 52
  2.6 23.1 %collective-permute-start.28 = (bf16[128,896]{1,0:T(8,128)(2,1)S(1)}, bf16[128,896]{1,0:T(8,128)(2,1)S(1)}, u32[]{:S(2)}, u32[]{:S(2)}) collective-permute-start(bf16[128,896]{1,0:T(8,128)(2,1)S(1)} %get-tuple-element.62), channel_id=1, source_target_pairs={{0,4},{4,0},{8,12},{12,8},{16,20},{20,16},{24,28},{28,24},{1,5},{5... | collective-permute-start | bytes 688136 | tf_op jit(solution)/shard_map/ppermute | solution.py:181
  5.6 20.0 %collective-permute-start.29 = (bf16[128,896]{1,0:T(8,128)(2,1)S(1)}, bf16[128,896]{1,0:T(8,128)(2,1)S(1)}, u32[]{:S(2)}, u32[]{:S(2)}) collective-permute-start(bf16[128,896]{1,0:T(8,128)(2,1)S(1)} %get-tuple-element.61), channel_id=1, source_target_pairs={{0,8},{4,12},{8,0},{12,4},{16,24},{20,28},{24,16},{28,20},{1,9},{5... | collective-permute-start | bytes 688136 | tf_op jit(solution)/shard_map/ppermute | solution.py:181
  7.2 28.9 %copy-start.4 = (s32[4]{0:T(128)S(1)}, s32[4]{0:T(128)}, u32[]{:S(2)}) copy-start(s32[4]{0:T(128)} %constant.71.clone) | copy-start | bytes 52
  7.2 18.4 %collective-permute-start.30 = (bf16[128,896]{1,0:T(8,128)(2,1)S(1)}, bf16[128,896]{1,0:T(8,128)(2,1)S(1)}, u32[]{:S(2)}, u32[]{:S(2)}) collective-permute-start(bf16[128,896]{1,0:T(8,128)(2,1)S(1)} %get-tuple-element.56), channel_id=1, source_target_pairs={{0,12},{4,8},{8,4},{12,0},{16,28},{20,24},{24,20},{28,16},{1,13},{... | collective-permute-start | bytes 688136 | tf_op jit(solution)/shard_map/ppermute | solution.py:181
  7.7 54.8 %copy-start.1 = (f32[1,128,896]{2,1,0:T(8,128)S(1)}, f32[1,128,896]{2,1,0:T(8,128)}, u32[]{:S(2)}) copy-start(f32[1,128,896]{2,1,0:T(8,128)} %param.33) | copy-start | bytes 1376260
  7.8 9.0 %collective-permute-start.24 = (f32[8]{0:T(128)S(1)}, f32[8]{0:T(128)S(1)}, u32[]{:S(2)}, u32[]{:S(2)}) collective-permute-start(f32[8]{0:T(128)S(1)} %convert_element_type.16), channel_id=1, source_target_pairs={{0,16},{4,20},{8,24},{12,28},{16,0},{20,4},{24,8},{28,12},{1,17},{... | collective-permute-start | bytes 104 | tf_op jit(solution)/shard_map/ppermute | solution.py:165
  17.0 4.0 %collective-permute-start.25 = (s32[8,128]{1,0:T(8,128)S(1)}, s32[8,128]{1,0:T(8,128)S(1)}, u32[]{:S(2)}, u32[]{:S(2)}) collective-permute-start(s32[8,128]{1,0:T(8,128)S(1)} %get-tuple-element.73), channel_id=1, source_target_pairs={{0,4},{4,0},{8,12},{12,8},{16,20},{20,16},{24,28},{28,24},{1,5},{5... | collective-permute-start | bytes 12296 | tf_op jit(solution)/shard_map/ppermute | solution.py:179
  17.6 6.5 %collective-permute-start.26 = (s32[8,128]{1,0:T(8,128)S(1)}, s32[8,128]{1,0:T(8,128)S(1)}, u32[]{:S(2)}, u32[]{:S(2)}) collective-permute-start(s32[8,128]{1,0:T(8,128)S(1)} %get-tuple-element.74), channel_id=1, source_target_pairs={{0,8},{4,12},{8,0},{12,4},{16,24},{20,28},{24,16},{28,20},{1,9},{5... | collective-permute-start | bytes 12296 | tf_op jit(solution)/shard_map/ppermute | solution.py:179
  21.0 4.6 %collective-permute-start.27 = (s32[8,128]{1,0:T(8,128)S(1)}, s32[8,128]{1,0:T(8,128)S(1)}, u32[]{:S(2)}, u32[]{:S(2)}) collective-permute-start(s32[8,128]{1,0:T(8,128)S(1)} %get-tuple-element.72), channel_id=1, source_target_pairs={{0,12},{4,8},{8,4},{12,0},{16,28},{20,24},{24,20},{28,16},{1,13},{... | collective-permute-start | bytes 12296 | tf_op jit(solution)/shard_map/ppermute | solution.py:179
  27.3 5.9 %collective-permute-start.31 = (bf16[128,896]{1,0:T(8,128)(2,1)S(1)}, bf16[128,896]{1,0:T(8,128)(2,1)S(1)}, u32[]{:S(2)}, u32[]{:S(2)}) collective-permute-start(bf16[128,896]{1,0:T(8,128)(2,1)S(1)} %sum_near.1), channel_id=1, source_target_pairs={{0,1},{1,0},{2,3},{3,2},{4,5},{5,4},{6,7},{7,6},{8,9},{9,8},{10,11... | collective-permute-start | bytes 688136 | tf_op jit(solution)/shard_map/ppermute | solution.py:191
  27.4 10.1 %collective-permute-start.33 = (bf16[128,896]{1,0:T(8,128)(2,1)S(1)}, bf16[128,896]{1,0:T(8,128)(2,1)S(1)}, u32[]{:S(2)}, u32[]{:S(2)}) collective-permute-start(bf16[128,896]{1,0:T(8,128)(2,1)S(1)} %get-tuple-element.59), channel_id=1, source_target_pairs={{0,4},{4,0},{8,12},{12,8},{16,20},{20,16},{24,28},{28,24},{1,5},{5... | collective-permute-start | bytes 688136 | tf_op jit(solution)/shard_map/ppermute | solution.py:181
  29.0 8.5 %collective-permute-start.34 = (bf16[128,896]{1,0:T(8,128)(2,1)S(1)}, bf16[128,896]{1,0:T(8,128)(2,1)S(1)}, u32[]{:S(2)}, u32[]{:S(2)}) collective-permute-start(bf16[128,896]{1,0:T(8,128)(2,1)S(1)} %get-tuple-element.58), channel_id=1, source_target_pairs={{0,8},{4,12},{8,0},{12,4},{16,24},{20,28},{24,16},{28,20},{1,9},{5... | collective-permute-start | bytes 688136 | tf_op jit(solution)/shard_map/ppermute | solution.py:181
  31.0 11.8 %collective-permute-start.35 = (bf16[128,896]{1,0:T(8,128)(2,1)S(1)}, bf16[128,896]{1,0:T(8,128)(2,1)S(1)}, u32[]{:S(2)}, u32[]{:S(2)}) collective-permute-start(bf16[128,896]{1,0:T(8,128)(2,1)S(1)} %get-tuple-element.57), channel_id=1, source_target_pairs={{0,12},{4,8},{8,4},{12,0},{16,28},{20,24},{24,20},{28,16},{1,13},{... | collective-permute-start | bytes 688136 | tf_op jit(solution)/shard_map/ppermute | solution.py:181
  33.3 29.1 %collective-permute-start.32 = (bf16[128,896]{1,0:T(8,128)(2,1)S(1)}, bf16[128,896]{1,0:T(8,128)(2,1)S(1)}, u32[]{:S(2)}, u32[]{:S(2)}) collective-permute-start(bf16[128,896]{1,0:T(8,128)(2,1)S(1)} %broadcast_select_fusion), channel_id=1, source_target_pairs={{0,2},{1,3},{2,0},{3,1},{4,6},{5,7},{6,4},{7,5},{8,10},{9,11},{10,... | collective-permute-start | bytes 688136 | tf_op jit(solution)/shard_map/ppermute | solution.py:193
  44.5 15.4 %collective-permute-start.20 = (bf16[136,896]{1,0:T(8,128)(2,1)S(1)}, bf16[136,896]{1,0:T(8,128)(2,1)}, u32[]{:S(2)}, u32[]{:S(2)}) collective-permute-start(bf16[136,896]{1,0:T(8,128)(2,1)S(1)} %param.20), channel_id=1, source_target_pairs={{0,19},{1,17},{2,16},{3,18},{4,23},{5,21},{6,20},{7,22},{8,27},{9,... | collective-permute-start | bytes 731144 | tf_op jit(solution)/shard_map/cond/branch_20_fun/ppermute | solution.py:202
where the time goes:
time: 67.5 us; the launch traced here: 67.2 us
  waiting for transfers between devices  26.6 us (39%)
  starting transfers between devices  22.3 us (33%)
  between operations  5.87 us (9%)
  other arithmetic  5.82 us (9%)
  Pallas kernels  3.38 us (5%)
  local copies, waits for them, and re-layouts  3.17 us (5%)
    ppermute x1, waiting for transfers between devices, route(): return lambda parts: lax.ppermute(parts, ('dp', 'expert'), pairs)  13.9 us
    ppermute x6, starting transfers between devices, staged_body(): rows[far] = lax.ppermute(rows[far], 'dp', pairs)  9.15 us
    ppermute x3, starting transfers between devices, staged_body(): note = lax.ppermute(note, 'dp', pairs)  7.02 us
    ppermute x1, waiting for transfers between devices, staged_body(): twin = lax.ppermute(peaks, 'dp', flips(dp_count, square))  5.82 us
    ppermute x6, waiting for transfers between devices, staged_body(): rows[far] = lax.ppermute(rows[far], 'dp', pairs)  5.26 us
    pallas_call x2, Pallas kernels, sum_counts(): pl.pallas_call(functools.partial(sum_kernel, far, rows), out_shape=jax.Sh...  3.38 us
    ppermute x1, starting transfers between devices, staged_body(): twin = lax.ppermute(peaks, 'dp', flips(dp_count, square))  3.04 us
    sub x1, other arithmetic, apply_update(): return (mean_grad, master_weight - learn_rate * mean_grad)  1.87 us
  transfers between devices with their start and end apart: 13, of which 4 were waited for; matrix products, arithmetic and copies ran while one was open for 5% of the time, Pallas kernels for 3%

commit v1 on v0

--- a/solution.py
+++ b/solution.py
@@ -144,6 +144,47 @@
     )(*notes, *raws)
 
 
+def update_kernel(dp_count, slots, own, beside, across, arrived, weight, mean, updated, step):
+    index = pl.program_id(0)
+    place = lax.axis_index("expert")
+    holder = jnp.int32(0)
+    for slot in range(slots.shape[0]):
+        holder = jnp.where(slots[slot] == place, slot, holder)
+    turn = holder ^ place
+    rows = mean.shape[1]
+    span = pl.ds(pl.multiple_of(index * rows, rows), rows)
+    last = own.shape[0] - arrived.shape[0]
+    tail = pl.ds(arrived.shape[0], last)
+
+    def nearby(where):
+        held, swapped, crossed = (ref[where, :].astype(jnp.float32) for ref in (own, beside, across))
+        return jnp.where(turn == 0, held, jnp.where(turn == 1, swapped, crossed))
+
+    size = nearby(tail)[0:1, :]
+    total = nearby(span) + arrived[span, :].astype(jnp.float32)
+    averaged = total * (size * (1.0 / dp_count))
+    mean[0] = averaged
+    updated[0] = weight[0] - learn_rate * averaged
+    step[...] = size[:, 0:1]
+
+
+def update(slots, own, beside, across, arrived, weight, dp_count):
+    rows, width = arrived.shape
+    parts = 4
+    whole = pl.BlockSpec(memory_space=pltpu.VMEM)
+    strip = pl.BlockSpec((1, rows // parts, width), lambda index: (0, index, 0))
+    block = jax.ShapeDtypeStruct((1, rows, width), jnp.float32)
+    return pl.pallas_call(
+        functools.partial(update_kernel, dp_count),
+        grid=(parts,),
+        out_shape=(block, block, jax.ShapeDtypeStruct((1, 1), jnp.float32)),
+        in_specs=[pl.BlockSpec(memory_space=pltpu.SMEM), whole, whole, whole, whole, strip],
+        out_specs=(strip, strip, pl.BlockSpec((1, 1), lambda index: (0, 0))),
+        compiler_params=pltpu.CompilerParams(vmem_limit_bytes=8 * 2**20),
+        name="update",
+    )(slots, own, beside, across, arrived, weight)
+
+
 def staged_body(expert_grads, round_offsets, slot_expert, master_weight):
     dp_count = lax.axis_size("dp")
     expert_count = lax.axis_size("expert")
@@ -168,12 +209,13 @@
     counts = jnp.sum(reached.astype(jnp.int32), axis=1)
     counts = jnp.pad(counts, (0, block_rows - dp_count))
 
+    later = lax.optimization_barrier(blocks)
     raw, notes = [[], []], []
     for near in range(square):
-        picked = [(me ^ near) ^ (far * square) for far in range(2)]
-        seeds = [pick(offsets, target) for target in picked]
+        targets = [(me ^ near) ^ (far * square) for far in range(2)]
+        seeds = [pick(offsets, target) for target in targets]
         note = jnp.concatenate([jnp.stack(seeds + [counts]), jnp.zeros((5, block_rows), jnp.int32)])
-        rows = [pick(blocks, target) for target in picked]
+        rows = [pick(blocks if near else later, targets[0]), pick(later, targets[1])]
         if near:
             pairs = flips(dp_count, near)
             note = lax.ppermute(note, "dp", pairs)
@@ -183,15 +225,13 @@
         for far in range(2):
             raw[far].append(rows[far])
 
-    holder_of = [
-        jnp.sum(jnp.where(slot_expert == (place ^ flip), jnp.arange(expert_count), 0))
-        for flip in range(expert_count)
-    ]
-    own = sum_counts(0, notes, raw[0], 0)
+    wanted = slot_expert == (place ^ 2)
+    holder = jnp.sum(jnp.where(wanted, jnp.arange(expert_count), 0))
+    own = sum_counts(0, notes, raw[0], 8)
     beside = lax.ppermute(own, "expert", flips(expert_count, 1))
-    across_wants = jnp.where(holder_of[2] == place, own, beside)
+    across_wants = jnp.where(holder == place, own, beside)
     across = lax.ppermute(across_wants, "expert", flips(expert_count, 2))
-    message = sum_counts(1, notes, raw[1], 8)
+    message = sum_counts(1, notes, raw[1], 0)
 
     def route(order):
         pairs = [
@@ -203,12 +243,7 @@
 
     orders = itertools.permutations(range(expert_count))
     arrived = lax.switch(branch, [route(order) for order in orders], message)
-    mine = holder_of[0]
-    near_sum = jnp.where(mine == place, own, jnp.where(mine == (place ^ 1), beside, across))
-    totals = near_sum.astype(jnp.float32) + arrived[:block_rows].astype(jnp.float32)
-    step = arrived[block_rows, 0].astype(jnp.float32)
-    mean_grad, new_weight = apply_update((totals * (step / dp_count))[None], master_weight)
-    return mean_grad, new_weight, step.reshape(1, 1)
+    return update(slot_expert, own, beside, across, arrived, master_weight, dp_count)
 
 
 def solution(mesh):

time: 67.5 us -> 58.2 us (0.86)
  starting transfers between devices: 22.3 us -> 18.4 us
  between operations: 5.87 us -> 2.06 us
  Pallas kernels: 3.38 us -> 5.92 us
  other arithmetic: 5.82 us -> 3.82 us
  local copies, waits for them, and re-layouts: 3.17 us -> 1.81 us
  waiting for transfers between devices: 26.6 us -> 25.9 us
    ppermute x1, waiting for transfers between devices: 5.82 us -> 0.01 us  [staged_body(): twin = lax.ppermute(peaks, 'dp', flips(dp_count, square))]
    ppermute x6, waiting for transfers between devices: 5.26 us -> 8.79 us  [staged_body(): rows[far] = lax.ppermute(rows[far], 'dp', pairs)]
    pallas_call x0 -> x1, Pallas kernels: none -> 2.54 us  [update(): pl.pallas_call(functools.partial(update_kernel, dp_count), grid=(parts,),...]
    ppermute x6, starting transfers between devices: 9.15 us -> 6.98 us  [staged_body(): rows[far] = lax.ppermute(rows[far], 'dp', pairs)]
    sub x1 -> x0, other arithmetic: 1.87 us -> none  [apply_update(): return (mean_grad, master_weight - learn_rate * mean_grad)]
    broadcast_in_dim x1 -> x0, other arithmetic: 1.77 us -> none  [staged_body(): (totals * (step / dp_count))[None]]
    reduce_max x2, other arithmetic: 0.56 us -> 2.19 us  [staged_body(): peaks = jnp.max(jnp.abs(blocks), axis=(1, 2)).astype(jnp.float32)]
    ppermute x3, waiting for transfers between devices: 1.59 us -> 3.18 us  [staged_body(): note = lax.ppermute(note, 'dp', pairs)]
  transfers between devices with their start and end apart: 13 -> 13, of which waited for: 4 -> 7; matrix products, arithmetic and copies ran while one was open for 5% -> 6% of each run, Pallas kernels for 3% -> 3%
where the time goes in v1:
time: 58.2 us; the launch traced here: 58 us
  waiting for transfers between devices  25.9 us (45%)
  starting transfers between devices  18.4 us (32%)
  Pallas kernels  5.92 us (10%)
  other arithmetic  3.82 us (7%)
  between operations  2.06 us (4%)
  local copies, waits for them, and re-layouts  1.81 us (3%)
    ppermute x1, waiting for transfers between devices, route(): return lambda parts: lax.ppermute(parts, ('dp', 'expert'), pairs)  13.8 us
    ppermute x6, waiting for transfers between devices, staged_body(): rows[far] = lax.ppermute(rows[far], 'dp', pairs)  8.79 us
    ppermute x6, starting transfers between devices, staged_body(): rows[far] = lax.ppermute(rows[far], 'dp', pairs)  6.98 us
    ppermute x3, starting transfers between devices, staged_body(): note = lax.ppermute(note, 'dp', pairs)  5.64 us
    ppermute x1, starting transfers between devices, staged_body(): twin = lax.ppermute(peaks, 'dp', flips(dp_count, square))  4.13 us
    pallas_call x2, Pallas kernels, sum_counts(): pl.pallas_call(functools.partial(sum_kernel, far, rows), out_shape=jax.Sh...  3.38 us
    ppermute x3, waiting for transfers between devices, staged_body(): note = lax.ppermute(note, 'dp', pairs)  3.18 us
    pallas_call x1, Pallas kernels, update(): pl.pallas_call(functools.partial(update_kernel, dp_count), grid=(parts,),...  2.54 us
  transfers between devices with their start and end apart: 13, of which 7 were waited for; matrix products, arithmetic and copies ran while one was open for 6% of the time, Pallas kernels for 3%

profile of v1, /device:TPU:0, one launch (start us, length us, event | category | flops | bytes accessed | tf_op | source)
XLA Modules:
  0.0 58.0 jit_solution(17654801284952611320)
XLA Ops:
  0.7 2.1 %abs_reduce_fusion = bf16[1024]{0:T(1024)(128)(2,1)S(1)} fusion(bf16[1,1,1024,896]{3,2,1,0:T(8,128)(2,1)} %param.30), kind=kLoop, calls=%fused_computation | loop fusion | flops 1833984 | bytes 1837056 | tf_op jit(solution)/shard_map/reduce_max | solution.py:205
  2.9 4.1 %collective-permute-start.24 = (f32[8]{0:T(128)S(1)}, f32[8]{0:T(128)S(1)}, u32[]{:S(2)}, u32[]{:S(2)}) collective-permute-start(f32[8]{0:T(128)S(1)} %convert_element_type.6), channel_id=1, source_target_pairs={{0,16},{4,20},{8,24},{12,28},{16,0},{20,4},{24,8},{28,12},{1,17},{... | collective-permute-start | bytes 104 | tf_op jit(solution)/shard_map/ppermute | solution.py:206
  7.0 0.8 %dynamic-slice_bitcast_fusion.4 = (bf16[128,896]{1,0:T(8,128)(2,1)S(1)}, bf16[128,896]{1,0:T(8,128)(2,1)}, bf16[128,896]{1,0:T(8,128)(2,1)}) fusion(bf16[8,128,896]{2,1,0:T(8,128)(2,1)S(1)} %bitcast.22, s32[]{:T(128)S(6)} %select_n.56, s32[]{:T(128)S(6)} %select_n.54, s32[]{:T(128)S(6)} %select_n.52), kind=kLoop, calls=%fused_computation.6 | loop fusion | bytes 1376268 | tf_op jit(solution)/shard_map/jit(dynamic_index_in_dim)/squeeze | solution.py:199
  7.8 1.5 %collective-permute-start.28 = (bf16[128,896]{1,0:T(8,128)(2,1)}, bf16[128,896]{1,0:T(8,128)(2,1)S(1)}, u32[]{:S(2)}, u32[]{:S(2)}) collective-permute-start(bf16[128,896]{1,0:T(8,128)(2,1)} %get-tuple-element.59), channel_id=1, source_target_pairs={{0,4},{4,0},{8,12},{12,8},{16,20},{20,16},{24,28},{28,24},{1,5},{5... | collective-permute-start | bytes 688136 | tf_op jit(solution)/shard_map/ppermute | solution.py:223
  9.3 1.6 %collective-permute-start.29 = (bf16[128,896]{1,0:T(8,128)(2,1)}, bf16[128,896]{1,0:T(8,128)(2,1)S(1)}, u32[]{:S(2)}, u32[]{:S(2)}) collective-permute-start(bf16[128,896]{1,0:T(8,128)(2,1)} %get-tuple-element.58), channel_id=1, source_target_pairs={{0,8},{4,12},{8,0},{12,4},{16,24},{20,28},{24,16},{28,20},{1,9},{5... | collective-permute-start | bytes 688136 | tf_op jit(solution)/shard_map/ppermute | solution.py:223
  11.7 1.5 %collective-permute-start.25 = (s32[8,128]{1,0:T(8,128)S(1)}, s32[8,128]{1,0:T(8,128)S(1)}, u32[]{:S(2)}, u32[]{:S(2)}) collective-permute-start(s32[8,128]{1,0:T(8,128)S(1)} %get-tuple-element.69), channel_id=1, source_target_pairs={{0,4},{4,0},{8,12},{12,8},{16,20},{20,16},{24,28},{28,24},{1,5},{5... | collective-permute-start | bytes 12296 | tf_op jit(solution)/shard_map/ppermute | solution.py:221
  13.2 1.6 %collective-permute-start.26 = (s32[8,128]{1,0:T(8,128)S(1)}, s32[8,128]{1,0:T(8,128)S(1)}, u32[]{:S(2)}, u32[]{:S(2)}) collective-permute-start(s32[8,128]{1,0:T(8,128)S(1)} %get-tuple-element.70), channel_id=1, source_target_pairs={{0,8},{4,12},{8,0},{12,4},{16,24},{20,28},{24,16},{28,20},{1,9},{5... | collective-permute-start | bytes 12296 | tf_op jit(solution)/shard_map/ppermute | solution.py:221
  14.8 1.0 %collective-permute-done.25.refs_1_ = s32[8,128]{1,0:T(8,128)S(1)} collective-permute-done((s32[8,128]{1,0:T(8,128)S(1)}, s32[8,128]{1,0:T(8,128)S(1)}, u32[]{:S(2)}, u32[]{:S(2)}) %collective-permute-start.25) | collective-permute-done | bytes 4128 | tf_op jit(solution)/shard_map/ppermute | solution.py:221
  15.8 2.5 %collective-permute-start.27 = (s32[8,128]{1,0:T(8,128)S(1)}, s32[8,128]{1,0:T(8,128)S(1)}, u32[]{:S(2)}, u32[]{:S(2)}) collective-permute-start(s32[8,128]{1,0:T(8,128)S(1)} %get-tuple-element.68), channel_id=1, source_target_pairs={{0,12},{4,8},{8,4},{12,0},{16,28},{20,24},{24,20},{28,16},{1,13},{... | collective-permute-start | bytes 12296 | tf_op jit(solution)/shard_map/ppermute | solution.py:221
  18.3 0.8 %dynamic-slice_bitcast_fusion = (bf16[128,896]{1,0:T(8,128)(2,1)}, bf16[128,896]{1,0:T(8,128)(2,1)}, bf16[128,896]{1,0:T(8,128)(2,1)}, bf16[128,896]{1,0:T(8,128)(2,1)S(1)}, bf16[128,896]{1,0:T(8,128)(2,1)S(1)}) fusion(bf16[8,128,896]{2,1,0:T(8,128)(2,1)S(1)} %bitcast.23, s32[]{:T(128)S(6)} %select_n.57, s32[]{:T(128)S(6)} %select_n.55, s32[]{:T(128)S(6)} %select_n.53, ...), kind=kLoop, calls=%fused_computation.2 | loop fusion | bytes 2293780 | tf_op jit(solution)/shard_map/jit(dynamic_index_in_dim)/squeeze | solution.py:199
  19.2 2.2 %collective-permute-done.26.refs_2_ = s32[8,128]{1,0:T(8,128)S(1)} collective-permute-done((s32[8,128]{1,0:T(8,128)S(1)}, s32[8,128]{1,0:T(8,128)S(1)}, u32[]{:S(2)}, u32[]{:S(2)}) %collective-permute-start.26) | collective-permute-done | bytes 4128 | tf_op jit(solution)/shard_map/ppermute | solution.py:221
  21.4 1.7 %sum_near.1.own = bf16[136,896]{1,0:T(8,128)(2,1)S(1)} custom-call(s32[8,128]{1,0:T(8,128)S(1)} %get-tuple-element.71.refs_0_, s32[8,128]{1,0:T(8,128)S(1)} %collective-permute-done.25.refs_1_, s32[8,128]{1,0:T(8,128)S(1)} %collective-permute-done.26.refs_2_, s32[8,128]{1,0:T(8,128)S(1)} %collective-permute-done.27.refs_3_, ...), custom_call_target="tpu_custom_call" | custom-call | flops 9175040 | bytes 1146880 | tf_op jit(solution)/shard_map/sum_near/pallas_call | solution.py:131
  23.2 0.6 %fusion.5 = s32[]{:T(128)} fusion(s32[4]{0:T(128)S(1)} %copy-done.1, s32[]{:T(128)S(6)} %xor.34), kind=kLoop, calls=%fused_computation.32 | loop fusion | flops 11 | bytes 24 | tf_op jit(solution)/shard_map/reduce_sum | solution.py:229
  24.7 1.6 %collective-permute-start.32 = (bf16[136,896]{1,0:T(8,128)(2,1)S(1)}, bf16[136,896]{1,0:T(8,128)(2,1)S(1)}, u32[]{:S(2)}, u32[]{:S(2)}) collective-permute-start(bf16[136,896]{1,0:T(8,128)(2,1)S(1)} %broadcast_select_fusion), channel_id=1, source_target_pairs={{0,2},{1,3},{2,0},{3,1},{4,6},{5,7},{6,4},{7,5},{8,10},{9,11},{10,... | collective-permute-start | bytes 731144 | tf_op jit(solution)/shard_map/ppermute | solution.py:233
  26.3 1.5 %collective-permute-start.33 = (bf16[128,896]{1,0:T(8,128)(2,1)S(1)}, bf16[128,896]{1,0:T(8,128)(2,1)S(1)}, u32[]{:S(2)}, u32[]{:S(2)}) collective-permute-start(bf16[128,896]{1,0:T(8,128)(2,1)S(1)} %copy-done.5), channel_id=1, source_target_pairs={{0,4},{4,0},{8,12},{12,8},{16,20},{20,16},{24,28},{28,24},{1,5},{5... | collective-permute-start | bytes 688136 | tf_op jit(solution)/shard_map/ppermute | solution.py:223
  27.8 1.6 %collective-permute-start.34 = (bf16[128,896]{1,0:T(8,128)(2,1)S(1)}, bf16[128,896]{1,0:T(8,128)(2,1)S(1)}, u32[]{:S(2)}, u32[]{:S(2)}) collective-permute-start(bf16[128,896]{1,0:T(8,128)(2,1)S(1)} %copy-done.4), channel_id=1, source_target_pairs={{0,8},{4,12},{8,0},{12,4},{16,24},{20,28},{24,16},{28,20},{1,9},{5... | collective-permute-start | bytes 688136 | tf_op jit(solution)/shard_map/ppermute | solution.py:223
  29.8 0.7 %select_reduce_fusion = s32[]{:T(128)} fusion(s32[4]{0:T(128)S(1)} %copy-done.7, s32[4]{0:T(128)S(1)} %copy-done.1), kind=kLoop, calls=%fused_computation.28 | loop fusion | flops 79 | bytes 36 | tf_op jit(solution)/shard_map/reduce_sum | solution.py:204
  31.1 2.7 %collective-permute-done.33.refs_5_ = bf16[128,896]{1,0:T(8,128)(2,1)S(1)} collective-permute-done((bf16[128,896]{1,0:T(8,128)(2,1)S(1)}, bf16[128,896]{1,0:T(8,128)(2,1)S(1)}, u32[]{:S(2)}, u32[]{:S(2)}) %collective-permute-start.33) | collective-permute-done | bytes 229408 | tf_op jit(solution)/shard_map/ppermute | solution.py:223
  33.8 2.4 %collective-permute-done.34.refs_6_ = bf16[128,896]{1,0:T(8,128)(2,1)S(1)} collective-permute-done((bf16[128,896]{1,0:T(8,128)(2,1)S(1)}, bf16[128,896]{1,0:T(8,128)(2,1)S(1)}, u32[]{:S(2)}, u32[]{:S(2)}) %collective-permute-start.34) | collective-permute-done | bytes 229408 | tf_op jit(solution)/shard_map/ppermute | solution.py:223
  36.3 3.7 %collective-permute-done.35.refs_7_ = bf16[128,896]{1,0:T(8,128)(2,1)S(1)} collective-permute-done((bf16[128,896]{1,0:T(8,128)(2,1)S(1)}, bf16[128,896]{1,0:T(8,128)(2,1)S(1)}, u32[]{:S(2)}, u32[]{:S(2)}) %collective-permute-start.35) | collective-permute-done | bytes 229408 | tf_op jit(solution)/shard_map/ppermute | solution.py:223
  39.9 1.7 %sum_far.1 = bf16[128,896]{1,0:T(8,128)(2,1)S(1)} custom-call(s32[8,128]{1,0:T(8,128)S(1)} %get-tuple-element.71.refs_0_, s32[8,128]{1,0:T(8,128)S(1)} %collective-permute-done.25.refs_1_, s32[8,128]{1,0:T(8,128)S(1)} %collective-permute-done.26.refs_2_, s32[8,128]{1,0:T(8,128)S(1)} %collective-permute-done.27.refs_3_, ...), custom_call_target="tpu_custom_call" | custom-call | flops 9175040 | bytes 1146880 | tf_op jit(solution)/shard_map/sum_far/pallas_call | solution.py:131
  41.6 13.9 %conditional.1 = (bf16[128,896]{1,0:T(8,128)(2,1)}) conditional(s32[]{:T(128)} %clamp.3, bf16[128,896]{1,0:T(8,128)(2,1)S(1)} %sum_far.1, bf16[128,896]{1,0:T(8,128)(2,1)S(1)} %sum_far.1, bf16[128,896]{1,0:T(8,128)(2,1)S(1)} %sum_far.1, bf16[128,896]{1,0:T(8,128)(2,1)S(1)} %sum_far.1, ...), branch_computations={%region_5.6_spmd, %region_6.7_spmd, %region_7.8_spmd, %region_8.9_... | conditional | bytes 917552 | solution.py:245
  41.7 13.8 %collective-permute-done.20 = bf16[128,896]{1,0:T(8,128)(2,1)} collective-permute-done((bf16[128,896]{1,0:T(8,128)(2,1)S(1)}, bf16[128,896]{1,0:T(8,128)(2,1)}, u32[]{:S(2)}, u32[]{:S(2)}) %collective-permute-start.20) | collective-permute-done | bytes 229408 | tf_op jit(solution)/shard_map/cond/branch_20_fun/ppermute | solution.py:242
  55.5 2.5 %update.1 = (f32[1,128,896]{2,1,0:T(8,128)}, f32[1,128,896]{2,1,0:T(8,128)}, f32[1,1]{1,0:T(1,128)}) custom-call(s32[4]{0:T(128)S(1)} %copy-done.1, bf16[136,896]{1,0:T(8,128)(2,1)S(1)} %sum_near.1.own, bf16[136,896]{1,0:T(8,128)(2,1)S(1)} %collective-permute-done.31.beside, bf16[136,896]{1,0:T(8,128)(2,1)S(1)} %collective-permute-done.32.across, ...), custom_call_target="tpu_custom_call" | custom-call | tf_op jit(solution)/shard_map/update/pallas_call | solution.py:177
  (39 shorter events, 1.7 us)
Async XLA Ops:
  0.6 10.8 %copy-start.8 = (f32[60]{0:T(128)S(1)}, f32[60]{0:T(128)}, u32[]{:S(2)}) copy-start(f32[60]{0:T(128)} %constant.66.clone) | copy-start | bytes 724
  0.6 6.3 %copy-start.2 = (bf16[1,1,1024,896]{3,2,1,0:T(8,128)(2,1)S(1)}, bf16[1,1,1024,896]{3,2,1,0:T(8,128)(2,1)}, u32[]{:S(2)}) copy-start(bf16[1,1,1024,896]{3,2,1,0:T(8,128)(2,1)} %param.30) | copy-start | bytes 5505028
  0.7 10.7 %copy-start.6 = (s32[1,1,1024]{2,1,0:T(1,128)S(1)}, s32[1,1,1024]{2,1,0:T(1,128)}, u32[]{:S(2)}) copy-start(s32[1,1,1024]{2,1,0:T(1,128)} %param.31) | copy-start | bytes 12292
  2.9 8.6 %collective-permute-start.24 = (f32[8]{0:T(128)S(1)}, f32[8]{0:T(128)S(1)}, u32[]{:S(2)}, u32[]{:S(2)}) collective-permute-start(f32[8]{0:T(128)S(1)} %convert_element_type.6), channel_id=1, source_target_pairs={{0,16},{4,20},{8,24},{12,28},{16,0},{20,4},{24,8},{28,12},{1,17},{... | collective-permute-start | bytes 104 | tf_op jit(solution)/shard_map/ppermute | solution.py:206
  7.8 15.4 %copy-start.1 = (s32[4]{0:T(128)S(1)}, s32[4]{0:T(128)}, u32[]{:S(2)}) copy-start(s32[4]{0:T(128)} %slots.1) | copy-start | bytes 52
  7.8 13.6 %collective-permute-start.28 = (bf16[128,896]{1,0:T(8,128)(2,1)}, bf16[128,896]{1,0:T(8,128)(2,1)S(1)}, u32[]{:S(2)}, u32[]{:S(2)}) collective-permute-start(bf16[128,896]{1,0:T(8,128)(2,1)} %get-tuple-element.59), channel_id=1, source_target_pairs={{0,4},{4,0},{8,12},{12,8},{16,20},{20,16},{24,28},{28,24},{1,5},{5... | collective-permute-start | bytes 688136 | tf_op jit(solution)/shard_map/ppermute | solution.py:223
  9.3 12.1 %collective-permute-start.29 = (bf16[128,896]{1,0:T(8,128)(2,1)}, bf16[128,896]{1,0:T(8,128)(2,1)S(1)}, u32[]{:S(2)}, u32[]{:S(2)}) collective-permute-start(bf16[128,896]{1,0:T(8,128)(2,1)} %get-tuple-element.58), channel_id=1, source_target_pairs={{0,8},{4,12},{8,0},{12,4},{16,24},{20,28},{24,16},{28,20},{1,9},{5... | collective-permute-start | bytes 688136 | tf_op jit(solution)/shard_map/ppermute | solution.py:223
  10.9 10.5 %collective-permute-start.30 = (bf16[128,896]{1,0:T(8,128)(2,1)S(1)}, bf16[128,896]{1,0:T(8,128)(2,1)S(1)}, u32[]{:S(2)}, u32[]{:S(2)}) collective-permute-start(bf16[128,896]{1,0:T(8,128)(2,1)S(1)} %get-tuple-element.57), channel_id=1, source_target_pairs={{0,12},{4,8},{8,4},{12,0},{16,28},{20,24},{24,20},{28,16},{1,13},{... | collective-permute-start | bytes 688136 | tf_op jit(solution)/shard_map/ppermute | solution.py:223
  11.7 4.1 %collective-permute-start.25 = (s32[8,128]{1,0:T(8,128)S(1)}, s32[8,128]{1,0:T(8,128)S(1)}, u32[]{:S(2)}, u32[]{:S(2)}) collective-permute-start(s32[8,128]{1,0:T(8,128)S(1)} %get-tuple-element.69), channel_id=1, source_target_pairs={{0,4},{4,0},{8,12},{12,8},{16,20},{20,16},{24,28},{28,24},{1,5},{5... | collective-permute-start | bytes 12296 | tf_op jit(solution)/shard_map/ppermute | solution.py:221
  13.2 8.1 %collective-permute-start.26 = (s32[8,128]{1,0:T(8,128)S(1)}, s32[8,128]{1,0:T(8,128)S(1)}, u32[]{:S(2)}, u32[]{:S(2)}) collective-permute-start(s32[8,128]{1,0:T(8,128)S(1)} %get-tuple-element.70), channel_id=1, source_target_pairs={{0,8},{4,12},{8,0},{12,4},{16,24},{20,28},{24,16},{28,20},{1,9},{5... | collective-permute-start | bytes 12296 | tf_op jit(solution)/shard_map/ppermute | solution.py:221
  15.8 14.0 %copy-start.7 = (s32[4]{0:T(128)S(1)}, s32[4]{0:T(128)}, u32[]{:S(2)}) copy-start(s32[4]{0:T(128)} %constant.65.clone) | copy-start | bytes 52
  15.8 5.6 %collective-permute-start.27 = (s32[8,128]{1,0:T(8,128)S(1)}, s32[8,128]{1,0:T(8,128)S(1)}, u32[]{:S(2)}, u32[]{:S(2)}) collective-permute-start(s32[8,128]{1,0:T(8,128)S(1)} %get-tuple-element.68), channel_id=1, source_target_pairs={{0,12},{4,8},{8,4},{12,0},{16,28},{20,24},{24,20},{28,16},{1,13},{... | collective-permute-start | bytes 12296 | tf_op jit(solution)/shard_map/ppermute | solution.py:221
  19.2 7.1 %copy-start.5 = (bf16[128,896]{1,0:T(8,128)(2,1)S(1)}, bf16[128,896]{1,0:T(8,128)(2,1)}, u32[]{:S(2)}) copy-start(bf16[128,896]{1,0:T(8,128)(2,1)} %get-tuple-element.54) | copy-start | bytes 688132
  19.2 8.6 %copy-start.4 = (bf16[128,896]{1,0:T(8,128)(2,1)S(1)}, bf16[128,896]{1,0:T(8,128)(2,1)}, u32[]{:S(2)}) copy-start(bf16[128,896]{1,0:T(8,128)(2,1)} %get-tuple-element.53) | copy-start | bytes 688132
  19.2 10.2 %copy-start.3 = (bf16[128,896]{1,0:T(8,128)(2,1)S(1)}, bf16[128,896]{1,0:T(8,128)(2,1)}, u32[]{:S(2)}) copy-start(bf16[128,896]{1,0:T(8,128)(2,1)} %get-tuple-element.52) | copy-start | bytes 688132
  19.2 36.3 %copy-start = (f32[1,128,896]{2,1,0:T(8,128)S(1)}, f32[1,128,896]{2,1,0:T(8,128)}, u32[]{:S(2)}) copy-start(f32[1,128,896]{2,1,0:T(8,128)} %weight.1) | copy-start | bytes 1376260
  23.1 1.6 %collective-permute-start.31 = (bf16[136,896]{1,0:T(8,128)(2,1)S(1)}, bf16[136,896]{1,0:T(8,128)(2,1)S(1)}, u32[]{:S(2)}, u32[]{:S(2)}) collective-permute-start(bf16[136,896]{1,0:T(8,128)(2,1)S(1)} %sum_near.1.own), channel_id=1, source_target_pairs={{0,1},{1,0},{2,3},{3,2},{4,5},{5,4},{6,7},{7,6},{8,9},{9,8},{10,11... | collective-permute-start | bytes 731144 | tf_op jit(solution)/shard_map/ppermute | solution.py:231
  24.7 30.8 %collective-permute-start.32 = (bf16[136,896]{1,0:T(8,128)(2,1)S(1)}, bf16[136,896]{1,0:T(8,128)(2,1)S(1)}, u32[]{:S(2)}, u32[]{:S(2)}) collective-permute-start(bf16[136,896]{1,0:T(8,128)(2,1)S(1)} %broadcast_select_fusion), channel_id=1, source_target_pairs={{0,2},{1,3},{2,0},{3,1},{4,6},{5,7},{6,4},{7,5},{8,10},{9,11},{10,... | collective-permute-start | bytes 731144 | tf_op jit(solution)/shard_map/ppermute | solution.py:233
  26.3 7.6 %collective-permute-start.33 = (bf16[128,896]{1,0:T(8,128)(2,1)S(1)}, bf16[128,896]{1,0:T(8,128)(2,1)S(1)}, u32[]{:S(2)}, u32[]{:S(2)}) collective-permute-start(bf16[128,896]{1,0:T(8,128)(2,1)S(1)} %copy-done.5), channel_id=1, source_target_pairs={{0,4},{4,0},{8,12},{12,8},{16,20},{20,16},{24,28},{28,24},{1,5},{5... | collective-permute-start | bytes 688136 | tf_op jit(solution)/shard_map/ppermute | solution.py:223
  27.8 8.5 %collective-permute-start.34 = (bf16[128,896]{1,0:T(8,128)(2,1)S(1)}, bf16[128,896]{1,0:T(8,128)(2,1)S(1)}, u32[]{:S(2)}, u32[]{:S(2)}) collective-permute-start(bf16[128,896]{1,0:T(8,128)(2,1)S(1)} %copy-done.4), channel_id=1, source_target_pairs={{0,8},{4,12},{8,0},{12,4},{16,24},{20,28},{24,16},{28,20},{1,9},{5... | collective-permute-start | bytes 688136 | tf_op jit(solution)/shard_map/ppermute | solution.py:223
  29.4 10.6 %collective-permute-start.35 = (bf16[128,896]{1,0:T(8,128)(2,1)S(1)}, bf16[128,896]{1,0:T(8,128)(2,1)S(1)}, u32[]{:S(2)}, u32[]{:S(2)}) collective-permute-start(bf16[128,896]{1,0:T(8,128)(2,1)S(1)} %copy-done.3), channel_id=1, source_target_pairs={{0,12},{4,8},{8,4},{12,0},{16,28},{20,24},{24,20},{28,16},{1,13},{... | collective-permute-start | bytes 688136 | tf_op jit(solution)/shard_map/ppermute | solution.py:223
  41.6 13.9 %collective-permute-start.20 = (bf16[128,896]{1,0:T(8,128)(2,1)S(1)}, bf16[128,896]{1,0:T(8,128)(2,1)}, u32[]{:S(2)}, u32[]{:S(2)}) collective-permute-start(bf16[128,896]{1,0:T(8,128)(2,1)S(1)} %param.20), channel_id=1, source_target_pairs={{0,19},{1,17},{2,16},{3,18},{4,23},{5,21},{6,20},{7,22},{8,27},{9,... | collective-permute-start | bytes 688136 | tf_op jit(solution)/shard_map/cond/branch_20_fun/ppermute | solution.py:242

commit v2 on v1

--- a/solution.py
+++ b/solution.py
@@ -89,8 +89,116 @@
     return result
 
 
+def block_at(grads, target, rows):
+    return grads.at[0, 0, pl.ds(pl.multiple_of(target * rows, rows), rows), :]
+
+
+def largest(ref):
+    height = 16
+    best = jnp.abs(ref[0:height, :])
+    for row in range(height, ref.shape[0], height):
+        best = jnp.maximum(best, jnp.abs(ref[row : row + height, :]))
+    best = jnp.max(best.astype(jnp.float32), axis=0, keepdims=True)
+    return jnp.max(best, axis=1, keepdims=True)
+
+
+def first_kernel(grads, *refs):
+    outs, sems = refs[:-1], refs[-1]
+    me = lax.axis_index("dp")
+    copies = []
+    for near in range(1, square):
+        out = outs[near - 1]
+        copy = pltpu.make_async_copy(block_at(grads, me ^ near, out.shape[0]), out, sems.at[near - 1])
+        copy.start()
+        copies.append(copy)
+    for copy in copies:
+        copy.wait()
+
+
+def second_kernel(grads, *refs):
+    given, outs, levels, sems = refs[: square - 1], refs[square - 1 : -2], refs[-2], refs[-1]
+    me = lax.axis_index("dp")
+    targets = [me] + [me ^ square ^ near for near in range(square)]
+    copies = []
+    for number, target in enumerate(targets):
+        out = outs[number]
+        copy = pltpu.make_async_copy(block_at(grads, target, out.shape[0]), out, sems.at[number])
+        copy.start()
+        copies.append(copy)
+    lanes = lax.broadcasted_iota(jnp.int32, levels.shape, 1)
+    peaks = jnp.zeros(levels.shape, jnp.float32)
+    for near in range(1, square):
+        peaks = jnp.where(lanes == (me ^ near), largest(given[near - 1]), peaks)
+    for number, target in enumerate(targets):
+        copies[number].wait()
+        peaks = jnp.where(lanes == target, largest(outs[number]), peaks)
+    counts = [jnp.zeros(levels.shape, jnp.int32) for _ in range(4)]
+    for power in range(low_power, high_power):
+        counts[power % 4] += (peaks >= jnp.float32(2.0**power)).astype(jnp.int32)
+    levels[...] = (counts[0] + counts[1]) + (counts[2] + counts[3])
+
+
+def pack(grads, rows, given):
+    width = grads.shape[-1]
+    vmem = pl.BlockSpec(memory_space=pltpu.VMEM)
+    block = jax.ShapeDtypeStruct((rows, width), grads.dtype)
+    count = square + 1 if given else square - 1
+    levels = [jax.ShapeDtypeStruct((8, rows), jnp.int32)] if given else []
+    return pl.pallas_call(
+        second_kernel if given else first_kernel,
+        out_shape=[block] * count + levels,
+        in_specs=[pl.BlockSpec(memory_space=pltpu.HBM)] + [vmem] * len(given),
+        out_specs=[vmem] * (count + len(levels)),
+        scratch_shapes=[pltpu.SemaphoreType.DMA((count,))],
+        compiler_params=pltpu.CompilerParams(vmem_limit_bytes=8 * 2**20),
+        name="pack_rest" if given else "pack_own",
+    )(pltpu.with_memory_space_constraint(grads, pltpu.HBM), *given)
+
+
+def noise_of(codes, columns):
+    mixed = codes + columns
+    mixed = jnp.bitwise_xor(mixed, jnp.right_shift(mixed, 13))
+    mixed = mixed * 1103515245
+    mixed = jnp.bitwise_xor(mixed, jnp.right_shift(mixed, 16))
+    return jnp.bitwise_and(jnp.right_shift(mixed, 12), 255).astype(jnp.float32) * (1.0 / 256.0)
+
+
+def fill_codes(far, notes, codes):
+    seeds = jnp.concatenate([note[far : far + 1, :] for note in notes] * 2)
+    codes[...] = jnp.transpose(seeds) * 747796405 + 1013904223
+
+
+def noise_kernel(far, *refs):
+    notes, out, codes = refs[:square], refs[square], refs[square + 1]
+    fill_codes(far, notes, codes)
+    height, width = 16, out.shape[2]
+    columns = lax.broadcasted_iota(jnp.int32, (1, width), 1) * 747796405
+
+    def step(index, carry):
+        span = pl.ds(pl.multiple_of(index * height, height), height)
+        for near in range(square):
+            out[near, span, :] = noise_of(codes[span, near : near + 1], columns).astype(jnp.bfloat16)
+        return carry
+
+    lax.fori_loop(0, out.shape[1] // height, step, 0)
+
+
+def make_noise(far, notes, rows, width):
+    vmem = pl.BlockSpec(memory_space=pltpu.VMEM)
+    return pl.pallas_call(
+        functools.partial(noise_kernel, far),
+        out_shape=jax.ShapeDtypeStruct((square, rows, width), jnp.bfloat16),
+        in_specs=[vmem] * square,
+        out_specs=vmem,
+        scratch_shapes=[pltpu.VMEM((rows, 2 * square), jnp.int32)],
+        compiler_params=pltpu.CompilerParams(vmem_limit_bytes=8 * 2**20),
+        name="noise",
+    )(*notes)
+
+
 def sum_kernel(far, rows, *refs):
-    notes, raws, out, codes = refs[:square], refs[square : 2 * square], refs[-2], refs[-1]
+    notes, raws, rest = refs[:square], refs[square : 2 * square], refs[2 * square :]
+    noise, out, codes = (None, *rest) if far == 0 else (*rest, None)
     target = lax.axis_index("dp") ^ (far * square)
     counts = notes[0][2:3, :]
     for note in notes[1:]:
@@ -99,23 +207,22 @@
     reached = jnp.where(lanes == target, counts, 0).astype(jnp.float32)
     exponent = jnp.max(reached, axis=1, keepdims=True).astype(jnp.int32) + (low_power - level_bits)
     inverse_step = power_of_two(-exponent)
-    seeds = jnp.concatenate([note[far : far + 1, :] for note in notes] * 2)
-    codes[...] = jnp.transpose(seeds) * 747796405 + 1013904223
     height, width = 16, raws[0].shape[1]
     columns = lax.broadcasted_iota(jnp.int32, (1, width), 1) * 747796405
+    if noise is None:
+        fill_codes(far, notes, codes)
 
     def step(index, carry):
         span = pl.ds(pl.multiple_of(index * height, height), height)
         total = jnp.zeros((height, width), jnp.float32)
         for near in range(square):
-            mixed = codes[span, near : near + 1] + columns
-            mixed = jnp.bitwise_xor(mixed, jnp.right_shift(mixed, 13))
-            mixed = mixed * 1103515245
-            mixed = jnp.bitwise_xor(mixed, jnp.right_shift(mixed, 16))
-            noise = jnp.bitwise_and(jnp.right_shift(mixed, 12), 255).astype(jnp.float32) * (1.0 / 256.0)
+            if noise is None:
+                drawn = noise_of(codes[span, near : near + 1], columns)
+            else:
+                drawn = noise[near, span, :].astype(jnp.float32)
             scaled = raws[near][span, :].astype(jnp.float32) * inverse_step
             floor_part = jnp.floor(scaled)
-            total = total + (floor_part + jnp.floor(scaled - floor_part + noise))
+            total = total + (floor_part + jnp.floor(scaled - floor_part + drawn))
         out[span, :] = total.astype(jnp.bfloat16)
         return carry
 
@@ -125,61 +232,73 @@
         out[rows:, :] = jnp.broadcast_to(power_of_two(exponent), tail).astype(jnp.bfloat16)
 
 
-def sum_counts(far, notes, raws, extra):
+def sum_counts(far, notes, raws, noise, extra):
     rows, width = raws[0].shape
-    whole = pl.BlockSpec(memory_space=pltpu.VMEM)
+    vmem = pl.BlockSpec(memory_space=pltpu.VMEM)
+    more = [noise] if far else []
     return pl.pallas_call(
         functools.partial(sum_kernel, far, rows),
         out_shape=jax.ShapeDtypeStruct((rows + extra, width), jnp.bfloat16),
-        in_specs=[whole] * (2 * square),
-        out_specs=whole,
-        scratch_shapes=[pltpu.VMEM((rows, 2 * square), jnp.int32)],
-        cost_estimate=pl.CostEstimate(
-            flops=20 * square * rows * width,
-            bytes_accessed=2 * (square + 1) * rows * width,
-            transcendentals=0,
-        ),
+        in_specs=[vmem] * (2 * square + len(more)),
+        out_specs=vmem,
+        scratch_shapes=[] if far else [pltpu.VMEM((rows, 2 * square), jnp.int32)],
         compiler_params=pltpu.CompilerParams(vmem_limit_bytes=8 * 2**20),
         name="sum_far" if far else "sum_near",
-    )(*notes, *raws)
-
-
-def update_kernel(dp_count, slots, own, beside, across, arrived, weight, mean, updated, step):
-    index = pl.program_id(0)
+    )(*notes, *raws, *more)
+
+
+def update_kernel(dp_count, slots, own, beside, across, arrived, weight, *refs):
+    mean, updated, step, means, news, sems = refs
     place = lax.axis_index("expert")
     holder = jnp.int32(0)
     for slot in range(slots.shape[0]):
         holder = jnp.where(slots[slot] == place, slot, holder)
     turn = holder ^ place
-    rows = mean.shape[1]
-    span = pl.ds(pl.multiple_of(index * rows, rows), rows)
-    last = own.shape[0] - arrived.shape[0]
-    tail = pl.ds(arrived.shape[0], last)
-
-    def nearby(where):
-        held, swapped, crossed = (ref[where, :].astype(jnp.float32) for ref in (own, beside, across))
+    rows = arrived.shape[0]
+
+    def nearby(span):
+        held, swapped, crossed = (ref[span, :].astype(jnp.float32) for ref in (own, beside, across))
         return jnp.where(turn == 0, held, jnp.where(turn == 1, swapped, crossed))
 
-    size = nearby(tail)[0:1, :]
-    total = nearby(span) + arrived[span, :].astype(jnp.float32)
-    averaged = total * (size * (1.0 / dp_count))
-    mean[0] = averaged
-    updated[0] = weight[0] - learn_rate * averaged
+    size = nearby(slice(rows, own.shape[0]))[0:1, :]
     step[...] = size[:, 0:1]
+    scale = size * (1.0 / dp_count)
+    parts = sems.shape[1]
+    height = rows // parts
+    copies = []
+    for part in range(parts):
+        span = slice(part * height, (part + 1) * height)
+        averaged = (nearby(span) + arrived[span, :].astype(jnp.float32)) * scale
+        means[span, :] = averaged
+        news[span, :] = weight[0, span, :] - learn_rate * averaged
+        for number, (source, target) in enumerate(((means, mean), (news, updated))):
+            copy = pltpu.make_async_copy(
+                source.at[pl.ds(part * height, height), :],
+                target.at[0, pl.ds(part * height, height), :],
+                sems.at[number, part],
+            )
+            copy.start()
+            copies.append(copy)
+    for copy in copies:
+        copy.wait()
 
 
 def update(slots, own, beside, across, arrived, weight, dp_count):
     rows, width = arrived.shape
     parts = 4
-    whole = pl.BlockSpec(memory_space=pltpu.VMEM)
-    strip = pl.BlockSpec((1, rows // parts, width), lambda index: (0, index, 0))
+    vmem = pl.BlockSpec(memory_space=pltpu.VMEM)
+    hbm = pl.BlockSpec(memory_space=pltpu.HBM)
     block = jax.ShapeDtypeStruct((1, rows, width), jnp.float32)
     return pl.pallas_call(
         functools.partial(update_kernel, dp_count),
-        grid=(parts,),
         out_shape=(block, block, jax.ShapeDtypeStruct((1, 1), jnp.float32)),
-        in_specs=[pl.BlockSpec(memory_space=pltpu.SMEM), whole, whole, whole, whole, strip],
-        out_specs=(strip, strip, pl.BlockSpec((1, 1), lambda index: (0, 0))),
+        in_specs=[pl.BlockSpec(memory_space=pltpu.SMEM)] + [vmem] * 5,
+        out_specs=(hbm, hbm, vmem),
+        scratch_shapes=[
+            pltpu.VMEM((rows, width), jnp.float32),
+            pltpu.VMEM((rows, width), jnp.float32),
+            pltpu.SemaphoreType.DMA((2, parts)),
+        ],
         compiler_params=pltpu.CompilerParams(vmem_limit_bytes=8 * 2**20),
         name="update",
     )(slots, own, beside, across, arrived, weight)
@@ -192,7 +311,6 @@
     block_rows = row_count // dp_count
     me = lax.axis_index("dp")
     place = lax.axis_index("expert")
-    blocks = expert_grads[0, 0].reshape(dp_count, block_rows, hidden)
     offsets = round_offsets[0, 0].reshape(dp_count, block_rows)
 
     def pick(array, index):
@@ -202,36 +320,30 @@
     weights = jnp.array([6, 2, 1, 0], jnp.int32)[:, None]
     lower = (slot_expert[:, None] > slot_expert[None, :]) & after
     branch = jnp.sum(jnp.where(lower, weights, 0))
-    peaks = jnp.max(jnp.abs(blocks), axis=(1, 2)).astype(jnp.float32)
-    twin = lax.ppermute(peaks, "dp", flips(dp_count, square))
-    powers = jnp.array([2.0**power for power in range(low_power, high_power)], jnp.float32)
-    reached = jnp.maximum(peaks, twin)[:, None] >= powers
-    counts = jnp.sum(reached.astype(jnp.int32), axis=1)
-    counts = jnp.pad(counts, (0, block_rows - dp_count))
-
-    later = lax.optimization_barrier(blocks)
-    raw, notes = [[], []], []
+    near_blocks = pack(expert_grads, block_rows, [])
+    *rest, levels = pack(expert_grads, block_rows, near_blocks)
+    twin = lax.ppermute(levels, "dp", flips(dp_count, square))
+    levels = jnp.maximum(levels[0], twin[0])
+
+    raw, notes = [[rest[0], *near_blocks], rest[1:]], []
     for near in range(square):
-        targets = [(me ^ near) ^ (far * square) for far in range(2)]
-        seeds = [pick(offsets, target) for target in targets]
-        note = jnp.concatenate([jnp.stack(seeds + [counts]), jnp.zeros((5, block_rows), jnp.int32)])
-        rows = [pick(blocks if near else later, targets[0]), pick(later, targets[1])]
+        seeds = [pick(offsets, (me ^ near) ^ (far * square)) for far in range(2)]
+        note = jnp.concatenate([jnp.stack(seeds + [levels]), jnp.zeros((5, block_rows), jnp.int32)])
         if near:
             pairs = flips(dp_count, near)
             note = lax.ppermute(note, "dp", pairs)
             for far in range(2):
-                rows[far] = lax.ppermute(rows[far], "dp", pairs)
+                raw[far][near] = lax.ppermute(raw[far][near], "dp", pairs)
         notes.append(note)
-        for far in range(2):
-            raw[far].append(rows[far])
 
     wanted = slot_expert == (place ^ 2)
-    holder = jnp.sum(jnp.where(wanted, jnp.arange(expert_count), 0))
-    own = sum_counts(0, notes, raw[0], 8)
+    crossing = jnp.sum(jnp.where(wanted, jnp.arange(expert_count), 0)) == place
+    own = sum_counts(0, notes, raw[0], None, 8)
     beside = lax.ppermute(own, "expert", flips(expert_count, 1))
-    across_wants = jnp.where(holder == place, own, beside)
+    across_wants = jnp.where(crossing, own, beside)
     across = lax.ppermute(across_wants, "expert", flips(expert_count, 2))
-    message = sum_counts(1, notes, raw[1], 0)
+    noise = make_noise(1, notes, block_rows, hidden)
+    message = sum_counts(1, notes, raw[1], noise, 0)
 
     def route(order):
         pairs = [

time: 58.2 us -> 61.8 us (1.062)
  Pallas kernels: 5.92 us -> 9.01 us
  starting transfers between devices: 18.4 us -> 20.9 us
  other arithmetic: 3.82 us -> 1.44 us
  waiting for transfers between devices: 25.9 us -> 28.1 us
  local copies, waits for them, and re-layouts: 1.81 us -> 0.11 us
    pallas_call x1 -> x4, Pallas kernels: 2.54 us -> 6.62 us  [the longest x2 2.82 us: pack(): pl.pallas_call(second_kernel if given else first_kernel, out_shape=[block...]
    ppermute x7, waiting for transfers between devices: 8.79 us -> 12.6 us  [the longest x6 7.76 us: staged_body(): raw[far][near] = lax.ppermute(raw[far][near], 'dp', pairs)]
    ppermute x3, starting transfers between devices: 5.64 us -> 7.94 us  [staged_body(): note = lax.ppermute(note, 'dp', pairs)]
    reduce_max x2 -> x0, other arithmetic: 2.19 us -> none  [staged_body(): peaks = jnp.max(jnp.abs(blocks), axis=(1, 2)).astype(jnp.float32)]
    squeeze x2 -> x0, local copies, waits for them, and re-layouts: 1.67 us -> none  [pick(): return lax.dynamic_index_in_dim(array, index, 0, keepdims=False)]
    ppermute x3, waiting for transfers between devices: 3.18 us -> 1.65 us  [staged_body(): note = lax.ppermute(note, 'dp', pairs)]
    pallas_call x2, Pallas kernels: 3.38 us -> 2.39 us  [sum_counts(): pl.pallas_call(functools.partial(sum_kernel, far, rows), out_shape=jax.Sh...]
  transfers between devices with their start and end apart: 13 -> 13, of which waited for: 7 -> 8; matrix products, arithmetic and copies ran while one was open for 6% -> 2% of each run, Pallas kernels for 3% -> 6%
where the time goes in v2:
time: 61.8 us; the launch traced here: 61.6 us
  waiting for transfers between devices  28.1 us (45%)
  starting transfers between devices  20.9 us (34%)
  Pallas kernels  9.01 us (15%)
  between operations  2.05 us (3%)
  other arithmetic  1.44 us (2%)
    ppermute x1, waiting for transfers between devices, route(): return lambda parts: lax.ppermute(parts, ('dp', 'expert'), pairs)  13.7 us
    ppermute x6, starting transfers between devices, staged_body(): raw[far][near] = lax.ppermute(raw[far][near], 'dp', pairs)  8.13 us
    ppermute x3, starting transfers between devices, staged_body(): note = lax.ppermute(note, 'dp', pairs)  7.94 us
    ppermute x6, waiting for transfers between devices, staged_body(): raw[far][near] = lax.ppermute(raw[far][near], 'dp', pairs)  7.76 us
    ppermute x1, waiting for transfers between devices, staged_body(): twin = lax.ppermute(levels, 'dp', flips(dp_count, square))  4.8 us
    ppermute x1, starting transfers between devices, staged_body(): twin = lax.ppermute(levels, 'dp', flips(dp_count, square))  3.04 us
    pallas_call x2, Pallas kernels, pack(): pl.pallas_call(second_kernel if given else first_kernel, out_shape=[block...  2.82 us
    pallas_call x1, Pallas kernels, update(): pl.pallas_call(functools.partial(update_kernel, dp_count), out_shape=(blo...  2.49 us
  transfers between devices with their start and end apart: 13, of which 8 were waited for; matrix products, arithmetic and copies ran while one was open for 2% of the time, Pallas kernels for 6%

profile of v2, /device:TPU:0, one launch (start us, length us, event | category | flops | bytes accessed | tf_op | source)
XLA Modules:
  0.0 61.6 jit_solution(8364829507802124915)
XLA Ops:
  0.6 1.2 %pack_own.1 = (bf16[128,896]{1,0:T(8,128)(2,1)S(1)}, bf16[128,896]{1,0:T(8,128)(2,1)S(1)}, bf16[128,896]{1,0:T(8,128)(2,1)S(1)}) custom-call(bf16[1,1,1024,896]{3,2,1,0:T(8,128)(2,1)} %grads.3), custom_call_target="tpu_custom_call" | custom-call | tf_op jit(solution)/shard_map/pack_own/pallas_call | solution.py:147
  1.8 3.1 %collective-permute-start.28 = (bf16[128,896]{1,0:T(8,128)(2,1)S(1)}, bf16[128,896]{1,0:T(8,128)(2,1)S(1)}, u32[]{:S(2)}, u32[]{:S(2)}) collective-permute-start(bf16[128,896]{1,0:T(8,128)(2,1)S(1)} %get-tuple-element.61.refs_0_), channel_id=1, source_target_pairs={{0,4},{4,0},{8,12},{12,8},{16,20},{20,16},{24,28},{28,24},{1,5},{5... | collective-permute-start | bytes 688136 | tf_op jit(solution)/shard_map/ppermute | solution.py:336
  4.9 1.6 %collective-permute-start.29 = (bf16[128,896]{1,0:T(8,128)(2,1)S(1)}, bf16[128,896]{1,0:T(8,128)(2,1)S(1)}, u32[]{:S(2)}, u32[]{:S(2)}) collective-permute-start(bf16[128,896]{1,0:T(8,128)(2,1)S(1)} %get-tuple-element.62.refs_1_), channel_id=1, source_target_pairs={{0,8},{4,12},{8,0},{12,4},{16,24},{20,28},{24,16},{28,20},{1,9},{5... | collective-permute-start | bytes 688136 | tf_op jit(solution)/shard_map/ppermute | solution.py:336
  6.5 1.6 %pack_rest.1 = (bf16[128,896]{1,0:T(8,128)(2,1)S(1)}, bf16[128,896]{1,0:T(8,128)(2,1)S(1)}, bf16[128,896]{1,0:T(8,128)(2,1)S(1)}, bf16[128,896]{1,0:T(8,128)(2,1...) custom-call(bf16[1,1,1024,896]{3,2,1,0:T(8,128)(2,1)} %grads.3, ...), custom_call_target="tpu_custom_call" | custom-call | tf_op jit(solution)/shard_map/pack_rest/pallas_call | solution.py:147
  8.1 3.0 %collective-permute-start.24 = (s32[8,128]{1,0:T(8,128)S(1)}, s32[8,128]{1,0:T(8,128)S(1)}, u32[]{:S(2)}, u32[]{:S(2)}) collective-permute-start(s32[8,128]{1,0:T(8,128)S(1)} %get-tuple-element.64), channel_id=1, source_target_pairs={{0,16},{4,20},{8,24},{12,28},{16,0},{20,4},{24,8},{28,12},{1,17},{... | collective-permute-start | bytes 12296 | tf_op jit(solution)/shard_map/ppermute | solution.py:325
  11.3 4.8 %collective-permute-done.24 = s32[8,128]{1,0:T(8,128)S(1)} collective-permute-done((s32[8,128]{1,0:T(8,128)S(1)}, s32[8,128]{1,0:T(8,128)S(1)}, u32[]{:S(2)}, u32[]{:S(2)}) %collective-permute-start.24) | collective-permute-done | bytes 4128 | tf_op jit(solution)/shard_map/ppermute | solution.py:325
  16.1 3.4 %collective-permute-start.27 = (s32[8,128]{1,0:T(8,128)S(1)}, s32[8,128]{1,0:T(8,128)S(1)}, u32[]{:S(2)}, u32[]{:S(2)}) collective-permute-start(s32[8,128]{1,0:T(8,128)S(1)} %get-tuple-element.78), channel_id=1, source_target_pairs={{0,12},{4,8},{8,4},{12,0},{16,28},{20,24},{24,20},{28,16},{1,13},{... | collective-permute-start | bytes 12296 | tf_op jit(solution)/shard_map/ppermute | solution.py:334
  19.6 1.5 %collective-permute-start.25 = (s32[8,128]{1,0:T(8,128)S(1)}, s32[8,128]{1,0:T(8,128)S(1)}, u32[]{:S(2)}, u32[]{:S(2)}) collective-permute-start(s32[8,128]{1,0:T(8,128)S(1)} %get-tuple-element.79), channel_id=1, source_target_pairs={{0,4},{4,0},{8,12},{12,8},{16,20},{20,16},{24,28},{28,24},{1,5},{5... | collective-permute-start | bytes 12296 | tf_op jit(solution)/shard_map/ppermute | solution.py:334
  21.2 3.0 %collective-permute-start.26 = (s32[8,128]{1,0:T(8,128)S(1)}, s32[8,128]{1,0:T(8,128)S(1)}, u32[]{:S(2)}, u32[]{:S(2)}) collective-permute-start(s32[8,128]{1,0:T(8,128)S(1)} %get-tuple-element.80), channel_id=1, source_target_pairs={{0,8},{4,12},{8,0},{12,4},{16,24},{20,28},{24,16},{28,20},{1,9},{5... | collective-permute-start | bytes 12296 | tf_op jit(solution)/shard_map/ppermute | solution.py:334
  24.2 1.6 %collective-permute-done.26.refs_2_ = s32[8,128]{1,0:T(8,128)S(1)} collective-permute-done((s32[8,128]{1,0:T(8,128)S(1)}, s32[8,128]{1,0:T(8,128)S(1)}, u32[]{:S(2)}, u32[]{:S(2)}) %collective-permute-start.26) | collective-permute-done | bytes 4128 | tf_op jit(solution)/shard_map/ppermute | solution.py:334
  25.8 1.7 %sum_near.1.own = bf16[136,896]{1,0:T(8,128)(2,1)S(1)} custom-call(s32[8,128]{1,0:T(8,128)S(1)} %get-tuple-element.81.refs_0_, s32[8,128]{1,0:T(8,128)S(1)} %collective-permute-done.25.refs_1_, s32[8,128]{1,0:T(8,128)S(1)} %collective-permute-done.26.refs_2_, s32[8,128]{1,0:T(8,128)S(1)} %collective-permute-done.27.refs_3_, ...), custom_call_target="tpu_custom_call" | custom-call | tf_op jit(solution)/shard_map/sum_near/pallas_call | solution.py:239
  27.5 0.6 %fusion.5 = s32[]{:T(128)} fusion(s32[4]{0:T(128)S(1)} %copy-done.1, s32[]{:T(128)S(6)} %xor.34), kind=kLoop, calls=%fused_computation.21 | loop fusion | flops 11 | bytes 24 | tf_op jit(solution)/shard_map/reduce_sum | solution.py:340
  29.1 1.6 %collective-permute-start.32 = (bf16[136,896]{1,0:T(8,128)(2,1)S(1)}, bf16[136,896]{1,0:T(8,128)(2,1)S(1)}, u32[]{:S(2)}, u32[]{:S(2)}) collective-permute-start(bf16[136,896]{1,0:T(8,128)(2,1)S(1)} %broadcast_select_fusion), channel_id=1, source_target_pairs={{0,2},{1,3},{2,0},{3,1},{4,6},{5,7},{6,4},{7,5},{8,10},{9,11},{10,... | collective-permute-start | bytes 731144 | tf_op jit(solution)/shard_map/ppermute | solution.py:344
  31.2 2.0 %collective-permute-start.34 = (bf16[128,896]{1,0:T(8,128)(2,1)S(1)}, bf16[128,896]{1,0:T(8,128)(2,1)S(1)}, u32[]{:S(2)}, u32[]{:S(2)}) collective-permute-start(bf16[128,896]{1,0:T(8,128)(2,1)S(1)} %get-tuple-element.68), channel_id=1, source_target_pairs={{0,8},{4,12},{8,0},{12,4},{16,24},{20,28},{24,16},{28,20},{1,9},{5... | collective-permute-start | bytes 688136 | tf_op jit(solution)/shard_map/ppermute | solution.py:336
  33.1 1.0 %collective-permute-start.35 = (bf16[128,896]{1,0:T(8,128)(2,1)S(1)}, bf16[128,896]{1,0:T(8,128)(2,1)S(1)}, u32[]{:S(2)}, u32[]{:S(2)}) collective-permute-start(bf16[128,896]{1,0:T(8,128)(2,1)S(1)} %get-tuple-element.69), channel_id=1, source_target_pairs={{0,12},{4,8},{8,4},{12,0},{16,28},{20,24},{24,20},{28,16},{1,13},{... | collective-permute-start | bytes 688136 | tf_op jit(solution)/shard_map/ppermute | solution.py:336
  34.1 0.7 %select_reduce_fusion = s32[]{:T(128)} fusion(s32[4]{0:T(128)S(1)} %copy-done.3, s32[4]{0:T(128)S(1)} %copy-done.1), kind=kLoop, calls=%fused_computation.9 | loop fusion | flops 79 | bytes 36 | tf_op jit(solution)/shard_map/reduce_sum | solution.py:322
  35.5 1.3 %noise.1.refs_8_ = bf16[4,128,896]{2,1,0:T(8,128)(2,1)S(1)} custom-call(s32[8,128]{1,0:T(8,128)S(1)} %get-tuple-element.81.refs_0_, s32[8,128]{1,0:T(8,128)S(1)} %collective-permute-done.25.refs_1_, s32[8,128]{1,0:T(8,128)S(1)} %collective-permute-done.26.refs_2_, s32[8,128]{1,0:T(8,128)S(1)} %collective-permute-done.27.refs_3_), custom_call_target="tpu_custom_call" | custom-call | tf_op jit(solution)/shard_map/noise/pallas_call | solution.py:188
  36.8 1.4 %collective-permute-done.33.refs_5_ = bf16[128,896]{1,0:T(8,128)(2,1)S(1)} collective-permute-done((bf16[128,896]{1,0:T(8,128)(2,1)S(1)}, bf16[128,896]{1,0:T(8,128)(2,1)S(1)}, u32[]{:S(2)}, u32[]{:S(2)}) %collective-permute-start.33) | collective-permute-done | bytes 229408 | tf_op jit(solution)/shard_map/ppermute | solution.py:336
  38.2 1.5 %collective-permute-done.34.refs_6_ = bf16[128,896]{1,0:T(8,128)(2,1)S(1)} collective-permute-done((bf16[128,896]{1,0:T(8,128)(2,1)S(1)}, bf16[128,896]{1,0:T(8,128)(2,1)S(1)}, u32[]{:S(2)}, u32[]{:S(2)}) %collective-permute-start.34) | collective-permute-done | bytes 229408 | tf_op jit(solution)/shard_map/ppermute | solution.py:336
  39.7 4.9 %collective-permute-done.35.refs_7_ = bf16[128,896]{1,0:T(8,128)(2,1)S(1)} collective-permute-done((bf16[128,896]{1,0:T(8,128)(2,1)S(1)}, bf16[128,896]{1,0:T(8,128)(2,1)S(1)}, u32[]{:S(2)}, u32[]{:S(2)}) %collective-permute-start.35) | collective-permute-done | bytes 229408 | tf_op jit(solution)/shard_map/ppermute | solution.py:336
  44.5 0.7 %sum_far.1 = bf16[128,896]{1,0:T(8,128)(2,1)S(1)} custom-call(s32[8,128]{1,0:T(8,128)S(1)} %get-tuple-element.81.refs_0_, s32[8,128]{1,0:T(8,128)S(1)} %collective-permute-done.25.refs_1_, s32[8,128]{1,0:T(8,128)S(1)} %collective-permute-done.26.refs_2_, s32[8,128]{1,0:T(8,128)S(1)} %collective-permute-done.27.refs_3_, ...), custom_call_target="tpu_custom_call" | custom-call | tf_op jit(solution)/shard_map/sum_far/pallas_call | solution.py:239
  45.2 13.9 %conditional.1 = (bf16[128,896]{1,0:T(8,128)(2,1)}) conditional(s32[]{:T(128)} %clamp.3, bf16[128,896]{1,0:T(8,128)(2,1)S(1)} %sum_far.1, bf16[128,896]{1,0:T(8,128)(2,1)S(1)} %sum_far.1, bf16[128,896]{1,0:T(8,128)(2,1)S(1)} %sum_far.1, bf16[128,896]{1,0:T(8,128)(2,1)S(1)} %sum_far.1, ...), branch_computations={%region_2.3_spmd, %region_3.4_spmd, %region_4.5_spmd, %region_5.6_... | conditional | bytes 917552 | solution.py:357
  45.4 13.7 %collective-permute-done.20 = bf16[128,896]{1,0:T(8,128)(2,1)} collective-permute-done((bf16[128,896]{1,0:T(8,128)(2,1)S(1)}, bf16[128,896]{1,0:T(8,128)(2,1)}, u32[]{:S(2)}, u32[]{:S(2)}) %collective-permute-start.20) | collective-permute-done | bytes 229408 | tf_op jit(solution)/shard_map/cond/branch_20_fun/ppermute | solution.py:354
  59.1 2.5 %update.1 = (f32[1,128,896]{2,1,0:T(8,128)}, f32[1,128,896]{2,1,0:T(8,128)}, f32[1,1]{1,0:T(1,128)}) custom-call(s32[4]{0:T(128)S(1)} %copy-done.1, bf16[136,896]{1,0:T(8,128)(2,1)S(1)} %sum_near.1.own, bf16[136,896]{1,0:T(8,128)(2,1)S(1)} %collective-permute-done.31.beside, bf16[136,896]{1,0:T(8,128)(2,1)S(1)} %collective-permute-done.32.across, ...), custom_call_target="tpu_custom_call" | custom-call | tf_op jit(solution)/shard_map/update/pallas_call | solution.py:292
  (25 shorter events, 1.3 us)
Async XLA Ops:
  0.6 10.5 %copy-start.2 = (s32[1,1,1024]{2,1,0:T(1,128)S(1)}, s32[1,1,1024]{2,1,0:T(1,128)}, u32[]{:S(2)}) copy-start(s32[1,1,1024]{2,1,0:T(1,128)} %param.30) | copy-start | bytes 12292
  1.8 23.9 %collective-permute-start.28 = (bf16[128,896]{1,0:T(8,128)(2,1)S(1)}, bf16[128,896]{1,0:T(8,128)(2,1)S(1)}, u32[]{:S(2)}, u32[]{:S(2)}) collective-permute-start(bf16[128,896]{1,0:T(8,128)(2,1)S(1)} %get-tuple-element.61.refs_0_), channel_id=1, source_target_pairs={{0,4},{4,0},{8,12},{12,8},{16,20},{20,16},{24,28},{28,24},{1,5},{5... | collective-permute-start | bytes 688136 | tf_op jit(solution)/shard_map/ppermute | solution.py:336
  4.9 20.8 %collective-permute-start.29 = (bf16[128,896]{1,0:T(8,128)(2,1)S(1)}, bf16[128,896]{1,0:T(8,128)(2,1)S(1)}, u32[]{:S(2)}, u32[]{:S(2)}) collective-permute-start(bf16[128,896]{1,0:T(8,128)(2,1)S(1)} %get-tuple-element.62.refs_1_), channel_id=1, source_target_pairs={{0,8},{4,12},{8,0},{12,4},{16,24},{20,28},{24,16},{28,20},{1,9},{5... | collective-permute-start | bytes 688136 | tf_op jit(solution)/shard_map/ppermute | solution.py:336
  6.5 21.1 %copy-start.1 = (s32[4]{0:T(128)S(1)}, s32[4]{0:T(128)}, u32[]{:S(2)}) copy-start(s32[4]{0:T(128)} %slots.1) | copy-start | bytes 52
  6.5 27.6 %copy-start.3 = (s32[4]{0:T(128)S(1)}, s32[4]{0:T(128)}, u32[]{:S(2)}) copy-start(s32[4]{0:T(128)} %constant.43.clone) | copy-start | bytes 52
  6.5 19.3 %collective-permute-start.30 = (bf16[128,896]{1,0:T(8,128)(2,1)S(1)}, bf16[128,896]{1,0:T(8,128)(2,1)S(1)}, u32[]{:S(2)}, u32[]{:S(2)}) collective-permute-start(bf16[128,896]{1,0:T(8,128)(2,1)S(1)} %get-tuple-element.63.refs_2_), channel_id=1, source_target_pairs={{0,12},{4,8},{8,4},{12,0},{16,28},{20,24},{24,20},{28,16},{1,13},{... | collective-permute-start | bytes 688136 | tf_op jit(solution)/shard_map/ppermute | solution.py:336
  8.1 8.0 %collective-permute-start.24 = (s32[8,128]{1,0:T(8,128)S(1)}, s32[8,128]{1,0:T(8,128)S(1)}, u32[]{:S(2)}, u32[]{:S(2)}) collective-permute-start(s32[8,128]{1,0:T(8,128)S(1)} %get-tuple-element.64), channel_id=1, source_target_pairs={{0,16},{4,20},{8,24},{12,28},{16,0},{20,4},{24,8},{28,12},{1,17},{... | collective-permute-start | bytes 12296 | tf_op jit(solution)/shard_map/ppermute | solution.py:325
  16.1 5.0 %collective-permute-start.27 = (s32[8,128]{1,0:T(8,128)S(1)}, s32[8,128]{1,0:T(8,128)S(1)}, u32[]{:S(2)}, u32[]{:S(2)}) collective-permute-start(s32[8,128]{1,0:T(8,128)S(1)} %get-tuple-element.78), channel_id=1, source_target_pairs={{0,12},{4,8},{8,4},{12,0},{16,28},{20,24},{24,20},{28,16},{1,13},{... | collective-permute-start | bytes 12296 | tf_op jit(solution)/shard_map/ppermute | solution.py:334
  19.6 4.6 %collective-permute-start.25 = (s32[8,128]{1,0:T(8,128)S(1)}, s32[8,128]{1,0:T(8,128)S(1)}, u32[]{:S(2)}, u32[]{:S(2)}) collective-permute-start(s32[8,128]{1,0:T(8,128)S(1)} %get-tuple-element.79), channel_id=1, source_target_pairs={{0,4},{4,0},{8,12},{12,8},{16,20},{20,16},{24,28},{28,24},{1,5},{5... | collective-permute-start | bytes 12296 | tf_op jit(solution)/shard_map/ppermute | solution.py:334
  21.2 4.6 %collective-permute-start.26 = (s32[8,128]{1,0:T(8,128)S(1)}, s32[8,128]{1,0:T(8,128)S(1)}, u32[]{:S(2)}, u32[]{:S(2)}) collective-permute-start(s32[8,128]{1,0:T(8,128)S(1)} %get-tuple-element.80), channel_id=1, source_target_pairs={{0,8},{4,12},{8,0},{12,4},{16,24},{20,28},{24,16},{28,20},{1,9},{5... | collective-permute-start | bytes 12296 | tf_op jit(solution)/shard_map/ppermute | solution.py:334
  27.4 1.6 %collective-permute-start.31 = (bf16[136,896]{1,0:T(8,128)(2,1)S(1)}, bf16[136,896]{1,0:T(8,128)(2,1)S(1)}, u32[]{:S(2)}, u32[]{:S(2)}) collective-permute-start(bf16[136,896]{1,0:T(8,128)(2,1)S(1)} %sum_near.1.own), channel_id=1, source_target_pairs={{0,1},{1,0},{2,3},{3,2},{4,5},{5,4},{6,7},{7,6},{8,9},{9,8},{10,11... | collective-permute-start | bytes 731144 | tf_op jit(solution)/shard_map/ppermute | solution.py:342
  28.8 30.3 %copy-start = (f32[1,128,896]{2,1,0:T(8,128)S(1)}, f32[1,128,896]{2,1,0:T(8,128)}, u32[]{:S(2)}) copy-start(f32[1,128,896]{2,1,0:T(8,128)} %weight.1) | copy-start | bytes 1376260
  29.1 30.1 %collective-permute-start.32 = (bf16[136,896]{1,0:T(8,128)(2,1)S(1)}, bf16[136,896]{1,0:T(8,128)(2,1)S(1)}, u32[]{:S(2)}, u32[]{:S(2)}) collective-permute-start(bf16[136,896]{1,0:T(8,128)(2,1)S(1)} %broadcast_select_fusion), channel_id=1, source_target_pairs={{0,2},{1,3},{2,0},{3,1},{4,6},{5,7},{6,4},{7,5},{8,10},{9,11},{10,... | collective-permute-start | bytes 731144 | tf_op jit(solution)/shard_map/ppermute | solution.py:344
  30.6 7.5 %collective-permute-start.33 = (bf16[128,896]{1,0:T(8,128)(2,1)S(1)}, bf16[128,896]{1,0:T(8,128)(2,1)S(1)}, u32[]{:S(2)}, u32[]{:S(2)}) collective-permute-start(bf16[128,896]{1,0:T(8,128)(2,1)S(1)} %get-tuple-element.67), channel_id=1, source_target_pairs={{0,4},{4,0},{8,12},{12,8},{16,20},{20,16},{24,28},{28,24},{1,5},{5... | collective-permute-start | bytes 688136 | tf_op jit(solution)/shard_map/ppermute | solution.py:336
  31.2 8.5 %collective-permute-start.34 = (bf16[128,896]{1,0:T(8,128)(2,1)S(1)}, bf16[128,896]{1,0:T(8,128)(2,1)S(1)}, u32[]{:S(2)}, u32[]{:S(2)}) collective-permute-start(bf16[128,896]{1,0:T(8,128)(2,1)S(1)} %get-tuple-element.68), channel_id=1, source_target_pairs={{0,8},{4,12},{8,0},{12,4},{16,24},{20,28},{24,16},{28,20},{1,9},{5... | collective-permute-start | bytes 688136 | tf_op jit(solution)/shard_map/ppermute | solution.py:336
  33.1 11.4 %collective-permute-start.35 = (bf16[128,896]{1,0:T(8,128)(2,1)S(1)}, bf16[128,896]{1,0:T(8,128)(2,1)S(1)}, u32[]{:S(2)}, u32[]{:S(2)}) collective-permute-start(bf16[128,896]{1,0:T(8,128)(2,1)S(1)} %get-tuple-element.69), channel_id=1, source_target_pairs={{0,12},{4,8},{8,4},{12,0},{16,28},{20,24},{24,20},{28,16},{1,13},{... | collective-permute-start | bytes 688136 | tf_op jit(solution)/shard_map/ppermute | solution.py:336
  45.3 13.9 %collective-permute-start.20 = (bf16[128,896]{1,0:T(8,128)(2,1)S(1)}, bf16[128,896]{1,0:T(8,128)(2,1)}, u32[]{:S(2)}, u32[]{:S(2)}) collective-permute-start(bf16[128,896]{1,0:T(8,128)(2,1)S(1)} %param.20), channel_id=1, source_target_pairs={{0,19},{1,17},{2,16},{3,18},{4,23},{5,21},{6,20},{7,22},{8,27},{9,... | collective-permute-start | bytes 688136 | tf_op jit(solution)/shard_map/cond/branch_20_fun/ppermute | solution.py:354

commit v3 on v2

--- a/solution.py
+++ b/solution.py
@@ -248,12 +248,11 @@
 
 
 def update_kernel(dp_count, slots, own, beside, across, arrived, weight, *refs):
-    mean, updated, step, means, news, sems = refs
+    mean, updated, step, means, news, size_out, sems, size_sem = refs
     place = lax.axis_index("expert")
-    holder = jnp.int32(0)
-    for slot in range(slots.shape[0]):
-        holder = jnp.where(slots[slot] == place, slot, holder)
-    turn = holder ^ place
+    positions = lax.broadcasted_iota(jnp.int32, slots.shape, 1)
+    turns = jnp.where(slots[...] == place, positions ^ place, 0).astype(jnp.float32)
+    turn = jnp.max(turns, axis=1, keepdims=True)
     rows = arrived.shape[0]
 
     def nearby(span):
@@ -261,11 +260,13 @@
         return jnp.where(turn == 0, held, jnp.where(turn == 1, swapped, crossed))
 
     size = nearby(slice(rows, own.shape[0]))[0:1, :]
-    step[...] = size[:, 0:1]
+    size_out[...] = size[:, 0:1]
+    size_copy = pltpu.make_async_copy(size_out, step, size_sem)
+    size_copy.start()
     scale = size * (1.0 / dp_count)
     parts = sems.shape[1]
     height = rows // parts
-    copies = []
+    copies = [size_copy]
     for part in range(parts):
         span = slice(part * height, (part + 1) * height)
         averaged = (nearby(span) + arrived[span, :].astype(jnp.float32)) * scale
@@ -292,16 +293,18 @@
     return pl.pallas_call(
         functools.partial(update_kernel, dp_count),
         out_shape=(block, block, jax.ShapeDtypeStruct((1, 1), jnp.float32)),
-        in_specs=[pl.BlockSpec(memory_space=pltpu.SMEM)] + [vmem] * 5,
-        out_specs=(hbm, hbm, vmem),
+        in_specs=[vmem] * 6,
+        out_specs=(hbm, hbm, hbm),
         scratch_shapes=[
             pltpu.VMEM((rows, width), jnp.float32),
             pltpu.VMEM((rows, width), jnp.float32),
+            pltpu.VMEM((1, 1), jnp.float32),
             pltpu.SemaphoreType.DMA((2, parts)),
+            pltpu.SemaphoreType.DMA,
         ],
         compiler_params=pltpu.CompilerParams(vmem_limit_bytes=8 * 2**20),
         name="update",
-    )(slots, own, beside, across, arrived, weight)
+    )(slots[None], own, beside, across, arrived, weight)
 
 
 def staged_body(expert_grads, round_offsets, slot_expert, master_weight):

time: 61.8 us -> 61.4 us (level)
  no operation moved by 1% of the time
where the time goes in v3:
time: 61.4 us; the launch traced here: 61.2 us
  waiting for transfers between devices  28.1 us (46%)
  starting transfers between devices  20.9 us (34%)
  Pallas kernels  8.58 us (14%)
  between operations  2.05 us (3%)
  other arithmetic  1.44 us (2%)
    ppermute x1, waiting for transfers between devices, route(): return lambda parts: lax.ppermute(parts, ('dp', 'expert'), pairs)  13.7 us
    ppermute x6, starting transfers between devices, staged_body(): raw[far][near] = lax.ppermute(raw[far][near], 'dp', pairs)  8.13 us
    ppermute x3, starting transfers between devices, staged_body(): note = lax.ppermute(note, 'dp', pairs)  7.94 us
    ppermute x6, waiting for transfers between devices, staged_body(): raw[far][near] = lax.ppermute(raw[far][near], 'dp', pairs)  7.76 us
    ppermute x1, waiting for transfers between devices, staged_body(): twin = lax.ppermute(levels, 'dp', flips(dp_count, square))  4.8 us
    ppermute x1, starting transfers between devices, staged_body(): twin = lax.ppermute(levels, 'dp', flips(dp_count, square))  3.04 us
    pallas_call x2, Pallas kernels, pack(): pl.pallas_call(second_kernel if given else first_kernel, out_shape=[block...  2.82 us
    pallas_call x2, Pallas kernels, sum_counts(): pl.pallas_call(functools.partial(sum_kernel, far, rows), out_shape=jax.Sh...  2.39 us
  transfers between devices with their start and end apart: 13, of which 8 were waited for; matrix products, arithmetic and copies ran while one was open for 2% of the time, Pallas kernels for 6%

profile of v3, /device:TPU:0, one launch (start us, length us, event | category | flops | bytes accessed | tf_op | source)
XLA Modules:
  0.0 61.2 jit_solution(6176712930599193745)
XLA Ops:
  0.6 1.2 %pack_own.1 = (bf16[128,896]{1,0:T(8,128)(2,1)S(1)}, bf16[128,896]{1,0:T(8,128)(2,1)S(1)}, bf16[128,896]{1,0:T(8,128)(2,1)S(1)}) custom-call(bf16[1,1,1024,896]{3,2,1,0:T(8,128)(2,1)} %grads.3), custom_call_target="tpu_custom_call" | custom-call | tf_op jit(solution)/shard_map/pack_own/pallas_call | solution.py:147
  1.8 3.1 %collective-permute-start.28 = (bf16[128,896]{1,0:T(8,128)(2,1)S(1)}, bf16[128,896]{1,0:T(8,128)(2,1)S(1)}, u32[]{:S(2)}, u32[]{:S(2)}) collective-permute-start(bf16[128,896]{1,0:T(8,128)(2,1)S(1)} %get-tuple-element.61.refs_0_), channel_id=1, source_target_pairs={{0,4},{4,0},{8,12},{12,8},{16,20},{20,16},{24,28},{28,24},{1,5},{5... | collective-permute-start | bytes 688136 | tf_op jit(solution)/shard_map/ppermute | solution.py:339
  4.9 1.6 %collective-permute-start.29 = (bf16[128,896]{1,0:T(8,128)(2,1)S(1)}, bf16[128,896]{1,0:T(8,128)(2,1)S(1)}, u32[]{:S(2)}, u32[]{:S(2)}) collective-permute-start(bf16[128,896]{1,0:T(8,128)(2,1)S(1)} %get-tuple-element.62.refs_1_), channel_id=1, source_target_pairs={{0,8},{4,12},{8,0},{12,4},{16,24},{20,28},{24,16},{28,20},{1,9},{5... | collective-permute-start | bytes 688136 | tf_op jit(solution)/shard_map/ppermute | solution.py:339
  6.5 1.6 %pack_rest.1 = (bf16[128,896]{1,0:T(8,128)(2,1)S(1)}, bf16[128,896]{1,0:T(8,128)(2,1)S(1)}, bf16[128,896]{1,0:T(8,128)(2,1)S(1)}, bf16[128,896]{1,0:T(8,128)(2,1...) custom-call(bf16[1,1,1024,896]{3,2,1,0:T(8,128)(2,1)} %grads.3, ...), custom_call_target="tpu_custom_call" | custom-call | tf_op jit(solution)/shard_map/pack_rest/pallas_call | solution.py:147
  8.1 3.0 %collective-permute-start.24 = (s32[8,128]{1,0:T(8,128)S(1)}, s32[8,128]{1,0:T(8,128)S(1)}, u32[]{:S(2)}, u32[]{:S(2)}) collective-permute-start(s32[8,128]{1,0:T(8,128)S(1)} %get-tuple-element.64), channel_id=1, source_target_pairs={{0,16},{4,20},{8,24},{12,28},{16,0},{20,4},{24,8},{28,12},{1,17},{... | collective-permute-start | bytes 12296 | tf_op jit(solution)/shard_map/ppermute | solution.py:328
  11.3 4.8 %collective-permute-done.24 = s32[8,128]{1,0:T(8,128)S(1)} collective-permute-done((s32[8,128]{1,0:T(8,128)S(1)}, s32[8,128]{1,0:T(8,128)S(1)}, u32[]{:S(2)}, u32[]{:S(2)}) %collective-permute-start.24) | collective-permute-done | bytes 4128 | tf_op jit(solution)/shard_map/ppermute | solution.py:328
  16.1 3.4 %collective-permute-start.27 = (s32[8,128]{1,0:T(8,128)S(1)}, s32[8,128]{1,0:T(8,128)S(1)}, u32[]{:S(2)}, u32[]{:S(2)}) collective-permute-start(s32[8,128]{1,0:T(8,128)S(1)} %get-tuple-element.78), channel_id=1, source_target_pairs={{0,12},{4,8},{8,4},{12,0},{16,28},{20,24},{24,20},{28,16},{1,13},{... | collective-permute-start | bytes 12296 | tf_op jit(solution)/shard_map/ppermute | solution.py:337
  19.6 1.5 %collective-permute-start.25 = (s32[8,128]{1,0:T(8,128)S(1)}, s32[8,128]{1,0:T(8,128)S(1)}, u32[]{:S(2)}, u32[]{:S(2)}) collective-permute-start(s32[8,128]{1,0:T(8,128)S(1)} %get-tuple-element.79), channel_id=1, source_target_pairs={{0,4},{4,0},{8,12},{12,8},{16,20},{20,16},{24,28},{28,24},{1,5},{5... | collective-permute-start | bytes 12296 | tf_op jit(solution)/shard_map/ppermute | solution.py:337
  21.2 3.0 %collective-permute-start.26 = (s32[8,128]{1,0:T(8,128)S(1)}, s32[8,128]{1,0:T(8,128)S(1)}, u32[]{:S(2)}, u32[]{:S(2)}) collective-permute-start(s32[8,128]{1,0:T(8,128)S(1)} %get-tuple-element.80), channel_id=1, source_target_pairs={{0,8},{4,12},{8,0},{12,4},{16,24},{20,28},{24,16},{28,20},{1,9},{5... | collective-permute-start | bytes 12296 | tf_op jit(solution)/shard_map/ppermute | solution.py:337
  24.2 1.6 %collective-permute-done.26.refs_2_ = s32[8,128]{1,0:T(8,128)S(1)} collective-permute-done((s32[8,128]{1,0:T(8,128)S(1)}, s32[8,128]{1,0:T(8,128)S(1)}, u32[]{:S(2)}, u32[]{:S(2)}) %collective-permute-start.26) | collective-permute-done | bytes 4128 | tf_op jit(solution)/shard_map/ppermute | solution.py:337
  25.8 1.7 %sum_near.1.own = bf16[136,896]{1,0:T(8,128)(2,1)S(1)} custom-call(s32[8,128]{1,0:T(8,128)S(1)} %get-tuple-element.81.refs_0_, s32[8,128]{1,0:T(8,128)S(1)} %collective-permute-done.25.refs_1_, s32[8,128]{1,0:T(8,128)S(1)} %collective-permute-done.26.refs_2_, s32[8,128]{1,0:T(8,128)S(1)} %collective-permute-done.27.refs_3_, ...), custom_call_target="tpu_custom_call" | custom-call | tf_op jit(solution)/shard_map/sum_near/pallas_call | solution.py:239
  27.5 0.6 %fusion.5 = s32[]{:T(128)} fusion(s32[4]{0:T(128)S(1)} %copy-done.1, s32[]{:T(128)S(6)} %xor.34), kind=kLoop, calls=%fused_computation.21 | loop fusion | flops 11 | bytes 24 | tf_op jit(solution)/shard_map/reduce_sum | solution.py:343
  29.1 1.6 %collective-permute-start.32 = (bf16[136,896]{1,0:T(8,128)(2,1)S(1)}, bf16[136,896]{1,0:T(8,128)(2,1)S(1)}, u32[]{:S(2)}, u32[]{:S(2)}) collective-permute-start(bf16[136,896]{1,0:T(8,128)(2,1)S(1)} %broadcast_select_fusion), channel_id=1, source_target_pairs={{0,2},{1,3},{2,0},{3,1},{4,6},{5,7},{6,4},{7,5},{8,10},{9,11},{10,... | collective-permute-start | bytes 731144 | tf_op jit(solution)/shard_map/ppermute | solution.py:347
  31.2 2.0 %collective-permute-start.34 = (bf16[128,896]{1,0:T(8,128)(2,1)S(1)}, bf16[128,896]{1,0:T(8,128)(2,1)S(1)}, u32[]{:S(2)}, u32[]{:S(2)}) collective-permute-start(bf16[128,896]{1,0:T(8,128)(2,1)S(1)} %get-tuple-element.68), channel_id=1, source_target_pairs={{0,8},{4,12},{8,0},{12,4},{16,24},{20,28},{24,16},{28,20},{1,9},{5... | collective-permute-start | bytes 688136 | tf_op jit(solution)/shard_map/ppermute | solution.py:339
  33.1 1.0 %collective-permute-start.35 = (bf16[128,896]{1,0:T(8,128)(2,1)S(1)}, bf16[128,896]{1,0:T(8,128)(2,1)S(1)}, u32[]{:S(2)}, u32[]{:S(2)}) collective-permute-start(bf16[128,896]{1,0:T(8,128)(2,1)S(1)} %get-tuple-element.69), channel_id=1, source_target_pairs={{0,12},{4,8},{8,4},{12,0},{16,28},{20,24},{24,20},{28,16},{1,13},{... | collective-permute-start | bytes 688136 | tf_op jit(solution)/shard_map/ppermute | solution.py:339
  34.1 0.7 %select_reduce_fusion = s32[]{:T(128)} fusion(s32[4]{0:T(128)S(1)} %copy-done.3, s32[4]{0:T(128)S(1)} %copy-done.1), kind=kLoop, calls=%fused_computation.9 | loop fusion | flops 79 | bytes 36 | tf_op jit(solution)/shard_map/reduce_sum | solution.py:325
  35.5 1.3 %noise.1.refs_8_ = bf16[4,128,896]{2,1,0:T(8,128)(2,1)S(1)} custom-call(s32[8,128]{1,0:T(8,128)S(1)} %get-tuple-element.81.refs_0_, s32[8,128]{1,0:T(8,128)S(1)} %collective-permute-done.25.refs_1_, s32[8,128]{1,0:T(8,128)S(1)} %collective-permute-done.26.refs_2_, s32[8,128]{1,0:T(8,128)S(1)} %collective-permute-done.27.refs_3_), custom_call_target="tpu_custom_call" | custom-call | tf_op jit(solution)/shard_map/noise/pallas_call | solution.py:188
  36.8 1.4 %collective-permute-done.33.refs_5_ = bf16[128,896]{1,0:T(8,128)(2,1)S(1)} collective-permute-done((bf16[128,896]{1,0:T(8,128)(2,1)S(1)}, bf16[128,896]{1,0:T(8,128)(2,1)S(1)}, u32[]{:S(2)}, u32[]{:S(2)}) %collective-permute-start.33) | collective-permute-done | bytes 229408 | tf_op jit(solution)/shard_map/ppermute | solution.py:339
  38.2 1.5 %collective-permute-done.34.refs_6_ = bf16[128,896]{1,0:T(8,128)(2,1)S(1)} collective-permute-done((bf16[128,896]{1,0:T(8,128)(2,1)S(1)}, bf16[128,896]{1,0:T(8,128)(2,1)S(1)}, u32[]{:S(2)}, u32[]{:S(2)}) %collective-permute-start.34) | collective-permute-done | bytes 229408 | tf_op jit(solution)/shard_map/ppermute | solution.py:339
  39.7 4.9 %collective-permute-done.35.refs_7_ = bf16[128,896]{1,0:T(8,128)(2,1)S(1)} collective-permute-done((bf16[128,896]{1,0:T(8,128)(2,1)S(1)}, bf16[128,896]{1,0:T(8,128)(2,1)S(1)}, u32[]{:S(2)}, u32[]{:S(2)}) %collective-permute-start.35) | collective-permute-done | bytes 229408 | tf_op jit(solution)/shard_map/ppermute | solution.py:339
  44.5 0.7 %sum_far.1 = bf16[128,896]{1,0:T(8,128)(2,1)S(1)} custom-call(s32[8,128]{1,0:T(8,128)S(1)} %get-tuple-element.81.refs_0_, s32[8,128]{1,0:T(8,128)S(1)} %collective-permute-done.25.refs_1_, s32[8,128]{1,0:T(8,128)S(1)} %collective-permute-done.26.refs_2_, s32[8,128]{1,0:T(8,128)S(1)} %collective-permute-done.27.refs_3_, ...), custom_call_target="tpu_custom_call" | custom-call | tf_op jit(solution)/shard_map/sum_far/pallas_call | solution.py:239
  45.2 13.9 %conditional.1 = (bf16[128,896]{1,0:T(8,128)(2,1)}) conditional(s32[]{:T(128)} %clamp.3, bf16[128,896]{1,0:T(8,128)(2,1)S(1)} %sum_far.1, bf16[128,896]{1,0:T(8,128)(2,1)S(1)} %sum_far.1, bf16[128,896]{1,0:T(8,128)(2,1)S(1)} %sum_far.1, bf16[128,896]{1,0:T(8,128)(2,1)S(1)} %sum_far.1, ...), branch_computations={%region_2.3_spmd, %region_3.4_spmd, %region_4.5_spmd, %region_5.6_... | conditional | bytes 917552 | solution.py:360
  45.4 13.7 %collective-permute-done.20 = bf16[128,896]{1,0:T(8,128)(2,1)} collective-permute-done((bf16[128,896]{1,0:T(8,128)(2,1)S(1)}, bf16[128,896]{1,0:T(8,128)(2,1)}, u32[]{:S(2)}, u32[]{:S(2)}) %collective-permute-start.20) | collective-permute-done | bytes 229408 | tf_op jit(solution)/shard_map/cond/branch_20_fun/ppermute | solution.py:357
  59.1 2.1 %update.1 = (f32[1,128,896]{2,1,0:T(8,128)}, f32[1,128,896]{2,1,0:T(8,128)}, f32[1,1]{1,0:T(1,128)}) custom-call(s32[1,4]{1,0:T(1,128)S(1)} %bitcast.2, bf16[136,896]{1,0:T(8,128)(2,1)S(1)} %sum_near.1.own, bf16[136,896]{1,0:T(8,128)(2,1)S(1)} %collective-permute-done.31.beside, bf16[136,896]{1,0:T(8,128)(2,1)S(1)} %collective-permute-done.32.across, ...), custom_call_target="tpu_custom_call" | custom-call | tf_op jit(solution)/shard_map/update/pallas_call | solution.py:293
  (25 shorter events, 1.3 us)
Async XLA Ops:
  0.6 10.5 %copy-start.2 = (s32[1,1,1024]{2,1,0:T(1,128)S(1)}, s32[1,1,1024]{2,1,0:T(1,128)}, u32[]{:S(2)}) copy-start(s32[1,1,1024]{2,1,0:T(1,128)} %param.30) | copy-start | bytes 12292
  1.8 23.9 %collective-permute-start.28 = (bf16[128,896]{1,0:T(8,128)(2,1)S(1)}, bf16[128,896]{1,0:T(8,128)(2,1)S(1)}, u32[]{:S(2)}, u32[]{:S(2)}) collective-permute-start(bf16[128,896]{1,0:T(8,128)(2,1)S(1)} %get-tuple-element.61.refs_0_), channel_id=1, source_target_pairs={{0,4},{4,0},{8,12},{12,8},{16,20},{20,16},{24,28},{28,24},{1,5},{5... | collective-permute-start | bytes 688136 | tf_op jit(solution)/shard_map/ppermute | solution.py:339
  4.9 20.8 %collective-permute-start.29 = (bf16[128,896]{1,0:T(8,128)(2,1)S(1)}, bf16[128,896]{1,0:T(8,128)(2,1)S(1)}, u32[]{:S(2)}, u32[]{:S(2)}) collective-permute-start(bf16[128,896]{1,0:T(8,128)(2,1)S(1)} %get-tuple-element.62.refs_1_), channel_id=1, source_target_pairs={{0,8},{4,12},{8,0},{12,4},{16,24},{20,28},{24,16},{28,20},{1,9},{5... | collective-permute-start | bytes 688136 | tf_op jit(solution)/shard_map/ppermute | solution.py:339
  6.5 21.1 %copy-start.1 = (s32[4]{0:T(128)S(1)}, s32[4]{0:T(128)}, u32[]{:S(2)}) copy-start(s32[4]{0:T(128)} %param.31) | copy-start | bytes 52
  6.5 27.6 %copy-start.3 = (s32[4]{0:T(128)S(1)}, s32[4]{0:T(128)}, u32[]{:S(2)}) copy-start(s32[4]{0:T(128)} %constant.43.clone) | copy-start | bytes 52
  6.5 19.3 %collective-permute-start.30 = (bf16[128,896]{1,0:T(8,128)(2,1)S(1)}, bf16[128,896]{1,0:T(8,128)(2,1)S(1)}, u32[]{:S(2)}, u32[]{:S(2)}) collective-permute-start(bf16[128,896]{1,0:T(8,128)(2,1)S(1)} %get-tuple-element.63.refs_2_), channel_id=1, source_target_pairs={{0,12},{4,8},{8,4},{12,0},{16,28},{20,24},{24,20},{28,16},{1,13},{... | collective-permute-start | bytes 688136 | tf_op jit(solution)/shard_map/ppermute | solution.py:339
  8.1 8.0 %collective-permute-start.24 = (s32[8,128]{1,0:T(8,128)S(1)}, s32[8,128]{1,0:T(8,128)S(1)}, u32[]{:S(2)}, u32[]{:S(2)}) collective-permute-start(s32[8,128]{1,0:T(8,128)S(1)} %get-tuple-element.64), channel_id=1, source_target_pairs={{0,16},{4,20},{8,24},{12,28},{16,0},{20,4},{24,8},{28,12},{1,17},{... | collective-permute-start | bytes 12296 | tf_op jit(solution)/shard_map/ppermute | solution.py:328
  16.1 5.0 %collective-permute-start.27 = (s32[8,128]{1,0:T(8,128)S(1)}, s32[8,128]{1,0:T(8,128)S(1)}, u32[]{:S(2)}, u32[]{:S(2)}) collective-permute-start(s32[8,128]{1,0:T(8,128)S(1)} %get-tuple-element.78), channel_id=1, source_target_pairs={{0,12},{4,8},{8,4},{12,0},{16,28},{20,24},{24,20},{28,16},{1,13},{... | collective-permute-start | bytes 12296 | tf_op jit(solution)/shard_map/ppermute | solution.py:337
  19.6 4.6 %collective-permute-start.25 = (s32[8,128]{1,0:T(8,128)S(1)}, s32[8,128]{1,0:T(8,128)S(1)}, u32[]{:S(2)}, u32[]{:S(2)}) collective-permute-start(s32[8,128]{1,0:T(8,128)S(1)} %get-tuple-element.79), channel_id=1, source_target_pairs={{0,4},{4,0},{8,12},{12,8},{16,20},{20,16},{24,28},{28,24},{1,5},{5... | collective-permute-start | bytes 12296 | tf_op jit(solution)/shard_map/ppermute | solution.py:337
  21.2 4.6 %collective-permute-start.26 = (s32[8,128]{1,0:T(8,128)S(1)}, s32[8,128]{1,0:T(8,128)S(1)}, u32[]{:S(2)}, u32[]{:S(2)}) collective-permute-start(s32[8,128]{1,0:T(8,128)S(1)} %get-tuple-element.80), channel_id=1, source_target_pairs={{0,8},{4,12},{8,0},{12,4},{16,24},{20,28},{24,16},{28,20},{1,9},{5... | collective-permute-start | bytes 12296 | tf_op jit(solution)/shard_map/ppermute | solution.py:337
  27.4 1.6 %collective-permute-start.31 = (bf16[136,896]{1,0:T(8,128)(2,1)S(1)}, bf16[136,896]{1,0:T(8,128)(2,1)S(1)}, u32[]{:S(2)}, u32[]{:S(2)}) collective-permute-start(bf16[136,896]{1,0:T(8,128)(2,1)S(1)} %sum_near.1.own), channel_id=1, source_target_pairs={{0,1},{1,0},{2,3},{3,2},{4,5},{5,4},{6,7},{7,6},{8,9},{9,8},{10,11... | collective-permute-start | bytes 731144 | tf_op jit(solution)/shard_map/ppermute | solution.py:345
  28.8 30.3 %copy-start = (f32[1,128,896]{2,1,0:T(8,128)S(1)}, f32[1,128,896]{2,1,0:T(8,128)}, u32[]{:S(2)}) copy-start(f32[1,128,896]{2,1,0:T(8,128)} %weight.1) | copy-start | bytes 1376260
  29.1 30.1 %collective-permute-start.32 = (bf16[136,896]{1,0:T(8,128)(2,1)S(1)}, bf16[136,896]{1,0:T(8,128)(2,1)S(1)}, u32[]{:S(2)}, u32[]{:S(2)}) collective-permute-start(bf16[136,896]{1,0:T(8,128)(2,1)S(1)} %broadcast_select_fusion), channel_id=1, source_target_pairs={{0,2},{1,3},{2,0},{3,1},{4,6},{5,7},{6,4},{7,5},{8,10},{9,11},{10,... | collective-permute-start | bytes 731144 | tf_op jit(solution)/shard_map/ppermute | solution.py:347
  30.6 7.5 %collective-permute-start.33 = (bf16[128,896]{1,0:T(8,128)(2,1)S(1)}, bf16[128,896]{1,0:T(8,128)(2,1)S(1)}, u32[]{:S(2)}, u32[]{:S(2)}) collective-permute-start(bf16[128,896]{1,0:T(8,128)(2,1)S(1)} %get-tuple-element.67), channel_id=1, source_target_pairs={{0,4},{4,0},{8,12},{12,8},{16,20},{20,16},{24,28},{28,24},{1,5},{5... | collective-permute-start | bytes 688136 | tf_op jit(solution)/shard_map/ppermute | solution.py:339
  31.2 8.5 %collective-permute-start.34 = (bf16[128,896]{1,0:T(8,128)(2,1)S(1)}, bf16[128,896]{1,0:T(8,128)(2,1)S(1)}, u32[]{:S(2)}, u32[]{:S(2)}) collective-permute-start(bf16[128,896]{1,0:T(8,128)(2,1)S(1)} %get-tuple-element.68), channel_id=1, source_target_pairs={{0,8},{4,12},{8,0},{12,4},{16,24},{20,28},{24,16},{28,20},{1,9},{5... | collective-permute-start | bytes 688136 | tf_op jit(solution)/shard_map/ppermute | solution.py:339
  33.1 11.4 %collective-permute-start.35 = (bf16[128,896]{1,0:T(8,128)(2,1)S(1)}, bf16[128,896]{1,0:T(8,128)(2,1)S(1)}, u32[]{:S(2)}, u32[]{:S(2)}) collective-permute-start(bf16[128,896]{1,0:T(8,128)(2,1)S(1)} %get-tuple-element.69), channel_id=1, source_target_pairs={{0,12},{4,8},{8,4},{12,0},{16,28},{20,24},{24,20},{28,16},{1,13},{... | collective-permute-start | bytes 688136 | tf_op jit(solution)/shard_map/ppermute | solution.py:339
  45.3 13.9 %collective-permute-start.20 = (bf16[128,896]{1,0:T(8,128)(2,1)S(1)}, bf16[128,896]{1,0:T(8,128)(2,1)}, u32[]{:S(2)}, u32[]{:S(2)}) collective-permute-start(bf16[128,896]{1,0:T(8,128)(2,1)S(1)} %param.20), channel_id=1, source_target_pairs={{0,19},{1,17},{2,16},{3,18},{4,23},{5,21},{6,20},{7,22},{8,27},{9,... | collective-permute-start | bytes 688136 | tf_op jit(solution)/shard_map/cond/branch_20_fun/ppermute | solution.py:357

commit v4 on v3

--- a/solution.py
+++ b/solution.py
@@ -106,53 +106,71 @@
     outs, sems = refs[:-1], refs[-1]
     me = lax.axis_index("dp")
     copies = []
-    for near in range(1, square):
-        out = outs[near - 1]
-        copy = pltpu.make_async_copy(block_at(grads, me ^ near, out.shape[0]), out, sems.at[near - 1])
-        copy.start()
-        copies.append(copy)
+    for number, out in enumerate(outs):
+        source = block_at(grads, me ^ (number + 1), out.shape[0])
+        copies.append(pltpu.make_async_copy(source, out, sems.at[number]))
+        copies[-1].start()
     for copy in copies:
         copy.wait()
 
 
-def second_kernel(grads, *refs):
-    given, outs, levels, sems = refs[: square - 1], refs[square - 1 : -2], refs[-2], refs[-1]
+def second_kernel(given_count, grads, offsets, *refs):
+    given, outs, rest = refs[:given_count], refs[given_count:-3], refs[-3:]
+    mine, posted, sems = rest
     me = lax.axis_index("dp")
-    targets = [me] + [me ^ square ^ near for near in range(square)]
+    targets = [me ^ turn for turn in (0, *range(given_count + 1, 2 * square))]
     copies = []
     for number, target in enumerate(targets):
-        out = outs[number]
-        copy = pltpu.make_async_copy(block_at(grads, target, out.shape[0]), out, sems.at[number])
-        copy.start()
-        copies.append(copy)
-    lanes = lax.broadcasted_iota(jnp.int32, levels.shape, 1)
-    peaks = jnp.zeros(levels.shape, jnp.float32)
-    for near in range(1, square):
-        peaks = jnp.where(lanes == (me ^ near), largest(given[near - 1]), peaks)
+        source = block_at(grads, target, outs[number].shape[0])
+        copies.append(pltpu.make_async_copy(source, outs[number], sems.at[number]))
+        copies[-1].start()
+    for row, turn in enumerate((0, square, 2, 2 ^ square)):
+        mine[row : row + 1, :] = offsets[pl.ds(me ^ turn, 1), :]
+        posted[row : row + 1, :] = offsets[pl.ds(me ^ 1 ^ turn, 1), :]
+    shape = (mine.shape[0] - square, mine.shape[1])
+    lanes = lax.broadcasted_iota(jnp.int32, shape, 1)
+    peaks = jnp.zeros(shape, jnp.float32)
+    for number in range(given_count):
+        peaks = jnp.where(lanes == (me ^ (number + 1)), largest(given[number]), peaks)
     for number, target in enumerate(targets):
         copies[number].wait()
         peaks = jnp.where(lanes == target, largest(outs[number]), peaks)
-    counts = [jnp.zeros(levels.shape, jnp.int32) for _ in range(4)]
+    counts = [jnp.zeros(shape, jnp.int32) for _ in range(4)]
     for power in range(low_power, high_power):
         counts[power % 4] += (peaks >= jnp.float32(2.0**power)).astype(jnp.int32)
-    levels[...] = (counts[0] + counts[1]) + (counts[2] + counts[3])
-
-
-def pack(grads, rows, given):
-    width = grads.shape[-1]
+    levels = (counts[0] + counts[1]) + (counts[2] + counts[3])
+    mine[square:, :] = levels
+    posted[square:, :] = levels
+
+
+def pack_first(grads, rows, count):
+    vmem = pl.BlockSpec(memory_space=pltpu.VMEM)
+    return pl.pallas_call(
+        first_kernel,
+        out_shape=[jax.ShapeDtypeStruct((rows, grads.shape[-1]), grads.dtype)] * count,
+        in_specs=[pl.BlockSpec(memory_space=pltpu.HBM)],
+        out_specs=[vmem] * count,
+        scratch_shapes=[pltpu.SemaphoreType.DMA((count,))],
+        compiler_params=pltpu.CompilerParams(vmem_limit_bytes=8 * 2**20),
+        name="pack_first",
+    )(pltpu.with_memory_space_constraint(grads, pltpu.HBM))
+
+
+def pack_second(grads, offsets, given):
+    rows, width = given[0].shape
+    count = 2 * square - len(given)
     vmem = pl.BlockSpec(memory_space=pltpu.VMEM)
     block = jax.ShapeDtypeStruct((rows, width), grads.dtype)
-    count = square + 1 if given else square - 1
-    levels = [jax.ShapeDtypeStruct((8, rows), jnp.int32)] if given else []
-    return pl.pallas_call(
-        second_kernel if given else first_kernel,
-        out_shape=[block] * count + levels,
-        in_specs=[pl.BlockSpec(memory_space=pltpu.HBM)] + [vmem] * len(given),
-        out_specs=[vmem] * (count + len(levels)),
+    note = jax.ShapeDtypeStruct((8, rows), jnp.int32)
+    return pl.pallas_call(
+        functools.partial(second_kernel, len(given)),
+        out_shape=[block] * count + [note] * 2,
+        in_specs=[pl.BlockSpec(memory_space=pltpu.HBM)] + [vmem] * (1 + len(given)),
+        out_specs=[vmem] * (count + 2),
         scratch_shapes=[pltpu.SemaphoreType.DMA((count,))],
         compiler_params=pltpu.CompilerParams(vmem_limit_bytes=8 * 2**20),
-        name="pack_rest" if given else "pack_own",
-    )(pltpu.with_memory_space_constraint(grads, pltpu.HBM), *given)
+        name="pack_second",
+    )(pltpu.with_memory_space_constraint(grads, pltpu.HBM), offsets, *given)
 
 
 def noise_of(codes, columns):
@@ -163,14 +181,10 @@
     return jnp.bitwise_and(jnp.right_shift(mixed, 12), 255).astype(jnp.float32) * (1.0 / 256.0)
 
 
-def fill_codes(far, notes, codes):
-    seeds = jnp.concatenate([note[far : far + 1, :] for note in notes] * 2)
-    codes[...] = jnp.transpose(seeds) * 747796405 + 1013904223
-
-
-def noise_kernel(far, *refs):
-    notes, out, codes = refs[:square], refs[square], refs[square + 1]
-    fill_codes(far, notes, codes)
+def noise_kernel(far, mine, beside, above, out, codes):
+    rows = [mine[far : far + 1, :], beside[far : far + 1, :]]
+    rows += [above[far : far + 1, :], above[far + 2 : far + 3, :]]
+    codes[...] = jnp.transpose(jnp.concatenate(rows * 2)) * 747796405 + 1013904223
     height, width = 16, out.shape[2]
     columns = lax.broadcasted_iota(jnp.int32, (1, width), 1) * 747796405
 
@@ -188,38 +202,30 @@
     return pl.pallas_call(
         functools.partial(noise_kernel, far),
         out_shape=jax.ShapeDtypeStruct((square, rows, width), jnp.bfloat16),
-        in_specs=[vmem] * square,
+        in_specs=[vmem] * len(notes),
         out_specs=vmem,
         scratch_shapes=[pltpu.VMEM((rows, 2 * square), jnp.int32)],
         compiler_params=pltpu.CompilerParams(vmem_limit_bytes=8 * 2**20),
-        name="noise",
+        name="noise_far" if far else "noise_near",
     )(*notes)
 
 
-def sum_kernel(far, rows, *refs):
-    notes, raws, rest = refs[:square], refs[square : 2 * square], refs[2 * square :]
-    noise, out, codes = (None, *rest) if far == 0 else (*rest, None)
+def sum_kernel(far, levels, twin, noise, *refs):
+    raws, out = refs[:square], refs[square]
     target = lax.axis_index("dp") ^ (far * square)
-    counts = notes[0][2:3, :]
-    for note in notes[1:]:
-        counts = jnp.maximum(counts, note[2:3, :])
+    counts = jnp.maximum(levels[0:1, :], twin[0:1, :])
     lanes = lax.broadcasted_iota(jnp.int32, counts.shape, 1)
     reached = jnp.where(lanes == target, counts, 0).astype(jnp.float32)
     exponent = jnp.max(reached, axis=1, keepdims=True).astype(jnp.int32) + (low_power - level_bits)
     inverse_step = power_of_two(-exponent)
-    height, width = 16, raws[0].shape[1]
-    columns = lax.broadcasted_iota(jnp.int32, (1, width), 1) * 747796405
-    if noise is None:
-        fill_codes(far, notes, codes)
+    height = 16
+    rows, width = raws[0].shape
 
     def step(index, carry):
         span = pl.ds(pl.multiple_of(index * height, height), height)
         total = jnp.zeros((height, width), jnp.float32)
         for near in range(square):
-            if noise is None:
-                drawn = noise_of(codes[span, near : near + 1], columns)
-            else:
-                drawn = noise[near, span, :].astype(jnp.float32)
+            drawn = noise[near, span, :].astype(jnp.float32)
             scaled = raws[near][span, :].astype(jnp.float32) * inverse_step
             floor_part = jnp.floor(scaled)
             total = total + (floor_part + jnp.floor(scaled - floor_part + drawn))
@@ -232,19 +238,17 @@
         out[rows:, :] = jnp.broadcast_to(power_of_two(exponent), tail).astype(jnp.bfloat16)
 
 
-def sum_counts(far, notes, raws, noise, extra):
+def sum_counts(far, levels, twin, noise, raws, extra):
     rows, width = raws[0].shape
     vmem = pl.BlockSpec(memory_space=pltpu.VMEM)
-    more = [noise] if far else []
-    return pl.pallas_call(
-        functools.partial(sum_kernel, far, rows),
+    return pl.pallas_call(
+        functools.partial(sum_kernel, far),
         out_shape=jax.ShapeDtypeStruct((rows + extra, width), jnp.bfloat16),
-        in_specs=[vmem] * (2 * square + len(more)),
+        in_specs=[vmem] * (3 + square),
         out_specs=vmem,
-        scratch_shapes=[] if far else [pltpu.VMEM((rows, 2 * square), jnp.int32)],
         compiler_params=pltpu.CompilerParams(vmem_limit_bytes=8 * 2**20),
         name="sum_far" if far else "sum_near",
-    )(*notes, *raws, *more)
+    )(levels, twin, noise, *raws)
 
 
 def update_kernel(dp_count, slots, own, beside, across, arrived, weight, *refs):
@@ -286,7 +290,7 @@
 
 def update(slots, own, beside, across, arrived, weight, dp_count):
     rows, width = arrived.shape
-    parts = 4
+    parts = 8
     vmem = pl.BlockSpec(memory_space=pltpu.VMEM)
     hbm = pl.BlockSpec(memory_space=pltpu.HBM)
     block = jax.ShapeDtypeStruct((1, rows, width), jnp.float32)
@@ -312,41 +316,37 @@
     expert_count = lax.axis_size("expert")
     row_count, hidden = expert_grads.shape[2:]
     block_rows = row_count // dp_count
-    me = lax.axis_index("dp")
     place = lax.axis_index("expert")
     offsets = round_offsets[0, 0].reshape(dp_count, block_rows)
-
-    def pick(array, index):
-        return lax.dynamic_index_in_dim(array, index, 0, keepdims=False)
 
     after = jnp.arange(expert_count)[None, :] > jnp.arange(expert_count)[:, None]
     weights = jnp.array([6, 2, 1, 0], jnp.int32)[:, None]
     lower = (slot_expert[:, None] > slot_expert[None, :]) & after
     branch = jnp.sum(jnp.where(lower, weights, 0))
-    near_blocks = pack(expert_grads, block_rows, [])
-    *rest, levels = pack(expert_grads, block_rows, near_blocks)
+    near_blocks = pack_first(expert_grads, block_rows, 2)
+    here, diagonal, *far_blocks, mine, posted = pack_second(expert_grads, offsets, near_blocks)
+    raw = [[here, near_blocks[0], near_blocks[1], diagonal], far_blocks]
+    for far in range(2):
+        for near in range(1, square):
+            raw[far][near] = lax.ppermute(raw[far][near], "dp", flips(dp_count, near))
+
+    aside = lax.ppermute(posted, "dp", flips(dp_count, 1))
+    levels = jnp.maximum(mine[square:], aside[square:])
+    upward = jnp.concatenate([mine[2:square], aside[2:square], levels])
+    above = lax.ppermute(upward, "dp", flips(dp_count, 2))
+    levels = jnp.maximum(levels, above[square:])
     twin = lax.ppermute(levels, "dp", flips(dp_count, square))
-    levels = jnp.maximum(levels[0], twin[0])
-
-    raw, notes = [[rest[0], *near_blocks], rest[1:]], []
-    for near in range(square):
-        seeds = [pick(offsets, (me ^ near) ^ (far * square)) for far in range(2)]
-        note = jnp.concatenate([jnp.stack(seeds + [levels]), jnp.zeros((5, block_rows), jnp.int32)])
-        if near:
-            pairs = flips(dp_count, near)
-            note = lax.ppermute(note, "dp", pairs)
-            for far in range(2):
-                raw[far][near] = lax.ppermute(raw[far][near], "dp", pairs)
-        notes.append(note)
+    noise = []
+    for far in range(2):
+        noise.append(make_noise(far, (mine, aside, above), block_rows, hidden))
 
     wanted = slot_expert == (place ^ 2)
     crossing = jnp.sum(jnp.where(wanted, jnp.arange(expert_count), 0)) == place
-    own = sum_counts(0, notes, raw[0], None, 8)
+    own = sum_counts(0, levels, twin, noise[0], raw[0], 8)
     beside = lax.ppermute(own, "expert", flips(expert_count, 1))
     across_wants = jnp.where(crossing, own, beside)
     across = lax.ppermute(across_wants, "expert", flips(expert_count, 2))
-    noise = make_noise(1, notes, block_rows, hidden)
-    message = sum_counts(1, notes, raw[1], noise, 0)
+    message = sum_counts(1, levels, twin, noise[1], raw[1], 0)
 
     def route(order):
         pairs = [

time: 61.4 us -> 57.7 us (0.940)
  starting transfers between devices: 20.9 us -> 17.3 us
    ppermute x9 -> x8, starting transfers between devices: 16.1 us -> 12.8 us  [the longest x6 7.58 us: staged_body(): raw[far][near] = lax.ppermute(raw[far][near], 'dp', flips(dp_count, near))]
    ppermute x1, waiting for transfers between devices: 4.8 us -> 2.65 us  [staged_body(): twin = lax.ppermute(levels, 'dp', flips(dp_count, square))]
    ppermute x9 -> x8, waiting for transfers between devices: 9.41 us -> 11.3 us  [the longest x6 9.73 us: staged_body(): raw[far][near] = lax.ppermute(raw[far][near], 'dp', flips(dp_count, near))]
    pallas_call x1 -> x2, Pallas kernels: 1.31 us -> 2.62 us  [make_noise(): pl.pallas_call(functools.partial(noise_kernel, far), out_shape=jax.ShapeD...]
    pallas_call x4, Pallas kernels: 5.21 us -> 4.2 us  [the longest x1 1.72 us: pack_second(): pl.pallas_call(functools.partial(second_kernel, len(given)), out_shape=[b...]
  transfers between devices with their start and end apart: 13 -> 12, of which waited for: 8 -> 8; matrix products, arithmetic and copies ran while one was open for 2% -> 2% of each run, Pallas kernels for 6% -> 6%
where the time goes in v4:
time: 57.7 us; the launch traced here: 57.5 us
  waiting for transfers between devices  27.8 us (48%)
  starting transfers between devices  17.3 us (30%)
  Pallas kernels  8.92 us (15%)
  between operations  2.07 us (4%)
  other arithmetic  1.38 us (2%)
    ppermute x1, waiting for transfers between devices, route(): return lambda parts: lax.ppermute(parts, ('dp', 'expert'), pairs)  13.6 us
    ppermute x6, waiting for transfers between devices, staged_body(): raw[far][near] = lax.ppermute(raw[far][near], 'dp', flips(dp_count, near))  9.73 us
    ppermute x6, starting transfers between devices, staged_body(): raw[far][near] = lax.ppermute(raw[far][near], 'dp', flips(dp_count, near))  7.58 us
    ppermute x1, starting transfers between devices, staged_body(): aside = lax.ppermute(posted, 'dp', flips(dp_count, 1))  3.06 us
    ppermute x1, starting transfers between devices, staged_body(): twin = lax.ppermute(levels, 'dp', flips(dp_count, square))  2.65 us
    ppermute x1, waiting for transfers between devices, staged_body(): twin = lax.ppermute(levels, 'dp', flips(dp_count, square))  2.65 us
    pallas_call x2, Pallas kernels, make_noise(): pl.pallas_call(functools.partial(noise_kernel, far), out_shape=jax.ShapeD...  2.62 us
    ppermute x1, starting transfers between devices, staged_body(): above = lax.ppermute(upward, 'dp', flips(dp_count, 2))  2.14 us
  transfers between devices with their start and end apart: 12, of which 8 were waited for; matrix products, arithmetic and copies ran while one was open for 2% of the time, Pallas kernels for 6%

profile of v4, /device:TPU:0, one launch (start us, length us, event | category | flops | bytes accessed | tf_op | source)
XLA Modules:
  0.0 57.5 jit_solution(7014812657690022210)
XLA Ops:
  0.6 1.1 %pack_first.1 = (bf16[128,896]{1,0:T(8,128)(2,1)S(1)}, bf16[128,896]{1,0:T(8,128)(2,1)S(1)}) custom-call(bf16[1,1,1024,896]{3,2,1,0:T(8,128)(2,1)} %grads.3), custom_call_target="tpu_custom_call" | custom-call | tf_op jit(solution)/shard_map/pack_first/pallas_call | solution.py:148
  1.7 1.7 %pack_second.1 = (bf16[128,896]{1,0:T(8,128)(2,1)S(1)}, bf16[128,896]{1,0:T(8,128)(2,1)S(1)}, bf16[128,896]{1,0:T(8,128)(2,1)S(1)}, bf16[128,896]{1,0:T(8,128)(2...) custom-call(bf16[1,1,1024,896]{3,2,1,0:T(8,128)(2,1)} %grads.3, ...), custom_call_target="tpu_custom_call" | custom-call | tf_op jit(solution)/shard_map/pack_second/pallas_call | solution.py:165
  3.5 3.1 %collective-permute-start.24 = (s32[8,128]{1,0:T(8,128)S(1)}, s32[8,128]{1,0:T(8,128)S(1)}, u32[]{:S(2)}, u32[]{:S(2)}) collective-permute-start(s32[8,128]{1,0:T(8,128)S(1)} %get-tuple-element.65), channel_id=1, source_target_pairs={{0,4},{4,0},{8,12},{12,8},{16,20},{20,16},{24,28},{28,24},{1,5},{5... | collective-permute-start | bytes 12296 | tf_op jit(solution)/shard_map/ppermute | solution.py:333
  6.5 1.6 %collective-permute-done.24.beside = s32[8,128]{1,0:T(8,128)S(1)} collective-permute-done((s32[8,128]{1,0:T(8,128)S(1)}, s32[8,128]{1,0:T(8,128)S(1)}, u32[]{:S(2)}, u32[]{:S(2)}) %collective-permute-start.24) | collective-permute-done | bytes 4128 | tf_op jit(solution)/shard_map/ppermute | solution.py:333
  8.2 2.1 %collective-permute-start.25 = (s32[8,128]{1,0:T(8,128)S(1)}, s32[8,128]{1,0:T(8,128)S(1)}, u32[]{:S(2)}, u32[]{:S(2)}) collective-permute-start(s32[8,128]{1,0:T(8,128)S(1)} %pad_add_fusion), channel_id=1, source_target_pairs={{0,8},{4,12},{8,0},{12,4},{16,24},{20,28},{24,16},{28,20},{1,9},{5... | collective-permute-start | bytes 12296 | tf_op jit(solution)/shard_map/ppermute | solution.py:336
  10.3 1.5 %collective-permute-start.27 = (bf16[128,896]{1,0:T(8,128)(2,1)S(1)}, bf16[128,896]{1,0:T(8,128)(2,1)S(1)}, u32[]{:S(2)}, u32[]{:S(2)}) collective-permute-start(bf16[128,896]{1,0:T(8,128)(2,1)S(1)} %get-tuple-element.62.refs_0_), channel_id=1, source_target_pairs={{0,4},{4,0},{8,12},{12,8},{16,20},{20,16},{24,28},{28,24},{1,5},{5... | collective-permute-start | bytes 688136 | tf_op jit(solution)/shard_map/ppermute | solution.py:331
  12.3 1.5 %collective-permute-start.29 = (bf16[128,896]{1,0:T(8,128)(2,1)S(1)}, bf16[128,896]{1,0:T(8,128)(2,1)S(1)}, u32[]{:S(2)}, u32[]{:S(2)}) collective-permute-start(bf16[128,896]{1,0:T(8,128)(2,1)S(1)} %get-tuple-element.67), channel_id=1, source_target_pairs={{0,12},{4,8},{8,4},{12,0},{16,28},{20,24},{24,20},{28,16},{1,13},{... | collective-permute-start | bytes 688136 | tf_op jit(solution)/shard_map/ppermute | solution.py:331
  13.8 2.7 %collective-permute-start.26 = (s32[4,128]{1,0:T(4,128)S(1)}, s32[4,128]{1,0:T(4,128)S(1)}, u32[]{:S(2)}, u32[]{:S(2)}) collective-permute-start(s32[4,128]{1,0:T(4,128)S(1)} %slice_maximum_fusion.levels), channel_id=1, source_target_pairs={{0,16},{4,20},{8,24},{12,28},{16,0},{20,4},{24,8},{28,12},{1,17},{... | collective-permute-start | bytes 6152 | tf_op jit(solution)/shard_map/ppermute | solution.py:338
  16.5 1.3 %noise_near.1.noise = bf16[4,128,896]{2,1,0:T(8,128)(2,1)S(1)} custom-call(s32[8,128]{1,0:T(8,128)S(1)} %get-tuple-element.64.mine, s32[8,128]{1,0:T(8,128)S(1)} %collective-permute-done.24.beside, s32[8,128]{1,0:T(8,128)S(1)} %collective-permute-done.25.above), custom_call_target="tpu_custom_call" | custom-call | tf_op jit(solution)/shard_map/noise_near/pallas_call | solution.py:202
  17.8 2.6 %collective-permute-done.26.twin = s32[4,128]{1,0:T(4,128)S(1)} collective-permute-done((s32[4,128]{1,0:T(4,128)S(1)}, s32[4,128]{1,0:T(4,128)S(1)}, u32[]{:S(2)}, u32[]{:S(2)}) %collective-permute-start.26) | collective-permute-done | bytes 2080 | tf_op jit(solution)/shard_map/ppermute | solution.py:338
  20.4 2.0 %collective-permute-done.29.refs_3_ = bf16[128,896]{1,0:T(8,128)(2,1)S(1)} collective-permute-done((bf16[128,896]{1,0:T(8,128)(2,1)S(1)}, bf16[128,896]{1,0:T(8,128)(2,1)S(1)}, u32[]{:S(2)}, u32[]{:S(2)}) %collective-permute-start.29) | collective-permute-done | bytes 229408 | tf_op jit(solution)/shard_map/ppermute | solution.py:331
  22.4 0.7 %sum_near.1.own = bf16[136,896]{1,0:T(8,128)(2,1)S(1)} custom-call(s32[4,128]{1,0:T(4,128)S(1)} %slice_maximum_fusion.levels, s32[4,128]{1,0:T(4,128)S(1)} %collective-permute-done.26.twin, bf16[4,128,896]{2,1,0:T(8,128)(2,1)S(1)} %noise_near.1.noise, bf16[128,896]{1,0:T(8,128)(2,1)S(1)} %get-tuple-element.66.refs_0_, ...), custom_call_target="tpu_custom_call" | custom-call | tf_op jit(solution)/shard_map/sum_near/pallas_call | solution.py:244
  24.7 1.6 %collective-permute-start.31 = (bf16[136,896]{1,0:T(8,128)(2,1)S(1)}, bf16[136,896]{1,0:T(8,128)(2,1)S(1)}, u32[]{:S(2)}, u32[]{:S(2)}) collective-permute-start(bf16[136,896]{1,0:T(8,128)(2,1)S(1)} %broadcast_select_fusion), channel_id=1, source_target_pairs={{0,2},{1,3},{2,0},{3,1},{4,6},{5,7},{6,4},{7,5},{8,10},{9,11},{10,... | collective-permute-start | bytes 731144 | tf_op jit(solution)/shard_map/ppermute | solution.py:348
  26.3 1.5 %collective-permute-start.32 = (bf16[128,896]{1,0:T(8,128)(2,1)S(1)}, bf16[128,896]{1,0:T(8,128)(2,1)S(1)}, u32[]{:S(2)}, u32[]{:S(2)}) collective-permute-start(bf16[128,896]{1,0:T(8,128)(2,1)S(1)} %get-tuple-element.69), channel_id=1, source_target_pairs={{0,4},{4,0},{8,12},{12,8},{16,20},{20,16},{24,28},{28,24},{1,5},{5... | collective-permute-start | bytes 688136 | tf_op jit(solution)/shard_map/ppermute | solution.py:331
  27.7 1.7 %collective-permute-start.33 = (bf16[128,896]{1,0:T(8,128)(2,1)S(1)}, bf16[128,896]{1,0:T(8,128)(2,1)S(1)}, u32[]{:S(2)}, u32[]{:S(2)}) collective-permute-start(bf16[128,896]{1,0:T(8,128)(2,1)S(1)} %get-tuple-element.70), channel_id=1, source_target_pairs={{0,8},{4,12},{8,0},{12,4},{16,24},{20,28},{24,16},{28,20},{1,9},{5... | collective-permute-start | bytes 688136 | tf_op jit(solution)/shard_map/ppermute | solution.py:331
  29.4 0.9 %collective-permute-start.34 = (bf16[128,896]{1,0:T(8,128)(2,1)S(1)}, bf16[128,896]{1,0:T(8,128)(2,1)S(1)}, u32[]{:S(2)}, u32[]{:S(2)}) collective-permute-start(bf16[128,896]{1,0:T(8,128)(2,1)S(1)} %get-tuple-element.71), channel_id=1, source_target_pairs={{0,12},{4,8},{8,4},{12,0},{16,28},{20,24},{24,20},{28,16},{1,13},{... | collective-permute-start | bytes 688136 | tf_op jit(solution)/shard_map/ppermute | solution.py:331
  30.4 0.7 %select_reduce_fusion = s32[]{:T(128)} fusion(s32[4]{0:T(128)S(1)} %copy-done.3, s32[4]{0:T(128)S(1)} %copy-done.1), kind=kLoop, calls=%fused_computation.2 | loop fusion | flops 79 | bytes 36 | tf_op jit(solution)/shard_map/reduce_sum | solution.py:325
  31.7 1.3 %noise_far.1.noise = bf16[4,128,896]{2,1,0:T(8,128)(2,1)S(1)} custom-call(s32[8,128]{1,0:T(8,128)S(1)} %get-tuple-element.64.mine, s32[8,128]{1,0:T(8,128)S(1)} %collective-permute-done.24.beside, s32[8,128]{1,0:T(8,128)S(1)} %collective-permute-done.25.above), custom_call_target="tpu_custom_call" | custom-call | tf_op jit(solution)/shard_map/noise_far/pallas_call | solution.py:202
  33.0 0.8 %collective-permute-done.32.refs_1_ = bf16[128,896]{1,0:T(8,128)(2,1)S(1)} collective-permute-done((bf16[128,896]{1,0:T(8,128)(2,1)S(1)}, bf16[128,896]{1,0:T(8,128)(2,1)S(1)}, u32[]{:S(2)}, u32[]{:S(2)}) %collective-permute-start.32) | collective-permute-done | bytes 229408 | tf_op jit(solution)/shard_map/ppermute | solution.py:331
  33.8 2.4 %collective-permute-done.33.refs_2_ = bf16[128,896]{1,0:T(8,128)(2,1)S(1)} collective-permute-done((bf16[128,896]{1,0:T(8,128)(2,1)S(1)}, bf16[128,896]{1,0:T(8,128)(2,1)S(1)}, u32[]{:S(2)}, u32[]{:S(2)}) %collective-permute-start.33) | collective-permute-done | bytes 229408 | tf_op jit(solution)/shard_map/ppermute | solution.py:331
  36.2 4.6 %collective-permute-done.34.refs_3_ = bf16[128,896]{1,0:T(8,128)(2,1)S(1)} collective-permute-done((bf16[128,896]{1,0:T(8,128)(2,1)S(1)}, bf16[128,896]{1,0:T(8,128)(2,1)S(1)}, u32[]{:S(2)}, u32[]{:S(2)}) %collective-permute-start.34) | collective-permute-done | bytes 229408 | tf_op jit(solution)/shard_map/ppermute | solution.py:331
  41.5 13.9 %conditional.1 = (bf16[128,896]{1,0:T(8,128)(2,1)}) conditional(s32[]{:T(128)} %clamp.3, bf16[128,896]{1,0:T(8,128)(2,1)S(1)} %sum_far.1, bf16[128,896]{1,0:T(8,128)(2,1)S(1)} %sum_far.1, bf16[128,896]{1,0:T(8,128)(2,1)S(1)} %sum_far.1, bf16[128,896]{1,0:T(8,128)(2,1)S(1)} %sum_far.1, ...), branch_computations={%region_2.3_spmd, %region_3.4_spmd, %region_4.5_spmd, %region_5.6_... | conditional | bytes 917552 | solution.py:360
  41.8 13.6 %collective-permute-done.20 = bf16[128,896]{1,0:T(8,128)(2,1)} collective-permute-done((bf16[128,896]{1,0:T(8,128)(2,1)S(1)}, bf16[128,896]{1,0:T(8,128)(2,1)}, u32[]{:S(2)}, u32[]{:S(2)}) %collective-permute-start.20) | collective-permute-done | bytes 229408 | tf_op jit(solution)/shard_map/cond/branch_20_fun/ppermute | solution.py:357
  55.4 2.1 %update.1 = (f32[1,128,896]{2,1,0:T(8,128)}, f32[1,128,896]{2,1,0:T(8,128)}, f32[1,1]{1,0:T(1,128)}) custom-call(s32[1,4]{1,0:T(1,128)S(1)} %bitcast.2, bf16[136,896]{1,0:T(8,128)(2,1)S(1)} %sum_near.1.own, bf16[136,896]{1,0:T(8,128)(2,1)S(1)} %collective-permute-done.30.beside, bf16[136,896]{1,0:T(8,128)(2,1)S(1)} %collective-permute-done.31.across, ...), custom_call_target="tpu_custom_call" | custom-call | tf_op jit(solution)/shard_map/update/pallas_call | solution.py:297
  (24 shorter events, 2.3 us)
Async XLA Ops:
  0.6 1.1 %copy-start.2 = (s32[1,1,1024]{2,1,0:T(1,128)S(1)}, s32[1,1,1024]{2,1,0:T(1,128)}, u32[]{:S(2)}) copy-start(s32[1,1,1024]{2,1,0:T(1,128)} %param.30) | copy-start | bytes 12292
  3.5 19.7 %copy-start.1 = (s32[4]{0:T(128)S(1)}, s32[4]{0:T(128)}, u32[]{:S(2)}) copy-start(s32[4]{0:T(128)} %param.31) | copy-start | bytes 52
  3.5 4.6 %collective-permute-start.24 = (s32[8,128]{1,0:T(8,128)S(1)}, s32[8,128]{1,0:T(8,128)S(1)}, u32[]{:S(2)}, u32[]{:S(2)}) collective-permute-start(s32[8,128]{1,0:T(8,128)S(1)} %get-tuple-element.65), channel_id=1, source_target_pairs={{0,4},{4,0},{8,12},{12,8},{16,20},{20,16},{24,28},{28,24},{1,5},{5... | collective-permute-start | bytes 12296 | tf_op jit(solution)/shard_map/ppermute | solution.py:333
  8.2 5.6 %collective-permute-start.25 = (s32[8,128]{1,0:T(8,128)S(1)}, s32[8,128]{1,0:T(8,128)S(1)}, u32[]{:S(2)}, u32[]{:S(2)}) collective-permute-start(s32[8,128]{1,0:T(8,128)S(1)} %pad_add_fusion), channel_id=1, source_target_pairs={{0,8},{4,12},{8,0},{12,4},{16,24},{20,28},{24,16},{28,20},{1,9},{5... | collective-permute-start | bytes 12296 | tf_op jit(solution)/shard_map/ppermute | solution.py:336
  10.3 10.1 %collective-permute-start.27 = (bf16[128,896]{1,0:T(8,128)(2,1)S(1)}, bf16[128,896]{1,0:T(8,128)(2,1)S(1)}, u32[]{:S(2)}, u32[]{:S(2)}) collective-permute-start(bf16[128,896]{1,0:T(8,128)(2,1)S(1)} %get-tuple-element.62.refs_0_), channel_id=1, source_target_pairs={{0,4},{4,0},{8,12},{12,8},{16,20},{20,16},{24,28},{28,24},{1,5},{5... | collective-permute-start | bytes 688136 | tf_op jit(solution)/shard_map/ppermute | solution.py:331
  11.8 8.6 %collective-permute-start.28 = (bf16[128,896]{1,0:T(8,128)(2,1)S(1)}, bf16[128,896]{1,0:T(8,128)(2,1)S(1)}, u32[]{:S(2)}, u32[]{:S(2)}) collective-permute-start(bf16[128,896]{1,0:T(8,128)(2,1)S(1)} %get-tuple-element.63.refs_1_), channel_id=1, source_target_pairs={{0,8},{4,12},{8,0},{12,4},{16,24},{20,28},{24,16},{28,20},{1,9},{5... | collective-permute-start | bytes 688136 | tf_op jit(solution)/shard_map/ppermute | solution.py:331
  12.3 10.1 %collective-permute-start.29 = (bf16[128,896]{1,0:T(8,128)(2,1)S(1)}, bf16[128,896]{1,0:T(8,128)(2,1)S(1)}, u32[]{:S(2)}, u32[]{:S(2)}) collective-permute-start(bf16[128,896]{1,0:T(8,128)(2,1)S(1)} %get-tuple-element.67), channel_id=1, source_target_pairs={{0,12},{4,8},{8,4},{12,0},{16,28},{20,24},{24,20},{28,16},{1,13},{... | collective-permute-start | bytes 688136 | tf_op jit(solution)/shard_map/ppermute | solution.py:331
  13.8 16.6 %copy-start.3 = (s32[4]{0:T(128)S(1)}, s32[4]{0:T(128)}, u32[]{:S(2)}) copy-start(s32[4]{0:T(128)} %constant.12.clone) | copy-start | bytes 52
  13.8 6.6 %collective-permute-start.26 = (s32[4,128]{1,0:T(4,128)S(1)}, s32[4,128]{1,0:T(4,128)S(1)}, u32[]{:S(2)}, u32[]{:S(2)}) collective-permute-start(s32[4,128]{1,0:T(4,128)S(1)} %slice_maximum_fusion.levels), channel_id=1, source_target_pairs={{0,16},{4,20},{8,24},{12,28},{16,0},{20,4},{24,8},{28,12},{1,17},{... | collective-permute-start | bytes 6152 | tf_op jit(solution)/shard_map/ppermute | solution.py:338
  23.1 1.6 %collective-permute-start.30 = (bf16[136,896]{1,0:T(8,128)(2,1)S(1)}, bf16[136,896]{1,0:T(8,128)(2,1)S(1)}, u32[]{:S(2)}, u32[]{:S(2)}) collective-permute-start(bf16[136,896]{1,0:T(8,128)(2,1)S(1)} %sum_near.1.own), channel_id=1, source_target_pairs={{0,1},{1,0},{2,3},{3,2},{4,5},{5,4},{6,7},{7,6},{8,9},{9,8},{10,11... | collective-permute-start | bytes 731144 | tf_op jit(solution)/shard_map/ppermute | solution.py:346
  24.5 30.9 %copy-start = (f32[1,128,896]{2,1,0:T(8,128)S(1)}, f32[1,128,896]{2,1,0:T(8,128)}, u32[]{:S(2)}) copy-start(f32[1,128,896]{2,1,0:T(8,128)} %weight.1) | copy-start | bytes 1376260
  24.7 30.7 %collective-permute-start.31 = (bf16[136,896]{1,0:T(8,128)(2,1)S(1)}, bf16[136,896]{1,0:T(8,128)(2,1)S(1)}, u32[]{:S(2)}, u32[]{:S(2)}) collective-permute-start(bf16[136,896]{1,0:T(8,128)(2,1)S(1)} %broadcast_select_fusion), channel_id=1, source_target_pairs={{0,2},{1,3},{2,0},{3,1},{4,6},{5,7},{6,4},{7,5},{8,10},{9,11},{10,... | collective-permute-start | bytes 731144 | tf_op jit(solution)/shard_map/ppermute | solution.py:348
  26.3 7.5 %collective-permute-start.32 = (bf16[128,896]{1,0:T(8,128)(2,1)S(1)}, bf16[128,896]{1,0:T(8,128)(2,1)S(1)}, u32[]{:S(2)}, u32[]{:S(2)}) collective-permute-start(bf16[128,896]{1,0:T(8,128)(2,1)S(1)} %get-tuple-element.69), channel_id=1, source_target_pairs={{0,4},{4,0},{8,12},{12,8},{16,20},{20,16},{24,28},{28,24},{1,5},{5... | collective-permute-start | bytes 688136 | tf_op jit(solution)/shard_map/ppermute | solution.py:331
  27.7 8.5 %collective-permute-start.33 = (bf16[128,896]{1,0:T(8,128)(2,1)S(1)}, bf16[128,896]{1,0:T(8,128)(2,1)S(1)}, u32[]{:S(2)}, u32[]{:S(2)}) collective-permute-start(bf16[128,896]{1,0:T(8,128)(2,1)S(1)} %get-tuple-element.70), channel_id=1, source_target_pairs={{0,8},{4,12},{8,0},{12,4},{16,24},{20,28},{24,16},{28,20},{1,9},{5... | collective-permute-start | bytes 688136 | tf_op jit(solution)/shard_map/ppermute | solution.py:331
  29.4 11.3 %collective-permute-start.34 = (bf16[128,896]{1,0:T(8,128)(2,1)S(1)}, bf16[128,896]{1,0:T(8,128)(2,1)S(1)}, u32[]{:S(2)}, u32[]{:S(2)}) collective-permute-start(bf16[128,896]{1,0:T(8,128)(2,1)S(1)} %get-tuple-element.71), channel_id=1, source_target_pairs={{0,12},{4,8},{8,4},{12,0},{16,28},{20,24},{24,20},{28,16},{1,13},{... | collective-permute-start | bytes 688136 | tf_op jit(solution)/shard_map/ppermute | solution.py:331
  41.5 13.9 %collective-permute-start.20 = (bf16[128,896]{1,0:T(8,128)(2,1)S(1)}, bf16[128,896]{1,0:T(8,128)(2,1)}, u32[]{:S(2)}, u32[]{:S(2)}) collective-permute-start(bf16[128,896]{1,0:T(8,128)(2,1)S(1)} %param.20), channel_id=1, source_target_pairs={{0,19},{1,17},{2,16},{3,18},{4,23},{5,21},{6,20},{7,22},{8,27},{9,... | collective-permute-start | bytes 688136 | tf_op jit(solution)/shard_map/cond/branch_20_fun/ppermute | solution.py:357

commit v5 on v4

--- a/solution.py
+++ b/solution.py
@@ -114,33 +114,62 @@
         copy.wait()
 
 
+def is_inner(index):
+    return ((index >> 1) ^ (index >> 2)) & 1
+
+
 def second_kernel(given_count, grads, offsets, *refs):
-    given, outs, rest = refs[:given_count], refs[given_count:-3], refs[-3:]
-    mine, posted, sems = rest
+    given, outs, (posted, sems) = refs[:given_count], refs[given_count:-2], refs[-2:]
     me = lax.axis_index("dp")
-    targets = [me ^ turn for turn in (0, *range(given_count + 1, 2 * square))]
+    inner = is_inner(me)
+    targets = [me ^ turn for turn in (0, 3, 4, 5)] + [me ^ (7 - inner), me ^ (6 + inner)]
     copies = []
     for number, target in enumerate(targets):
         source = block_at(grads, target, outs[number].shape[0])
         copies.append(pltpu.make_async_copy(source, outs[number], sems.at[number]))
         copies[-1].start()
-    for row, turn in enumerate((0, square, 2, 2 ^ square)):
-        mine[row : row + 1, :] = offsets[pl.ds(me ^ turn, 1), :]
-        posted[row : row + 1, :] = offsets[pl.ds(me ^ 1 ^ turn, 1), :]
-    shape = (mine.shape[0] - square, mine.shape[1])
-    lanes = lax.broadcasted_iota(jnp.int32, shape, 1)
-    peaks = jnp.zeros(shape, jnp.float32)
+    count = offsets.shape[0]
+    posted[0:count, :] = offsets[...]
+    lanes = lax.broadcasted_iota(jnp.int32, offsets.shape, 1)
+    peaks = jnp.zeros(offsets.shape, jnp.float32)
     for number in range(given_count):
         peaks = jnp.where(lanes == (me ^ (number + 1)), largest(given[number]), peaks)
     for number, target in enumerate(targets):
         copies[number].wait()
         peaks = jnp.where(lanes == target, largest(outs[number]), peaks)
-    counts = [jnp.zeros(shape, jnp.int32) for _ in range(4)]
+    counts = [jnp.zeros(offsets.shape, jnp.int32) for _ in range(4)]
     for power in range(low_power, high_power):
         counts[power % 4] += (peaks >= jnp.float32(2.0**power)).astype(jnp.int32)
-    levels = (counts[0] + counts[1]) + (counts[2] + counts[3])
-    mine[square:, :] = levels
-    posted[square:, :] = levels
+    posted[count:, :] = (counts[0] + counts[1]) + (counts[2] + counts[3])
+
+
+def note_kernel(posted, twin, mine, aside):
+    me = lax.axis_index("dp")
+    count = posted.shape[0] // 2
+
+    def fill(out, row, target):
+        out[row : row + 1, :] = posted[pl.ds(target, 1), :]
+        far = posted[pl.ds(target ^ 6, 1), :]
+        out[row + 1 : row + 2, :] = jnp.where(is_inner(target) == 1, twin[pl.ds(target, 1), :], far)
+
+    levels = jnp.maximum(posted[count : count + 4, :], twin[count : count + 4, :])
+    for out, turn in ((mine, 0), (aside, 1)):
+        fill(out, 0, me ^ turn)
+        fill(out, 2, me ^ turn ^ 2)
+        out[4:8, :] = levels
+
+
+def make_notes(posted, twin):
+    vmem = pl.BlockSpec(memory_space=pltpu.VMEM)
+    note = jax.ShapeDtypeStruct((8, posted.shape[1]), jnp.int32)
+    return pl.pallas_call(
+        note_kernel,
+        out_shape=[note] * 2,
+        in_specs=[vmem] * 2,
+        out_specs=[vmem] * 2,
+        compiler_params=pltpu.CompilerParams(vmem_limit_bytes=8 * 2**20),
+        name="notes",
+    )(posted, twin)
 
 
 def pack_first(grads, rows, count):
@@ -161,12 +190,12 @@
     count = 2 * square - len(given)
     vmem = pl.BlockSpec(memory_space=pltpu.VMEM)
     block = jax.ShapeDtypeStruct((rows, width), grads.dtype)
-    note = jax.ShapeDtypeStruct((8, rows), jnp.int32)
+    posted = jax.ShapeDtypeStruct((2 * offsets.shape[0], rows), jnp.int32)
     return pl.pallas_call(
         functools.partial(second_kernel, len(given)),
-        out_shape=[block] * count + [note] * 2,
+        out_shape=[block] * count + [posted],
         in_specs=[pl.BlockSpec(memory_space=pltpu.HBM)] + [vmem] * (1 + len(given)),
-        out_specs=[vmem] * (count + 2),
+        out_specs=[vmem] * (count + 1),
         scratch_shapes=[pltpu.SemaphoreType.DMA((count,))],
         compiler_params=pltpu.CompilerParams(vmem_limit_bytes=8 * 2**20),
         name="pack_second",
@@ -181,10 +210,19 @@
     return jnp.bitwise_and(jnp.right_shift(mixed, 12), 255).astype(jnp.float32) * (1.0 / 256.0)
 
 
-def noise_kernel(far, mine, beside, above, out, codes):
-    rows = [mine[far : far + 1, :], beside[far : far + 1, :]]
+def fill_codes(far, mine, aside, above, codes):
+    rows = [mine[far : far + 1, :], aside[far : far + 1, :]]
     rows += [above[far : far + 1, :], above[far + 2 : far + 3, :]]
+    if far:
+        inner = is_inner(lax.axis_index("dp")) == 1
+        here, y, z, diagonal = rows
+        rows = [jnp.where(inner, diagonal, here), jnp.where(inner, z, y)]
+        rows += [jnp.where(inner, here, z), jnp.where(inner, y, diagonal)]
     codes[...] = jnp.transpose(jnp.concatenate(rows * 2)) * 747796405 + 1013904223
+
+
+def noise_kernel(mine, aside, above, out, codes):
+    fill_codes(1, mine, aside, above, codes)
     height, width = 16, out.shape[2]
     columns = lax.broadcasted_iota(jnp.int32, (1, width), 1) * 747796405
 
@@ -197,36 +235,49 @@
     lax.fori_loop(0, out.shape[1] // height, step, 0)
 
 
-def make_noise(far, notes, rows, width):
-    vmem = pl.BlockSpec(memory_space=pltpu.VMEM)
-    return pl.pallas_call(
-        functools.partial(noise_kernel, far),
+def far_noise(notes, rows, width):
+    vmem = pl.BlockSpec(memory_space=pltpu.VMEM)
+    return pl.pallas_call(
+        noise_kernel,
         out_shape=jax.ShapeDtypeStruct((square, rows, width), jnp.bfloat16),
         in_specs=[vmem] * len(notes),
         out_specs=vmem,
         scratch_shapes=[pltpu.VMEM((rows, 2 * square), jnp.int32)],
         compiler_params=pltpu.CompilerParams(vmem_limit_bytes=8 * 2**20),
-        name="noise_far" if far else "noise_near",
+        name="noise",
     )(*notes)
 
 
-def sum_kernel(far, levels, twin, noise, *refs):
-    raws, out = refs[:square], refs[square]
-    target = lax.axis_index("dp") ^ (far * square)
-    counts = jnp.maximum(levels[0:1, :], twin[0:1, :])
+def sum_kernel(far, rows, mine, upward, aside, above, *refs):
+    me = lax.axis_index("dp")
+    inner = is_inner(me) == 1
+    if far:
+        noise, stays, *raws, out = refs
+        target = jnp.where(inner, me, me ^ 6)
+    else:
+        *raws, out, codes = refs
+        target = me
+        fill_codes(0, mine, aside, above, codes)
+    counts = jnp.maximum(upward[square : square + 1, :], above[square : square + 1, :])
     lanes = lax.broadcasted_iota(jnp.int32, counts.shape, 1)
     reached = jnp.where(lanes == target, counts, 0).astype(jnp.float32)
     exponent = jnp.max(reached, axis=1, keepdims=True).astype(jnp.int32) + (low_power - level_bits)
     inverse_step = power_of_two(-exponent)
-    height = 16
-    rows, width = raws[0].shape
+    height, width = 16, raws[0].shape[1]
+    columns = lax.broadcasted_iota(jnp.int32, (1, width), 1) * 747796405
 
     def step(index, carry):
         span = pl.ds(pl.multiple_of(index * height, height), height)
         total = jnp.zeros((height, width), jnp.float32)
         for near in range(square):
-            drawn = noise[near, span, :].astype(jnp.float32)
-            scaled = raws[near][span, :].astype(jnp.float32) * inverse_step
+            if far:
+                drawn = noise[near, span, :].astype(jnp.float32)
+            else:
+                drawn = noise_of(codes[span, near : near + 1], columns)
+            values = raws[near][span, :].astype(jnp.float32)
+            if far and near == 0:
+                values = jnp.where(inner, values, stays[span, :].astype(jnp.float32))
+            scaled = values * inverse_step
             floor_part = jnp.floor(scaled)
             total = total + (floor_part + jnp.floor(scaled - floor_part + drawn))
         out[span, :] = total.astype(jnp.bfloat16)
@@ -238,17 +289,18 @@
         out[rows:, :] = jnp.broadcast_to(power_of_two(exponent), tail).astype(jnp.bfloat16)
 
 
-def sum_counts(far, levels, twin, noise, raws, extra):
-    rows, width = raws[0].shape
-    vmem = pl.BlockSpec(memory_space=pltpu.VMEM)
-    return pl.pallas_call(
-        functools.partial(sum_kernel, far),
+def sum_counts(far, notes, raws, extra):
+    rows, width = raws[-1].shape
+    vmem = pl.BlockSpec(memory_space=pltpu.VMEM)
+    return pl.pallas_call(
+        functools.partial(sum_kernel, far, rows),
         out_shape=jax.ShapeDtypeStruct((rows + extra, width), jnp.bfloat16),
-        in_specs=[vmem] * (3 + square),
+        in_specs=[vmem] * (len(notes) + len(raws)),
         out_specs=vmem,
+        scratch_shapes=[] if far else [pltpu.VMEM((rows, 2 * square), jnp.int32)],
         compiler_params=pltpu.CompilerParams(vmem_limit_bytes=8 * 2**20),
         name="sum_far" if far else "sum_near",
-    )(levels, twin, noise, *raws)
+    )(*notes, *raws)
 
 
 def update_kernel(dp_count, slots, own, beside, across, arrived, weight, *refs):
@@ -290,7 +342,7 @@
 
 def update(slots, own, beside, across, arrived, weight, dp_count):
     rows, width = arrived.shape
-    parts = 8
+    parts = 4
     vmem = pl.BlockSpec(memory_space=pltpu.VMEM)
     hbm = pl.BlockSpec(memory_space=pltpu.HBM)
     block = jax.ShapeDtypeStruct((1, rows, width), jnp.float32)
@@ -324,33 +376,41 @@
     lower = (slot_expert[:, None] > slot_expert[None, :]) & after
     branch = jnp.sum(jnp.where(lower, weights, 0))
     near_blocks = pack_first(expert_grads, block_rows, 2)
-    here, diagonal, *far_blocks, mine, posted = pack_second(expert_grads, offsets, near_blocks)
-    raw = [[here, near_blocks[0], near_blocks[1], diagonal], far_blocks]
-    for far in range(2):
-        for near in range(1, square):
-            raw[far][near] = lax.ppermute(raw[far][near], "dp", flips(dp_count, near))
-
-    aside = lax.ppermute(posted, "dp", flips(dp_count, 1))
+    packed = pack_second(expert_grads, offsets, near_blocks)
+    here, diagonal, four, five, fa, last, posted = packed
+    raw = [here, near_blocks[0], near_blocks[1], diagonal]
+    for near in range(1, square):
+        raw[near] = lax.ppermute(raw[near], "dp", flips(dp_count, near))
+
+    def mixed(inner_turn, outer_turn):
+        turns = [inner_turn if is_inner(index) else outer_turn for index in range(dp_count)]
+        return [(index, index ^ turn) for index, turn in enumerate(turns) if turn]
+
+    fa = lax.ppermute(fa, "dp", mixed(6, 1))
+    four = lax.ppermute(four, "dp", mixed(2, 4))
+    five = lax.ppermute(five, "dp", mixed(3, 5))
+    crossed = lax.ppermute(last, "dp", mixed(7, 0))
+
+    twin = lax.ppermute(posted, "dp", flips(dp_count, square))
+    mine, sideways = make_notes(posted, twin)
+    aside = lax.ppermute(sideways, "dp", flips(dp_count, 1))
     levels = jnp.maximum(mine[square:], aside[square:])
     upward = jnp.concatenate([mine[2:square], aside[2:square], levels])
     above = lax.ppermute(upward, "dp", flips(dp_count, 2))
-    levels = jnp.maximum(levels, above[square:])
-    twin = lax.ppermute(levels, "dp", flips(dp_count, square))
-    noise = []
-    for far in range(2):
-        noise.append(make_noise(far, (mine, aside, above), block_rows, hidden))
+    noise = far_noise((mine, aside, above), block_rows, hidden)
 
     wanted = slot_expert == (place ^ 2)
     crossing = jnp.sum(jnp.where(wanted, jnp.arange(expert_count), 0)) == place
-    own = sum_counts(0, levels, twin, noise[0], raw[0], 8)
+    own = sum_counts(0, (mine, upward, aside, above), raw, 8)
     beside = lax.ppermute(own, "expert", flips(expert_count, 1))
     across_wants = jnp.where(crossing, own, beside)
     across = lax.ppermute(across_wants, "expert", flips(expert_count, 2))
-    message = sum_counts(1, levels, twin, noise[1], raw[1], 0)
+    raws = (noise, last, crossed, fa, four, five)
+    message = sum_counts(1, (mine, upward, aside, above), raws, 0)
 
     def route(order):
         pairs = [
-            (block * expert_count + slot, (block ^ square) * expert_count + order[slot])
+            (block * expert_count + slot, (block if is_inner(block) else block ^ 6) * expert_count + order[slot])
             for block in range(dp_count)
             for slot in range(expert_count)
         ]

time: 57.7 us -> 65 us (1.13)
  the two profiles are of different devices: /device:TPU:0 before, /device:TPU:16 now
where the time goes in v5:
time: 65 us; the launch traced here: 64.7 us
  waiting for transfers between devices  35.5 us (55%)
  starting transfers between devices  17.1 us (26%)
  Pallas kernels  8.6 us (13%)
  between operations  2.09 us (3%)
  other arithmetic  1.38 us (2%)
    ppermute x1, waiting for transfers between devices, staged_body(): crossed = lax.ppermute(last, 'dp', mixed(7, 0))  8.95 us
    ppermute x1, waiting for transfers between devices, staged_body(): fa = lax.ppermute(fa, 'dp', mixed(6, 1))  8.87 us
    ppermute x1, waiting for transfers between devices, route(): return lambda parts: lax.ppermute(parts, ('dp', 'expert'), pairs)  6.09 us
    ppermute x1, waiting for transfers between devices, staged_body(): above = lax.ppermute(upward, 'dp', flips(dp_count, 2))  5.97 us
    ppermute x1, waiting for transfers between devices, staged_body(): twin = lax.ppermute(posted, 'dp', flips(dp_count, square))  4.54 us
    ppermute x3, starting transfers between devices, staged_body(): raw[near] = lax.ppermute(raw[near], 'dp', flips(dp_count, near))  3.49 us
    ppermute x1, starting transfers between devices, staged_body(): crossed = lax.ppermute(last, 'dp', mixed(7, 0))  3.18 us
    pallas_call x2, Pallas kernels, sum_counts(): pl.pallas_call(functools.partial(sum_kernel, far, rows), out_shape=jax.Sh...  2.41 us
  transfers between devices with their start and end apart: 13, of which 7 were waited for; matrix products, arithmetic and copies ran while one was open for 2% of the time, Pallas kernels for 3%

profile of v5, /device:TPU:16, one launch (start us, length us, event | category | flops | bytes accessed | tf_op | source)
XLA Modules:
  0.0 64.7 jit_solution(8959598766828714732)
XLA Ops:
  0.6 1.1 %pack_first.1 = (bf16[128,896]{1,0:T(8,128)(2,1)S(1)}, bf16[128,896]{1,0:T(8,128)(2,1)S(1)}) custom-call(bf16[1,1,1024,896]{3,2,1,0:T(8,128)(2,1)} %grads.3), custom_call_target="tpu_custom_call" | custom-call | tf_op jit(solution)/shard_map/pack_first/pallas_call | solution.py:177
  1.8 1.7 %pack_second.1 = (bf16[128,896]{1,0:T(8,128)(2,1)S(1)}, bf16[128,896]{1,0:T(8,128)(2,1)S(1)}, bf16[128,896]{1,0:T(8,128)(2,1)S(1)}, bf16[128,896]{1,0:T(8,128)(2...) custom-call(bf16[1,1,1024,896]{3,2,1,0:T(8,128)(2,1)} %grads.3, ...), custom_call_target="tpu_custom_call" | custom-call | tf_op jit(solution)/shard_map/pack_second/pallas_call | solution.py:194
  3.6 4.5 %collective-permute-done.24.twin = s32[16,128]{1,0:T(8,128)S(1)} collective-permute-done((s32[16,128]{1,0:T(8,128)S(1)}, s32[16,128]{1,0:T(8,128)S(1)}, u32[]{:S(2)}, u32[]{:S(2)}) %collective-permute-start.24) | collective-permute-done | bytes 8224 | tf_op jit(solution)/shard_map/ppermute | solution.py:394
  8.1 1.6 %collective-permute-start.25 = (s32[8,128]{1,0:T(8,128)S(1)}, s32[8,128]{1,0:T(8,128)S(1)}, u32[]{:S(2)}, u32[]{:S(2)}) collective-permute-start(s32[8,128]{1,0:T(8,128)S(1)} %get-tuple-element.67), channel_id=1, source_target_pairs={{0,4},{4,0},{8,12},{12,8},{16,20},{20,16},{24,28},{28,24},{1,5},{5... | collective-permute-start | bytes 12296 | tf_op jit(solution)/shard_map/ppermute | solution.py:396
  10.2 1.6 %collective-permute-start.28 = (bf16[128,896]{1,0:T(8,128)(2,1)S(1)}, bf16[128,896]{1,0:T(8,128)(2,1)S(1)}, u32[]{:S(2)}, u32[]{:S(2)}) collective-permute-start(bf16[128,896]{1,0:T(8,128)(2,1)S(1)} %get-tuple-element.64.refs_1_), channel_id=1, source_target_pairs={{0,8},{4,12},{8,0},{12,4},{16,24},{20,28},{24,16},{28,20},{1,9},{5... | collective-permute-start | bytes 688136 | tf_op jit(solution)/shard_map/ppermute | solution.py:383
  11.8 1.4 %collective-permute-start.29 = (bf16[128,896]{1,0:T(8,128)(2,1)S(1)}, bf16[128,896]{1,0:T(8,128)(2,1)S(1)}, u32[]{:S(2)}, u32[]{:S(2)}) collective-permute-start(bf16[128,896]{1,0:T(8,128)(2,1)S(1)} %get-tuple-element.69), channel_id=1, source_target_pairs={{0,12},{4,8},{8,4},{12,0},{16,28},{20,24},{24,20},{28,16},{1,13},{... | collective-permute-start | bytes 688136 | tf_op jit(solution)/shard_map/ppermute | solution.py:383
  13.2 1.6 %collective-permute-start.26 = (s32[8,128]{1,0:T(8,128)S(1)}, s32[8,128]{1,0:T(8,128)S(1)}, u32[]{:S(2)}, u32[]{:S(2)}) collective-permute-start(s32[8,128]{1,0:T(8,128)S(1)} %pad_add_fusion.upward), channel_id=1, source_target_pairs={{0,8},{4,12},{8,0},{12,4},{16,24},{20,28},{24,16},{28,20},{1,9},{5... | collective-permute-start | bytes 12296 | tf_op jit(solution)/shard_map/ppermute | solution.py:399
  14.9 6.0 %collective-permute-done.26.above = s32[8,128]{1,0:T(8,128)S(1)} collective-permute-done((s32[8,128]{1,0:T(8,128)S(1)}, s32[8,128]{1,0:T(8,128)S(1)}, u32[]{:S(2)}, u32[]{:S(2)}) %collective-permute-start.26) | collective-permute-done | bytes 4128 | tf_op jit(solution)/shard_map/ppermute | solution.py:399
  20.9 0.9 %collective-permute-done.29.refs_3_ = bf16[128,896]{1,0:T(8,128)(2,1)S(1)} collective-permute-done((bf16[128,896]{1,0:T(8,128)(2,1)S(1)}, bf16[128,896]{1,0:T(8,128)(2,1)S(1)}, u32[]{:S(2)}, u32[]{:S(2)}) %collective-permute-start.29) | collective-permute-done | bytes 229408 | tf_op jit(solution)/shard_map/ppermute | solution.py:383
  21.8 1.7 %sum_near.1.own = bf16[136,896]{1,0:T(8,128)(2,1)S(1)} custom-call(s32[8,128]{1,0:T(8,128)S(1)} %get-tuple-element.66.mine, s32[8,128]{1,0:T(8,128)S(1)} %pad_add_fusion.upward, s32[8,128]{1,0:T(8,128)S(1)} %collective-permute-done.25.aside, s32[8,128]{1,0:T(8,128)S(1)} %collective-permute-done.26.above, bf16[128,896]{1,0:T(8,128)(2,1)S(1)} %get-tuple-element.68.refs_0_, ...), custom_call_target="tpu_custom_call" | custom-call | tf_op jit(solution)/shard_map/sum_near/pallas_call | solution.py:295
  23.6 0.6 fusion.1
  25.1 1.6 %collective-permute-start.31 = (bf16[136,896]{1,0:T(8,128)(2,1)S(1)}, bf16[136,896]{1,0:T(8,128)(2,1)S(1)}, u32[]{:S(2)}, u32[]{:S(2)}) collective-permute-start(bf16[136,896]{1,0:T(8,128)(2,1)S(1)} %broadcast_select_fusion), channel_id=1, source_target_pairs={{0,2},{1,3},{2,0},{3,1},{4,6},{5,7},{6,4},{7,5},{8,10},{9,11},{10,... | collective-permute-start | bytes 731144 | tf_op jit(solution)/shard_map/ppermute | solution.py:407
  27.1 1.8 %collective-permute-start.34 = (bf16[128,896]{1,0:T(8,128)(2,1)S(1)}, bf16[128,896]{1,0:T(8,128)(2,1)S(1)}, u32[]{:S(2)}, u32[]{:S(2)}) collective-permute-start(bf16[128,896]{1,0:T(8,128)(2,1)S(1)} %get-tuple-element.72), channel_id=1, source_target_pairs={{0,16},{4,20},{8,0},{12,4},{16,24},{20,28},{24,8},{28,12},{1,17},{... | collective-permute-start | bytes 688136 | tf_op jit(solution)/shard_map/ppermute | solution.py:390
  28.8 1.3 %collective-permute-start.35 = (bf16[128,896]{1,0:T(8,128)(2,1)S(1)}, bf16[128,896]{1,0:T(8,128)(2,1)S(1)}, u32[]{:S(2)}, u32[]{:S(2)}) collective-permute-start(bf16[128,896]{1,0:T(8,128)(2,1)S(1)} %get-tuple-element.73), channel_id=1, source_target_pairs={{0,20},{4,16},{8,4},{12,0},{16,28},{20,24},{24,12},{28,8},{1,21},{... | collective-permute-start | bytes 688136 | tf_op jit(solution)/shard_map/ppermute | solution.py:391
  30.2 3.2 %collective-permute-start.32 = (bf16[128,896]{1,0:T(8,128)(2,1)S(1)}, bf16[128,896]{1,0:T(8,128)(2,1)S(1)}, u32[]{:S(2)}, u32[]{:S(2)}) collective-permute-start(bf16[128,896]{1,0:T(8,128)(2,1)S(1)} %get-tuple-element.70.refs_1_), channel_id=1, source_target_pairs={{8,20},{12,16},{16,12},{20,8},{9,21},{13,17},{17,13},{21,9},{10,22... | collective-permute-start | bytes 688136 | tf_op jit(solution)/shard_map/ppermute | solution.py:392
  33.4 0.7 %select_reduce_fusion = s32[]{:T(128)} fusion(s32[4]{0:T(128)S(1)} %copy-done.3, s32[4]{0:T(128)S(1)} %copy-done.1), kind=kLoop, calls=%fused_computation.2 | loop fusion | flops 79 | bytes 36 | tf_op jit(solution)/shard_map/reduce_sum | solution.py:377
  34.7 1.3 %noise.1.refs_0_ = bf16[4,128,896]{2,1,0:T(8,128)(2,1)S(1)} custom-call(s32[8,128]{1,0:T(8,128)S(1)} %get-tuple-element.66.mine, s32[8,128]{1,0:T(8,128)S(1)} %collective-permute-done.25.aside, s32[8,128]{1,0:T(8,128)S(1)} %collective-permute-done.26.above), custom_call_target="tpu_custom_call" | custom-call | tf_op jit(solution)/shard_map/noise/pallas_call | solution.py:240
  36.1 8.9 %collective-permute-done.33.refs_3_ = bf16[128,896]{1,0:T(8,128)(2,1)S(1)} collective-permute-done((bf16[128,896]{1,0:T(8,128)(2,1)S(1)}, bf16[128,896]{1,0:T(8,128)(2,1)S(1)}, u32[]{:S(2)}, u32[]{:S(2)}) %collective-permute-start.33) | collective-permute-done | bytes 229408 | tf_op jit(solution)/shard_map/ppermute | solution.py:389
  44.9 9.0 %collective-permute-done.32.refs_2_ = bf16[128,896]{1,0:T(8,128)(2,1)S(1)} collective-permute-done((bf16[128,896]{1,0:T(8,128)(2,1)S(1)}, bf16[128,896]{1,0:T(8,128)(2,1)S(1)}, u32[]{:S(2)}, u32[]{:S(2)}) %collective-permute-start.32) | collective-permute-done | bytes 229408 | tf_op jit(solution)/shard_map/ppermute | solution.py:392
  53.9 0.7 %sum_far.1 = bf16[128,896]{1,0:T(8,128)(2,1)S(1)} custom-call(s32[8,128]{1,0:T(8,128)S(1)} %get-tuple-element.66.mine, s32[8,128]{1,0:T(8,128)S(1)} %pad_add_fusion.upward, s32[8,128]{1,0:T(8,128)S(1)} %collective-permute-done.25.aside, s32[8,128]{1,0:T(8,128)S(1)} %collective-permute-done.26.above, bf16[4,128,896]{2,1,0:T(8,128)(2,1)S(1)} %noise.1.refs_0_, ...), custom_call_target="tpu_custom_call" | custom-call | tf_op jit(solution)/shard_map/sum_far/pallas_call | solution.py:295
  54.6 8.1 %conditional.1 = (bf16[128,896]{1,0:T(8,128)(2,1)}) conditional(s32[]{:T(128)} %clamp.3, bf16[128,896]{1,0:T(8,128)(2,1)S(1)} %sum_far.1, bf16[128,896]{1,0:T(8,128)(2,1)S(1)} %sum_far.1, bf16[128,896]{1,0:T(8,128)(2,1)S(1)} %sum_far.1, bf16[128,896]{1,0:T(8,128)(2,1)S(1)} %sum_far.1, ...), branch_computations={%region_2.3_spmd, %region_3.4_spmd, %region_4.5_spmd, %region_5.6_... | conditional | bytes 917552 | solution.py:420
  54.7 1.9 %collective-permute-start.20 = (bf16[128,896]{1,0:T(8,128)(2,1)S(1)}, bf16[128,896]{1,0:T(8,128)(2,1)}, u32[]{:S(2)}, u32[]{:S(2)}) collective-permute-start(bf16[128,896]{1,0:T(8,128)(2,1)S(1)} %param.20), channel_id=1, source_target_pairs={{0,27},{1,25},{2,24},{3,26},{4,31},{5,29},{6,28},{7,30},{8,11},{9,... | collective-permute-start | bytes 688136 | tf_op jit(solution)/shard_map/cond/branch_20_fun/ppermute | solution.py:417
  56.6 6.1 %collective-permute-done.20 = bf16[128,896]{1,0:T(8,128)(2,1)} collective-permute-done((bf16[128,896]{1,0:T(8,128)(2,1)S(1)}, bf16[128,896]{1,0:T(8,128)(2,1)}, u32[]{:S(2)}, u32[]{:S(2)}) %collective-permute-start.20) | collective-permute-done | bytes 229408 | tf_op jit(solution)/shard_map/cond/branch_20_fun/ppermute | solution.py:417
  62.7 2.1 %update.1 = (f32[1,128,896]{2,1,0:T(8,128)}, f32[1,128,896]{2,1,0:T(8,128)}, f32[1,1]{1,0:T(1,128)}) custom-call(s32[1,4]{1,0:T(1,128)S(1)} %bitcast.2, bf16[136,896]{1,0:T(8,128)(2,1)S(1)} %sum_near.1.own, bf16[136,896]{1,0:T(8,128)(2,1)S(1)} %collective-permute-done.30.beside, bf16[136,896]{1,0:T(8,128)(2,1)S(1)} %collective-permute-done.31.across, ...), custom_call_target="tpu_custom_call" | custom-call | tf_op jit(solution)/shard_map/update/pallas_call | solution.py:349
  (25 shorter events, 1.4 us)
Async XLA Ops:
  0.6 1.1 %copy-start.2 = (s32[1,1,1024]{2,1,0:T(1,128)S(1)}, s32[1,1,1024]{2,1,0:T(1,128)}, u32[]{:S(2)}) copy-start(s32[1,1,1024]{2,1,0:T(1,128)} %param.30) | copy-start | bytes 12292
  1.7 21.8 %copy-start.1 = (s32[4]{0:T(128)S(1)}, s32[4]{0:T(128)}, u32[]{:S(2)}) copy-start(s32[4]{0:T(128)} %param.31) | copy-start | bytes 52
  1.7 31.6 %copy-start.3 = (s32[4]{0:T(128)S(1)}, s32[4]{0:T(128)}, u32[]{:S(2)}) copy-start(s32[4]{0:T(128)} %constant.12.clone) | copy-start | bytes 52
  3.5 4.6 %collective-permute-start.24 = (s32[16,128]{1,0:T(8,128)S(1)}, s32[16,128]{1,0:T(8,128)S(1)}, u32[]{:S(2)}, u32[]{:S(2)}) collective-permute-start(s32[16,128]{1,0:T(8,128)S(1)} %get-tuple-element.65.posted), channel_id=1, source_target_pairs={{0,16},{4,20},{8,24},{12,28},{16,0},{20,4},{24,8},{28,12},{1,17},{... | collective-permute-start | bytes 24584 | tf_op jit(solution)/shard_map/ppermute | solution.py:394
  8.1 5.1 %collective-permute-start.25 = (s32[8,128]{1,0:T(8,128)S(1)}, s32[8,128]{1,0:T(8,128)S(1)}, u32[]{:S(2)}, u32[]{:S(2)}) collective-permute-start(s32[8,128]{1,0:T(8,128)S(1)} %get-tuple-element.67), channel_id=1, source_target_pairs={{0,4},{4,0},{8,12},{12,8},{16,20},{20,16},{24,28},{28,24},{1,5},{5... | collective-permute-start | bytes 12296 | tf_op jit(solution)/shard_map/ppermute | solution.py:396
  9.7 11.1 %collective-permute-start.27 = (bf16[128,896]{1,0:T(8,128)(2,1)S(1)}, bf16[128,896]{1,0:T(8,128)(2,1)S(1)}, u32[]{:S(2)}, u32[]{:S(2)}) collective-permute-start(bf16[128,896]{1,0:T(8,128)(2,1)S(1)} %get-tuple-element.63.refs_0_), channel_id=1, source_target_pairs={{0,4},{4,0},{8,12},{12,8},{16,20},{20,16},{24,28},{28,24},{1,5},{5... | collective-permute-start | bytes 688136 | tf_op jit(solution)/shard_map/ppermute | solution.py:383
  10.2 10.6 %collective-permute-start.28 = (bf16[128,896]{1,0:T(8,128)(2,1)S(1)}, bf16[128,896]{1,0:T(8,128)(2,1)S(1)}, u32[]{:S(2)}, u32[]{:S(2)}) collective-permute-start(bf16[128,896]{1,0:T(8,128)(2,1)S(1)} %get-tuple-element.64.refs_1_), channel_id=1, source_target_pairs={{0,8},{4,12},{8,0},{12,4},{16,24},{20,28},{24,16},{28,20},{1,9},{5... | collective-permute-start | bytes 688136 | tf_op jit(solution)/shard_map/ppermute | solution.py:383
  11.8 10.0 %collective-permute-start.29 = (bf16[128,896]{1,0:T(8,128)(2,1)S(1)}, bf16[128,896]{1,0:T(8,128)(2,1)S(1)}, u32[]{:S(2)}, u32[]{:S(2)}) collective-permute-start(bf16[128,896]{1,0:T(8,128)(2,1)S(1)} %get-tuple-element.69), channel_id=1, source_target_pairs={{0,12},{4,8},{8,4},{12,0},{16,28},{20,24},{24,20},{28,16},{1,13},{... | collective-permute-start | bytes 688136 | tf_op jit(solution)/shard_map/ppermute | solution.py:383
  13.2 7.6 %collective-permute-start.26 = (s32[8,128]{1,0:T(8,128)S(1)}, s32[8,128]{1,0:T(8,128)S(1)}, u32[]{:S(2)}, u32[]{:S(2)}) collective-permute-start(s32[8,128]{1,0:T(8,128)S(1)} %pad_add_fusion.upward), channel_id=1, source_target_pairs={{0,8},{4,12},{8,0},{12,4},{16,24},{20,28},{24,16},{28,20},{1,9},{5... | collective-permute-start | bytes 12296 | tf_op jit(solution)/shard_map/ppermute | solution.py:399
  23.5 1.6 %collective-permute-start.30 = (bf16[136,896]{1,0:T(8,128)(2,1)S(1)}, bf16[136,896]{1,0:T(8,128)(2,1)S(1)}, u32[]{:S(2)}, u32[]{:S(2)}) collective-permute-start(bf16[136,896]{1,0:T(8,128)(2,1)S(1)} %sum_near.1.own), channel_id=1, source_target_pairs={{0,1},{1,0},{2,3},{3,2},{4,5},{5,4},{6,7},{7,6},{8,9},{9,8},{10,11... | collective-permute-start | bytes 731144 | tf_op jit(solution)/shard_map/ppermute | solution.py:405
  24.8 37.8 %copy-start = (f32[1,128,896]{2,1,0:T(8,128)S(1)}, f32[1,128,896]{2,1,0:T(8,128)}, u32[]{:S(2)}) copy-start(f32[1,128,896]{2,1,0:T(8,128)} %weight.1) | copy-start | bytes 1376260
  25.1 37.6 %collective-permute-start.31 = (bf16[136,896]{1,0:T(8,128)(2,1)S(1)}, bf16[136,896]{1,0:T(8,128)(2,1)S(1)}, u32[]{:S(2)}, u32[]{:S(2)}) collective-permute-start(bf16[136,896]{1,0:T(8,128)(2,1)S(1)} %broadcast_select_fusion), channel_id=1, source_target_pairs={{0,2},{1,3},{2,0},{3,1},{4,6},{5,7},{6,4},{7,5},{8,10},{9,11},{10,... | collective-permute-start | bytes 731144 | tf_op jit(solution)/shard_map/ppermute | solution.py:407
  26.6 18.3 %collective-permute-start.33 = (bf16[128,896]{1,0:T(8,128)(2,1)S(1)}, bf16[128,896]{1,0:T(8,128)(2,1)S(1)}, u32[]{:S(2)}, u32[]{:S(2)}) collective-permute-start(bf16[128,896]{1,0:T(8,128)(2,1)S(1)} %get-tuple-element.71), channel_id=1, source_target_pairs={{0,4},{4,0},{8,16},{12,20},{16,8},{20,12},{24,28},{28,24},{1,5},{5... | collective-permute-start | bytes 688136 | tf_op jit(solution)/shard_map/ppermute | solution.py:389
  27.1 17.9 %collective-permute-start.34 = (bf16[128,896]{1,0:T(8,128)(2,1)S(1)}, bf16[128,896]{1,0:T(8,128)(2,1)S(1)}, u32[]{:S(2)}, u32[]{:S(2)}) collective-permute-start(bf16[128,896]{1,0:T(8,128)(2,1)S(1)} %get-tuple-element.72), channel_id=1, source_target_pairs={{0,16},{4,20},{8,0},{12,4},{16,24},{20,28},{24,8},{28,12},{1,17},{... | collective-permute-start | bytes 688136 | tf_op jit(solution)/shard_map/ppermute | solution.py:390
  28.8 16.1 %collective-permute-start.35 = (bf16[128,896]{1,0:T(8,128)(2,1)S(1)}, bf16[128,896]{1,0:T(8,128)(2,1)S(1)}, u32[]{:S(2)}, u32[]{:S(2)}) collective-permute-start(bf16[128,896]{1,0:T(8,128)(2,1)S(1)} %get-tuple-element.73), channel_id=1, source_target_pairs={{0,20},{4,16},{8,4},{12,0},{16,28},{20,24},{24,12},{28,8},{1,21},{... | collective-permute-start | bytes 688136 | tf_op jit(solution)/shard_map/ppermute | solution.py:391
  30.2 23.7 %collective-permute-start.32 = (bf16[128,896]{1,0:T(8,128)(2,1)S(1)}, bf16[128,896]{1,0:T(8,128)(2,1)S(1)}, u32[]{:S(2)}, u32[]{:S(2)}) collective-permute-start(bf16[128,896]{1,0:T(8,128)(2,1)S(1)} %get-tuple-element.70.refs_1_), channel_id=1, source_target_pairs={{8,20},{12,16},{16,12},{20,8},{9,21},{13,17},{17,13},{21,9},{10,22... | collective-permute-start | bytes 688136 | tf_op jit(solution)/shard_map/ppermute | solution.py:392
  54.7 8.0 %collective-permute-start.20 = (bf16[128,896]{1,0:T(8,128)(2,1)S(1)}, bf16[128,896]{1,0:T(8,128)(2,1)}, u32[]{:S(2)}, u32[]{:S(2)}) collective-permute-start(bf16[128,896]{1,0:T(8,128)(2,1)S(1)} %param.20), channel_id=1, source_target_pairs={{0,27},{1,25},{2,24},{3,26},{4,31},{5,29},{6,28},{7,30},{8,11},{9,... | collective-permute-start | bytes 688136 | tf_op jit(solution)/shard_map/cond/branch_20_fun/ppermute | solution.py:417

commit v6 on v5

--- a/solution.py
+++ b/solution.py
@@ -102,27 +102,29 @@
     return jnp.max(best, axis=1, keepdims=True)
 
 
+def is_inner(index):
+    return ((index >> 1) ^ (index >> 2)) & 1
+
+
 def first_kernel(grads, *refs):
     outs, sems = refs[:-1], refs[-1]
     me = lax.axis_index("dp")
     copies = []
+    targets = [me ^ 1, me ^ 2, me ^ (7 - is_inner(me))]
     for number, out in enumerate(outs):
-        source = block_at(grads, me ^ (number + 1), out.shape[0])
+        source = block_at(grads, targets[number], out.shape[0])
         copies.append(pltpu.make_async_copy(source, out, sems.at[number]))
         copies[-1].start()
     for copy in copies:
         copy.wait()
 
 
-def is_inner(index):
-    return ((index >> 1) ^ (index >> 2)) & 1
-
-
 def second_kernel(given_count, grads, offsets, *refs):
     given, outs, (posted, sems) = refs[:given_count], refs[given_count:-2], refs[-2:]
     me = lax.axis_index("dp")
     inner = is_inner(me)
-    targets = [me ^ turn for turn in (0, 3, 4, 5)] + [me ^ (7 - inner), me ^ (6 + inner)]
+    targets = [me ^ turn for turn in (0, 3, 4, 5)] + [me ^ (6 + inner)]
+    sources = [me ^ 1, me ^ 2, me ^ (7 - inner)]
     copies = []
     for number, target in enumerate(targets):
         source = block_at(grads, target, outs[number].shape[0])
@@ -133,7 +135,7 @@
     lanes = lax.broadcasted_iota(jnp.int32, offsets.shape, 1)
     peaks = jnp.zeros(offsets.shape, jnp.float32)
     for number in range(given_count):
-        peaks = jnp.where(lanes == (me ^ (number + 1)), largest(given[number]), peaks)
+        peaks = jnp.where(lanes == sources[number], largest(given[number]), peaks)
     for number, target in enumerate(targets):
         copies[number].wait()
         peaks = jnp.where(lanes == target, largest(outs[number]), peaks)
@@ -153,9 +155,9 @@
         out[row + 1 : row + 2, :] = jnp.where(is_inner(target) == 1, twin[pl.ds(target, 1), :], far)
 
     levels = jnp.maximum(posted[count : count + 4, :], twin[count : count + 4, :])
-    for out, turn in ((mine, 0), (aside, 1)):
+    for out, turn in ((mine, 0), (aside, 2)):
         fill(out, 0, me ^ turn)
-        fill(out, 2, me ^ turn ^ 2)
+        fill(out, 2, me ^ turn ^ 1)
         out[4:8, :] = levels
 
 
@@ -211,8 +213,8 @@
 
 
 def fill_codes(far, mine, aside, above, codes):
-    rows = [mine[far : far + 1, :], aside[far : far + 1, :]]
-    rows += [above[far : far + 1, :], above[far + 2 : far + 3, :]]
+    rows = [mine[far : far + 1, :], above[far : far + 1, :]]
+    rows += [aside[far : far + 1, :], above[far + 2 : far + 3, :]]
     if far:
         inner = is_inner(lax.axis_index("dp")) == 1
         here, y, z, diagonal = rows
@@ -375,10 +377,10 @@
     weights = jnp.array([6, 2, 1, 0], jnp.int32)[:, None]
     lower = (slot_expert[:, None] > slot_expert[None, :]) & after
     branch = jnp.sum(jnp.where(lower, weights, 0))
-    near_blocks = pack_first(expert_grads, block_rows, 2)
-    packed = pack_second(expert_grads, offsets, near_blocks)
-    here, diagonal, four, five, fa, last, posted = packed
-    raw = [here, near_blocks[0], near_blocks[1], diagonal]
+    first_blocks = pack_first(expert_grads, block_rows, 3)
+    packed = pack_second(expert_grads, offsets, first_blocks)
+    here, diagonal, four, five, last, posted = packed
+    raw, fa = [here, first_blocks[0], first_blocks[1], diagonal], first_blocks[2]
     for near in range(1, square):
         raw[near] = lax.ppermute(raw[near], "dp", flips(dp_count, near))
 
@@ -393,10 +395,10 @@
 
     twin = lax.ppermute(posted, "dp", flips(dp_count, square))
     mine, sideways = make_notes(posted, twin)
-    aside = lax.ppermute(sideways, "dp", flips(dp_count, 1))
+    aside = lax.ppermute(sideways, "dp", flips(dp_count, 2))
     levels = jnp.maximum(mine[square:], aside[square:])
     upward = jnp.concatenate([mine[2:square], aside[2:square], levels])
-    above = lax.ppermute(upward, "dp", flips(dp_count, 2))
+    above = lax.ppermute(upward, "dp", flips(dp_count, 1))
     noise = far_noise((mine, aside, above), block_rows, hidden)
 
     wanted = slot_expert == (place ^ 2)

time: 65 us -> 65.9 us (1.014)
  waiting for transfers between devices: 35.5 us -> 36.9 us
    ppermute x3, waiting for transfers between devices: 0.91 us -> 4.18 us  [staged_body(): raw[near] = lax.ppermute(raw[near], 'dp', flips(dp_count, near))]
    ppermute x2, waiting for transfers between devices: 5.97 us -> 2.75 us  [the longest x1 2.75 us: staged_body(): above = lax.ppermute(upward, 'dp', flips(dp_count, 1))]
    ppermute x1, starting transfers between devices: 3.18 us -> 1.91 us  [staged_body(): crossed = lax.ppermute(last, 'dp', mixed(7, 0))]
    ppermute x1, starting transfers between devices: 1.35 us -> 2.43 us  [staged_body(): five = lax.ppermute(five, 'dp', mixed(3, 5))]
    ppermute x1, waiting for transfers between devices: 8.95 us -> 9.81 us  [staged_body(): crossed = lax.ppermute(last, 'dp', mixed(7, 0))]
  transfers between devices with their start and end apart: 13 -> 13, of which waited for: 7 -> 8; matrix products, arithmetic and copies ran while one was open for 2% -> 2% of each run, Pallas kernels for 3% -> 3%
where the time goes in v6:
time: 65.9 us; the launch traced here: 65.7 us
  waiting for transfers between devices  36.9 us (56%)
  starting transfers between devices  16.6 us (25%)
  Pallas kernels  8.62 us (13%)
  between operations  2.09 us (3%)
  other arithmetic  1.38 us (2%)
    ppermute x1, waiting for transfers between devices, staged_body(): crossed = lax.ppermute(last, 'dp', mixed(7, 0))  9.81 us
    ppermute x1, waiting for transfers between devices, staged_body(): fa = lax.ppermute(fa, 'dp', mixed(6, 1))  9.28 us
    ppermute x1, waiting for transfers between devices, route(): return lambda parts: lax.ppermute(parts, ('dp', 'expert'), pairs)  6.09 us
    ppermute x1, waiting for transfers between devices, staged_body(): twin = lax.ppermute(posted, 'dp', flips(dp_count, square))  4.54 us
    ppermute x3, waiting for transfers between devices, staged_body(): raw[near] = lax.ppermute(raw[near], 'dp', flips(dp_count, near))  4.18 us
    ppermute x3, starting transfers between devices, staged_body(): raw[near] = lax.ppermute(raw[near], 'dp', flips(dp_count, near))  3.49 us
    ppermute x1, waiting for transfers between devices, staged_body(): above = lax.ppermute(upward, 'dp', flips(dp_count, 1))  2.75 us
    ppermute x1, starting transfers between devices, staged_body(): five = lax.ppermute(five, 'dp', mixed(3, 5))  2.43 us
  transfers between devices with their start and end apart: 13, of which 8 were waited for; matrix products, arithmetic and copies ran while one was open for 2% of the time, Pallas kernels for 3%

profile of v6, /device:TPU:16, one launch (start us, length us, event | category | flops | bytes accessed | tf_op | source)
XLA Modules:
  0.0 65.7 jit_solution(11131150651216185402)
XLA Ops:
  0.6 1.2 %pack_first.1 = (bf16[128,896]{1,0:T(8,128)(2,1)S(1)}, bf16[128,896]{1,0:T(8,128)(2,1)S(1)}, bf16[128,896]{1,0:T(8,128)(2,1)S(1)}) custom-call(bf16[1,1,1024,896]{3,2,1,0:T(8,128)(2,1)} %grads.3), custom_call_target="tpu_custom_call" | custom-call | tf_op jit(solution)/shard_map/pack_first/pallas_call | solution.py:179
  1.9 1.6 %pack_second.1 = (bf16[128,896]{1,0:T(8,128)(2,1)S(1)}, bf16[128,896]{1,0:T(8,128)(2,1)S(1)}, bf16[128,896]{1,0:T(8,128)(2,1)S(1)}, bf16[128,896]{1,0:T(8,128)(2...) custom-call(bf16[1,1,1024,896]{3,2,1,0:T(8,128)(2,1)} %grads.3, s32[8,128]{1,0:T(8,128)S(1)} %bitcast.3, ...), custom_call_target="tpu_custom_call" | custom-call | tf_op jit(solution)/shard_map/pack_second/pallas_call | solution.py:196
  3.6 4.5 %collective-permute-done.24.twin = s32[16,128]{1,0:T(8,128)S(1)} collective-permute-done((s32[16,128]{1,0:T(8,128)S(1)}, s32[16,128]{1,0:T(8,128)S(1)}, u32[]{:S(2)}, u32[]{:S(2)}) %collective-permute-start.24) | collective-permute-done | bytes 8224 | tf_op jit(solution)/shard_map/ppermute | solution.py:396
  8.1 1.6 %collective-permute-start.25 = (s32[8,128]{1,0:T(8,128)S(1)}, s32[8,128]{1,0:T(8,128)S(1)}, u32[]{:S(2)}, u32[]{:S(2)}) collective-permute-start(s32[8,128]{1,0:T(8,128)S(1)} %get-tuple-element.68), channel_id=1, source_target_pairs={{0,8},{4,12},{8,0},{12,4},{16,24},{20,28},{24,16},{28,20},{1,9},{5... | collective-permute-start | bytes 12296 | tf_op jit(solution)/shard_map/ppermute | solution.py:398
  9.8 1.5 %collective-permute-start.27 = (bf16[128,896]{1,0:T(8,128)(2,1)S(1)}, bf16[128,896]{1,0:T(8,128)(2,1)S(1)}, u32[]{:S(2)}, u32[]{:S(2)}) collective-permute-start(bf16[128,896]{1,0:T(8,128)(2,1)S(1)} %get-tuple-element.63.refs_0_), channel_id=1, source_target_pairs={{0,4},{4,0},{8,12},{12,8},{16,20},{20,16},{24,28},{28,24},{1,5},{5... | collective-permute-start | bytes 688136 | tf_op jit(solution)/shard_map/ppermute | solution.py:385
  11.8 1.5 %collective-permute-start.29 = (bf16[128,896]{1,0:T(8,128)(2,1)S(1)}, bf16[128,896]{1,0:T(8,128)(2,1)S(1)}, u32[]{:S(2)}, u32[]{:S(2)}) collective-permute-start(bf16[128,896]{1,0:T(8,128)(2,1)S(1)} %get-tuple-element.70), channel_id=1, source_target_pairs={{0,12},{4,8},{8,4},{12,0},{16,28},{20,24},{24,20},{28,16},{1,13},{... | collective-permute-start | bytes 688136 | tf_op jit(solution)/shard_map/ppermute | solution.py:385
  13.3 1.6 %collective-permute-start.26 = (s32[8,128]{1,0:T(8,128)S(1)}, s32[8,128]{1,0:T(8,128)S(1)}, u32[]{:S(2)}, u32[]{:S(2)}) collective-permute-start(s32[8,128]{1,0:T(8,128)S(1)} %pad_add_fusion.upward), channel_id=1, source_target_pairs={{0,4},{4,0},{8,12},{12,8},{16,20},{20,16},{24,28},{28,24},{1,5},{5... | collective-permute-start | bytes 12296 | tf_op jit(solution)/shard_map/ppermute | solution.py:401
  14.9 2.8 %collective-permute-done.26.above = s32[8,128]{1,0:T(8,128)S(1)} collective-permute-done((s32[8,128]{1,0:T(8,128)S(1)}, s32[8,128]{1,0:T(8,128)S(1)}, u32[]{:S(2)}, u32[]{:S(2)}) %collective-permute-start.26) | collective-permute-done | bytes 4128 | tf_op jit(solution)/shard_map/ppermute | solution.py:401
  17.7 1.7 %collective-permute-done.28.refs_2_ = bf16[128,896]{1,0:T(8,128)(2,1)S(1)} collective-permute-done((bf16[128,896]{1,0:T(8,128)(2,1)S(1)}, bf16[128,896]{1,0:T(8,128)(2,1)S(1)}, u32[]{:S(2)}, u32[]{:S(2)}) %collective-permute-start.28) | collective-permute-done | bytes 229408 | tf_op jit(solution)/shard_map/ppermute | solution.py:385
  19.4 2.4 %collective-permute-done.29.refs_3_ = bf16[128,896]{1,0:T(8,128)(2,1)S(1)} collective-permute-done((bf16[128,896]{1,0:T(8,128)(2,1)S(1)}, bf16[128,896]{1,0:T(8,128)(2,1)S(1)}, u32[]{:S(2)}, u32[]{:S(2)}) %collective-permute-start.29) | collective-permute-done | bytes 229408 | tf_op jit(solution)/shard_map/ppermute | solution.py:385
  21.8 1.7 %sum_near.1.own = bf16[136,896]{1,0:T(8,128)(2,1)S(1)} custom-call(s32[8,128]{1,0:T(8,128)S(1)} %get-tuple-element.67.mine, s32[8,128]{1,0:T(8,128)S(1)} %pad_add_fusion.upward, s32[8,128]{1,0:T(8,128)S(1)} %collective-permute-done.25.aside, s32[8,128]{1,0:T(8,128)S(1)} %collective-permute-done.26.above, bf16[128,896]{1,0:T(8,128)(2,1)S(1)} %get-tuple-element.69.refs_0_, ...), custom_call_target="tpu_custom_call" | custom-call | tf_op jit(solution)/shard_map/sum_near/pallas_call | solution.py:297
  25.1 1.6 %collective-permute-start.31 = (bf16[136,896]{1,0:T(8,128)(2,1)S(1)}, bf16[136,896]{1,0:T(8,128)(2,1)S(1)}, u32[]{:S(2)}, u32[]{:S(2)}) collective-permute-start(bf16[136,896]{1,0:T(8,128)(2,1)S(1)} %broadcast_select_fusion), channel_id=1, source_target_pairs={{0,2},{1,3},{2,0},{3,1},{4,6},{5,7},{6,4},{7,5},{8,10},{9,11},{10,... | collective-permute-start | bytes 731144 | tf_op jit(solution)/shard_map/ppermute | solution.py:409
  26.7 2.0 %collective-permute-start.34 = (bf16[128,896]{1,0:T(8,128)(2,1)S(1)}, bf16[128,896]{1,0:T(8,128)(2,1)S(1)}, u32[]{:S(2)}, u32[]{:S(2)}) collective-permute-start(bf16[128,896]{1,0:T(8,128)(2,1)S(1)} %get-tuple-element.72), channel_id=1, source_target_pairs={{0,16},{4,20},{8,0},{12,4},{16,24},{20,28},{24,8},{28,12},{1,17},{... | collective-permute-start | bytes 688136 | tf_op jit(solution)/shard_map/ppermute | solution.py:392
  28.7 2.4 %collective-permute-start.35 = (bf16[128,896]{1,0:T(8,128)(2,1)S(1)}, bf16[128,896]{1,0:T(8,128)(2,1)S(1)}, u32[]{:S(2)}, u32[]{:S(2)}) collective-permute-start(bf16[128,896]{1,0:T(8,128)(2,1)S(1)} %get-tuple-element.73), channel_id=1, source_target_pairs={{0,20},{4,16},{8,4},{12,0},{16,28},{20,24},{24,12},{28,8},{1,21},{... | collective-permute-start | bytes 688136 | tf_op jit(solution)/shard_map/ppermute | solution.py:393
  31.1 1.9 %collective-permute-start.32 = (bf16[128,896]{1,0:T(8,128)(2,1)S(1)}, bf16[128,896]{1,0:T(8,128)(2,1)S(1)}, u32[]{:S(2)}, u32[]{:S(2)}) collective-permute-start(bf16[128,896]{1,0:T(8,128)(2,1)S(1)} %get-tuple-element.71.refs_1_), channel_id=1, source_target_pairs={{8,20},{12,16},{16,12},{20,8},{9,21},{13,17},{17,13},{21,9},{10,22... | collective-permute-start | bytes 688136 | tf_op jit(solution)/shard_map/ppermute | solution.py:394
  33.0 0.7 %select_reduce_fusion = s32[]{:T(128)} fusion(s32[4]{0:T(128)S(1)} %copy-done.3, s32[4]{0:T(128)S(1)} %copy-done.1), kind=kLoop, calls=%fused_computation.2 | loop fusion | flops 79 | bytes 36 | tf_op jit(solution)/shard_map/reduce_sum | solution.py:379
  34.4 1.3 %noise.1.refs_0_ = bf16[4,128,896]{2,1,0:T(8,128)(2,1)S(1)} custom-call(s32[8,128]{1,0:T(8,128)S(1)} %get-tuple-element.67.mine, s32[8,128]{1,0:T(8,128)S(1)} %collective-permute-done.25.aside, s32[8,128]{1,0:T(8,128)S(1)} %collective-permute-done.26.above), custom_call_target="tpu_custom_call" | custom-call | tf_op jit(solution)/shard_map/noise/pallas_call | solution.py:242
  35.7 9.3 %collective-permute-done.33.refs_3_ = bf16[128,896]{1,0:T(8,128)(2,1)S(1)} collective-permute-done((bf16[128,896]{1,0:T(8,128)(2,1)S(1)}, bf16[128,896]{1,0:T(8,128)(2,1)S(1)}, u32[]{:S(2)}, u32[]{:S(2)}) %collective-permute-start.33) | collective-permute-done | bytes 229408 | tf_op jit(solution)/shard_map/ppermute | solution.py:391
  45.0 9.8 %collective-permute-done.32.refs_2_ = bf16[128,896]{1,0:T(8,128)(2,1)S(1)} collective-permute-done((bf16[128,896]{1,0:T(8,128)(2,1)S(1)}, bf16[128,896]{1,0:T(8,128)(2,1)S(1)}, u32[]{:S(2)}, u32[]{:S(2)}) %collective-permute-start.32) | collective-permute-done | bytes 229408 | tf_op jit(solution)/shard_map/ppermute | solution.py:394
  54.8 0.7 %sum_far.1 = bf16[128,896]{1,0:T(8,128)(2,1)S(1)} custom-call(s32[8,128]{1,0:T(8,128)S(1)} %get-tuple-element.67.mine, s32[8,128]{1,0:T(8,128)S(1)} %pad_add_fusion.upward, s32[8,128]{1,0:T(8,128)S(1)} %collective-permute-done.25.aside, s32[8,128]{1,0:T(8,128)S(1)} %collective-permute-done.26.above, bf16[4,128,896]{2,1,0:T(8,128)(2,1)S(1)} %noise.1.refs_0_, ...), custom_call_target="tpu_custom_call" | custom-call | tf_op jit(solution)/shard_map/sum_far/pallas_call | solution.py:297
  55.5 8.1 %conditional.1 = (bf16[128,896]{1,0:T(8,128)(2,1)}) conditional(s32[]{:T(128)} %clamp.3, bf16[128,896]{1,0:T(8,128)(2,1)S(1)} %sum_far.1, bf16[128,896]{1,0:T(8,128)(2,1)S(1)} %sum_far.1, bf16[128,896]{1,0:T(8,128)(2,1)S(1)} %sum_far.1, bf16[128,896]{1,0:T(8,128)(2,1)S(1)} %sum_far.1, ...), branch_computations={%region_2.3_spmd, %region_3.4_spmd, %region_4.5_spmd, %region_5.6_... | conditional | bytes 917552 | solution.py:422
  55.6 1.9 %collective-permute-start.20 = (bf16[128,896]{1,0:T(8,128)(2,1)S(1)}, bf16[128,896]{1,0:T(8,128)(2,1)}, u32[]{:S(2)}, u32[]{:S(2)}) collective-permute-start(bf16[128,896]{1,0:T(8,128)(2,1)S(1)} %param.20), channel_id=1, source_target_pairs={{0,27},{1,25},{2,24},{3,26},{4,31},{5,29},{6,28},{7,30},{8,11},{9,... | collective-permute-start | bytes 688136 | tf_op jit(solution)/shard_map/cond/branch_20_fun/ppermute | solution.py:419
  57.5 6.1 %collective-permute-done.20 = bf16[128,896]{1,0:T(8,128)(2,1)} collective-permute-done((bf16[128,896]{1,0:T(8,128)(2,1)S(1)}, bf16[128,896]{1,0:T(8,128)(2,1)}, u32[]{:S(2)}, u32[]{:S(2)}) %collective-permute-start.20) | collective-permute-done | bytes 229408 | tf_op jit(solution)/shard_map/cond/branch_20_fun/ppermute | solution.py:419
  63.6 2.1 %update.1 = (f32[1,128,896]{2,1,0:T(8,128)}, f32[1,128,896]{2,1,0:T(8,128)}, f32[1,1]{1,0:T(1,128)}) custom-call(s32[1,4]{1,0:T(1,128)S(1)} %bitcast.2, bf16[136,896]{1,0:T(8,128)(2,1)S(1)} %sum_near.1.own, bf16[136,896]{1,0:T(8,128)(2,1)S(1)} %collective-permute-done.30.beside, bf16[136,896]{1,0:T(8,128)(2,1)S(1)} %collective-permute-done.31.across, ...), custom_call_target="tpu_custom_call" | custom-call | tf_op jit(solution)/shard_map/update/pallas_call | solution.py:351
  (25 shorter events, 1.5 us)
Async XLA Ops:
  0.6 1.2 %copy-start.2 = (s32[1,1,1024]{2,1,0:T(1,128)S(1)}, s32[1,1,1024]{2,1,0:T(1,128)}, u32[]{:S(2)}) copy-start(s32[1,1,1024]{2,1,0:T(1,128)} %param.30) | copy-start | bytes 12292
  1.9 21.8 %copy-start.1 = (s32[4]{0:T(128)S(1)}, s32[4]{0:T(128)}, u32[]{:S(2)}) copy-start(s32[4]{0:T(128)} %param.31) | copy-start | bytes 52
  1.9 31.2 %copy-start.3 = (s32[4]{0:T(128)S(1)}, s32[4]{0:T(128)}, u32[]{:S(2)}) copy-start(s32[4]{0:T(128)} %constant.12.clone) | copy-start | bytes 52
  3.5 4.6 %collective-permute-start.24 = (s32[16,128]{1,0:T(8,128)S(1)}, s32[16,128]{1,0:T(8,128)S(1)}, u32[]{:S(2)}, u32[]{:S(2)}) collective-permute-start(s32[16,128]{1,0:T(8,128)S(1)} %get-tuple-element.66.posted), channel_id=1, source_target_pairs={{0,16},{4,20},{8,24},{12,28},{16,0},{20,4},{24,8},{28,12},{1,17},{... | collective-permute-start | bytes 24584 | tf_op jit(solution)/shard_map/ppermute | solution.py:396
  8.1 5.1 %collective-permute-start.25 = (s32[8,128]{1,0:T(8,128)S(1)}, s32[8,128]{1,0:T(8,128)S(1)}, u32[]{:S(2)}, u32[]{:S(2)}) collective-permute-start(s32[8,128]{1,0:T(8,128)S(1)} %get-tuple-element.68), channel_id=1, source_target_pairs={{0,8},{4,12},{8,0},{12,4},{16,24},{20,28},{24,16},{28,20},{1,9},{5... | collective-permute-start | bytes 12296 | tf_op jit(solution)/shard_map/ppermute | solution.py:398
  9.8 7.9 %collective-permute-start.27 = (bf16[128,896]{1,0:T(8,128)(2,1)S(1)}, bf16[128,896]{1,0:T(8,128)(2,1)S(1)}, u32[]{:S(2)}, u32[]{:S(2)}) collective-permute-start(bf16[128,896]{1,0:T(8,128)(2,1)S(1)} %get-tuple-element.63.refs_0_), channel_id=1, source_target_pairs={{0,4},{4,0},{8,12},{12,8},{16,20},{20,16},{24,28},{28,24},{1,5},{5... | collective-permute-start | bytes 688136 | tf_op jit(solution)/shard_map/ppermute | solution.py:385
  11.3 8.1 %collective-permute-start.28 = (bf16[128,896]{1,0:T(8,128)(2,1)S(1)}, bf16[128,896]{1,0:T(8,128)(2,1)S(1)}, u32[]{:S(2)}, u32[]{:S(2)}) collective-permute-start(bf16[128,896]{1,0:T(8,128)(2,1)S(1)} %get-tuple-element.64.refs_1_), channel_id=1, source_target_pairs={{0,8},{4,12},{8,0},{12,4},{16,24},{20,28},{24,16},{28,20},{1,9},{5... | collective-permute-start | bytes 688136 | tf_op jit(solution)/shard_map/ppermute | solution.py:385
  11.8 10.1 %collective-permute-start.29 = (bf16[128,896]{1,0:T(8,128)(2,1)S(1)}, bf16[128,896]{1,0:T(8,128)(2,1)S(1)}, u32[]{:S(2)}, u32[]{:S(2)}) collective-permute-start(bf16[128,896]{1,0:T(8,128)(2,1)S(1)} %get-tuple-element.70), channel_id=1, source_target_pairs={{0,12},{4,8},{8,4},{12,0},{16,28},{20,24},{24,20},{28,16},{1,13},{... | collective-permute-start | bytes 688136 | tf_op jit(solution)/shard_map/ppermute | solution.py:385
  13.3 4.3 %collective-permute-start.26 = (s32[8,128]{1,0:T(8,128)S(1)}, s32[8,128]{1,0:T(8,128)S(1)}, u32[]{:S(2)}, u32[]{:S(2)}) collective-permute-start(s32[8,128]{1,0:T(8,128)S(1)} %pad_add_fusion.upward), channel_id=1, source_target_pairs={{0,4},{4,0},{8,12},{12,8},{16,20},{20,16},{24,28},{28,24},{1,5},{5... | collective-permute-start | bytes 12296 | tf_op jit(solution)/shard_map/ppermute | solution.py:401
  23.5 1.6 %collective-permute-start.30 = (bf16[136,896]{1,0:T(8,128)(2,1)S(1)}, bf16[136,896]{1,0:T(8,128)(2,1)S(1)}, u32[]{:S(2)}, u32[]{:S(2)}) collective-permute-start(bf16[136,896]{1,0:T(8,128)(2,1)S(1)} %sum_near.1.own), channel_id=1, source_target_pairs={{0,1},{1,0},{2,3},{3,2},{4,5},{5,4},{6,7},{7,6},{8,9},{9,8},{10,11... | collective-permute-start | bytes 731144 | tf_op jit(solution)/shard_map/ppermute | solution.py:407
  24.9 38.7 %copy-start = (f32[1,128,896]{2,1,0:T(8,128)S(1)}, f32[1,128,896]{2,1,0:T(8,128)}, u32[]{:S(2)}) copy-start(f32[1,128,896]{2,1,0:T(8,128)} %weight.1) | copy-start | bytes 1376260
  25.1 38.5 %collective-permute-start.31 = (bf16[136,896]{1,0:T(8,128)(2,1)S(1)}, bf16[136,896]{1,0:T(8,128)(2,1)S(1)}, u32[]{:S(2)}, u32[]{:S(2)}) collective-permute-start(bf16[136,896]{1,0:T(8,128)(2,1)S(1)} %broadcast_select_fusion), channel_id=1, source_target_pairs={{0,2},{1,3},{2,0},{3,1},{4,6},{5,7},{6,4},{7,5},{8,10},{9,11},{10,... | collective-permute-start | bytes 731144 | tf_op jit(solution)/shard_map/ppermute | solution.py:409
  26.7 18.3 %collective-permute-start.33 = (bf16[128,896]{1,0:T(8,128)(2,1)S(1)}, bf16[128,896]{1,0:T(8,128)(2,1)S(1)}, u32[]{:S(2)}, u32[]{:S(2)}) collective-permute-start(bf16[128,896]{1,0:T(8,128)(2,1)S(1)} %get-tuple-element.65.refs_2_), channel_id=1, source_target_pairs={{0,4},{4,0},{8,16},{12,20},{16,8},{20,12},{24,28},{28,24},{1,5},{5... | collective-permute-start | bytes 688136 | tf_op jit(solution)/shard_map/ppermute | solution.py:391
  26.7 18.3 %collective-permute-start.34 = (bf16[128,896]{1,0:T(8,128)(2,1)S(1)}, bf16[128,896]{1,0:T(8,128)(2,1)S(1)}, u32[]{:S(2)}, u32[]{:S(2)}) collective-permute-start(bf16[128,896]{1,0:T(8,128)(2,1)S(1)} %get-tuple-element.72), channel_id=1, source_target_pairs={{0,16},{4,20},{8,0},{12,4},{16,24},{20,28},{24,8},{28,12},{1,17},{... | collective-permute-start | bytes 688136 | tf_op jit(solution)/shard_map/ppermute | solution.py:392
  28.7 16.3 %collective-permute-start.35 = (bf16[128,896]{1,0:T(8,128)(2,1)S(1)}, bf16[128,896]{1,0:T(8,128)(2,1)S(1)}, u32[]{:S(2)}, u32[]{:S(2)}) collective-permute-start(bf16[128,896]{1,0:T(8,128)(2,1)S(1)} %get-tuple-element.73), channel_id=1, source_target_pairs={{0,20},{4,16},{8,4},{12,0},{16,28},{20,24},{24,12},{28,8},{1,21},{... | collective-permute-start | bytes 688136 | tf_op jit(solution)/shard_map/ppermute | solution.py:393
  31.1 23.7 %collective-permute-start.32 = (bf16[128,896]{1,0:T(8,128)(2,1)S(1)}, bf16[128,896]{1,0:T(8,128)(2,1)S(1)}, u32[]{:S(2)}, u32[]{:S(2)}) collective-permute-start(bf16[128,896]{1,0:T(8,128)(2,1)S(1)} %get-tuple-element.71.refs_1_), channel_id=1, source_target_pairs={{8,20},{12,16},{16,12},{20,8},{9,21},{13,17},{17,13},{21,9},{10,22... | collective-permute-start | bytes 688136 | tf_op jit(solution)/shard_map/ppermute | solution.py:394
  55.6 8.0 %collective-permute-start.20 = (bf16[128,896]{1,0:T(8,128)(2,1)S(1)}, bf16[128,896]{1,0:T(8,128)(2,1)}, u32[]{:S(2)}, u32[]{:S(2)}) collective-permute-start(bf16[128,896]{1,0:T(8,128)(2,1)S(1)} %param.20), channel_id=1, source_target_pairs={{0,27},{1,25},{2,24},{3,26},{4,31},{5,29},{6,28},{7,30},{8,11},{9,... | collective-permute-start | bytes 688136 | tf_op jit(solution)/shard_map/cond/branch_20_fun/ppermute | solution.py:419

commit v7 on v6

--- a/solution.py
+++ b/solution.py
@@ -225,7 +225,7 @@
 
 def noise_kernel(mine, aside, above, out, codes):
     fill_codes(1, mine, aside, above, codes)
-    height, width = 16, out.shape[2]
+    height, width = 32, out.shape[2]
     columns = lax.broadcasted_iota(jnp.int32, (1, width), 1) * 747796405
 
     def step(index, carry):
@@ -265,7 +265,7 @@
     reached = jnp.where(lanes == target, counts, 0).astype(jnp.float32)
     exponent = jnp.max(reached, axis=1, keepdims=True).astype(jnp.int32) + (low_power - level_bits)
     inverse_step = power_of_two(-exponent)
-    height, width = 16, raws[0].shape[1]
+    height, width = 32, raws[0].shape[1]
     columns = lax.broadcasted_iota(jnp.int32, (1, width), 1) * 747796405
 
     def step(index, carry):
@@ -305,13 +305,52 @@
     )(*notes, *raws)
 
 
+def choose_kernel(slots, own, beside, out):
+    place = lax.axis_index("expert")
+    positions = lax.broadcasted_iota(jnp.int32, slots.shape, 1)
+    wanted = jnp.where(positions == place, slots[...], -1) == (place ^ 2)
+    holds = jnp.max(wanted.astype(jnp.float32), axis=1, keepdims=True)
+    height = 8
+
+    def step(index, carry):
+        span = pl.ds(pl.multiple_of(index * height, height), height)
+        held, swapped = own[span, :].astype(jnp.float32), beside[span, :].astype(jnp.float32)
+        out[span, :] = jnp.where(holds > 0, held, swapped).astype(out.dtype)
+        return carry
+
+    lax.fori_loop(0, out.shape[0] // height, step, 0)
+
+
+def choose(slots, own, beside):
+    vmem = pl.BlockSpec(memory_space=pltpu.VMEM)
+    return pl.pallas_call(
+        choose_kernel,
+        out_shape=jax.ShapeDtypeStruct(own.shape, own.dtype),
+        in_specs=[vmem] * 3,
+        out_specs=vmem,
+        compiler_params=pltpu.CompilerParams(vmem_limit_bytes=8 * 2**20),
+        name="choose",
+    )(slots[None], own, beside)
+
+
 def update_kernel(dp_count, slots, own, beside, across, arrived, weight, *refs):
-    mean, updated, step, means, news, size_out, sems, size_sem = refs
+    mean, updated, step, landed, means, news, size_out, sems, size_sem = refs
+    rows = arrived.shape[0]
+    parts = sems.shape[1]
+    height = rows // parts
+
+    def strip(part):
+        return pl.ds(pl.multiple_of(part * height, height), height)
+
+    def fetch(part):
+        return pltpu.make_async_copy(arrived.at[strip(part), :], landed.at[strip(part), :], sems.at[2, part])
+
+    for part in range(parts):
+        fetch(part).start()
     place = lax.axis_index("expert")
     positions = lax.broadcasted_iota(jnp.int32, slots.shape, 1)
     turns = jnp.where(slots[...] == place, positions ^ place, 0).astype(jnp.float32)
     turn = jnp.max(turns, axis=1, keepdims=True)
-    rows = arrived.shape[0]
 
     def nearby(span):
         held, swapped, crossed = (ref[span, :].astype(jnp.float32) for ref in (own, beside, across))
@@ -322,24 +361,32 @@
     size_copy = pltpu.make_async_copy(size_out, step, size_sem)
     size_copy.start()
     scale = size * (1.0 / dp_count)
-    parts = sems.shape[1]
-    height = rows // parts
-    copies = [size_copy]
-    for part in range(parts):
-        span = slice(part * height, (part + 1) * height)
-        averaged = (nearby(span) + arrived[span, :].astype(jnp.float32)) * scale
+
+    def copies(part):
+        span = strip(part)
+        return [
+            pltpu.make_async_copy(source.at[span, :], target.at[0, span, :], sems.at[number, part])
+            for number, (source, target) in enumerate(((means, mean), (news, updated)))
+        ]
+
+    def step_part(part, carry):
+        span = strip(part)
+        fetch(part).wait()
+        averaged = (nearby(span) + landed[span, :].astype(jnp.float32)) * scale
         means[span, :] = averaged
         news[span, :] = weight[0, span, :] - learn_rate * averaged
-        for number, (source, target) in enumerate(((means, mean), (news, updated))):
-            copy = pltpu.make_async_copy(
-                source.at[pl.ds(part * height, height), :],
-                target.at[0, pl.ds(part * height, height), :],
-                sems.at[number, part],
-            )
+        for copy in copies(part):
             copy.start()
-            copies.append(copy)
-    for copy in copies:
-        copy.wait()
+        return carry
+
+    def wait_part(part, carry):
+        for copy in copies(part):
+            copy.wait()
+        return carry
+
+    lax.fori_loop(0, parts, step_part, 0)
+    lax.fori_loop(0, parts, wait_part, 0)
+    size_copy.wait()
 
 
 def update(slots, own, beside, across, arrived, weight, dp_count):
@@ -351,13 +398,14 @@
     return pl.pallas_call(
         functools.partial(update_kernel, dp_count),
         out_shape=(block, block, jax.ShapeDtypeStruct((1, 1), jnp.float32)),
-        in_specs=[vmem] * 6,
+        in_specs=[vmem] * 4 + [hbm, vmem],
         out_specs=(hbm, hbm, hbm),
         scratch_shapes=[
+            pltpu.VMEM((rows, width), arrived.dtype),
             pltpu.VMEM((rows, width), jnp.float32),
             pltpu.VMEM((rows, width), jnp.float32),
             pltpu.VMEM((1, 1), jnp.float32),
-            pltpu.SemaphoreType.DMA((2, parts)),
+            pltpu.SemaphoreType.DMA((3, parts)),
             pltpu.SemaphoreType.DMA,
         ],
         compiler_params=pltpu.CompilerParams(vmem_limit_bytes=8 * 2**20),
@@ -370,7 +418,6 @@
     expert_count = lax.axis_size("expert")
     row_count, hidden = expert_grads.shape[2:]
     block_rows = row_count // dp_count
-    place = lax.axis_index("expert")
     offsets = round_offsets[0, 0].reshape(dp_count, block_rows)
 
     after = jnp.arange(expert_count)[None, :] > jnp.arange(expert_count)[:, None]
@@ -401,12 +448,9 @@
     above = lax.ppermute(upward, "dp", flips(dp_count, 1))
     noise = far_noise((mine, aside, above), block_rows, hidden)
 
-    wanted = slot_expert == (place ^ 2)
-    crossing = jnp.sum(jnp.where(wanted, jnp.arange(expert_count), 0)) == place
     own = sum_counts(0, (mine, upward, aside, above), raw, 8)
     beside = lax.ppermute(own, "expert", flips(expert_count, 1))
-    across_wants = jnp.where(crossing, own, beside)
-    across = lax.ppermute(across_wants, "expert", flips(expert_count, 2))
+    across = lax.ppermute(choose(slot_expert, own, beside), "expert", flips(expert_count, 2))
     raws = (noise, last, crossed, fa, four, five)
     message = sum_counts(1, (mine, upward, aside, above), raws, 0)
 

time: 65.9 us -> 65.5 us (level)
  waiting for transfers between devices: 36.9 us -> 38.3 us
  between operations: 2.09 us -> 1.42 us
  other arithmetic: 1.38 us -> 0.72 us
    ppermute x1, waiting for transfers between devices: 0.18 us -> 1.5 us  [staged_body(): beside = lax.ppermute(own, 'expert', flips(expert_count, 1))]
  transfers between devices with their start and end apart: 13 -> 13, of which waited for: 8 -> 8; matrix products, arithmetic and copies ran while one was open for 2% -> 1% of each run, Pallas kernels for 3% -> 3%
where the time goes in v7:
time: 65.5 us; the launch traced here: 65.3 us
  waiting for transfers between devices  38.3 us (58%)
  starting transfers between devices  16.6 us (25%)
  Pallas kernels  8.12 us (12%)
  between operations  1.42 us (2%)
  other arithmetic  0.72 us (1%)
    ppermute x1, waiting for transfers between devices, staged_body(): crossed = lax.ppermute(last, 'dp', mixed(7, 0))  9.73 us
    ppermute x1, waiting for transfers between devices, staged_body(): fa = lax.ppermute(fa, 'dp', mixed(6, 1))  9.48 us
    ppermute x1, waiting for transfers between devices, route(): return lambda parts: lax.ppermute(parts, ('dp', 'expert'), pairs)  6.09 us
    ppermute x1, waiting for transfers between devices, staged_body(): twin = lax.ppermute(posted, 'dp', flips(dp_count, square))  4.54 us
    ppermute x3, waiting for transfers between devices, staged_body(): raw[near] = lax.ppermute(raw[near], 'dp', flips(dp_count, near))  4.18 us
    ppermute x3, starting transfers between devices, staged_body(): raw[near] = lax.ppermute(raw[near], 'dp', flips(dp_count, near))  3.49 us
    ppermute x1, waiting for transfers between devices, staged_body(): above = lax.ppermute(upward, 'dp', flips(dp_count, 1))  2.75 us
    ppermute x1, starting transfers between devices, staged_body(): five = lax.ppermute(five, 'dp', mixed(3, 5))  2.43 us
  transfers between devices with their start and end apart: 13, of which 8 were waited for; matrix products, arithmetic and copies ran while one was open for 1% of the time, Pallas kernels for 3%

profile of v7, /device:TPU:16, one launch (start us, length us, event | category | flops | bytes accessed | tf_op | source)
XLA Modules:
  0.0 65.3 jit_solution(14046538828819710085)
XLA Ops:
  0.6 1.2 %pack_first.1 = (bf16[128,896]{1,0:T(8,128)(2,1)S(1)}, bf16[128,896]{1,0:T(8,128)(2,1)S(1)}, bf16[128,896]{1,0:T(8,128)(2,1)S(1)}) custom-call(bf16[1,1,1024,896]{3,2,1,0:T(8,128)(2,1)} %grads.3), custom_call_target="tpu_custom_call" | custom-call | tf_op jit(solution)/shard_map/pack_first/pallas_call | solution.py:179
  1.9 1.6 %pack_second.1 = (bf16[128,896]{1,0:T(8,128)(2,1)S(1)}, bf16[128,896]{1,0:T(8,128)(2,1)S(1)}, bf16[128,896]{1,0:T(8,128)(2,1)S(1)}, bf16[128,896]{1,0:T(8,128)(2...) custom-call(bf16[1,1,1024,896]{3,2,1,0:T(8,128)(2,1)} %grads.3, s32[8,128]{1,0:T(8,128)S(1)} %bitcast.4, ...), custom_call_target="tpu_custom_call" | custom-call | tf_op jit(solution)/shard_map/pack_second/pallas_call | solution.py:196
  3.6 4.5 %collective-permute-done.24.twin = s32[16,128]{1,0:T(8,128)S(1)} collective-permute-done((s32[16,128]{1,0:T(8,128)S(1)}, s32[16,128]{1,0:T(8,128)S(1)}, u32[]{:S(2)}, u32[]{:S(2)}) %collective-permute-start.24) | collective-permute-done | bytes 8224 | tf_op jit(solution)/shard_map/ppermute | solution.py:443
  8.1 1.6 %collective-permute-start.25 = (s32[8,128]{1,0:T(8,128)S(1)}, s32[8,128]{1,0:T(8,128)S(1)}, u32[]{:S(2)}, u32[]{:S(2)}) collective-permute-start(s32[8,128]{1,0:T(8,128)S(1)} %get-tuple-element.68), channel_id=1, source_target_pairs={{0,8},{4,12},{8,0},{12,4},{16,24},{20,28},{24,16},{28,20},{1,9},{5... | collective-permute-start | bytes 12296 | tf_op jit(solution)/shard_map/ppermute | solution.py:445
  9.8 1.5 %collective-permute-start.27 = (bf16[128,896]{1,0:T(8,128)(2,1)S(1)}, bf16[128,896]{1,0:T(8,128)(2,1)S(1)}, u32[]{:S(2)}, u32[]{:S(2)}) collective-permute-start(bf16[128,896]{1,0:T(8,128)(2,1)S(1)} %get-tuple-element.63.refs_0_), channel_id=1, source_target_pairs={{0,4},{4,0},{8,12},{12,8},{16,20},{20,16},{24,28},{28,24},{1,5},{5... | collective-permute-start | bytes 688136 | tf_op jit(solution)/shard_map/ppermute | solution.py:432
  11.8 1.5 %collective-permute-start.29 = (bf16[128,896]{1,0:T(8,128)(2,1)S(1)}, bf16[128,896]{1,0:T(8,128)(2,1)S(1)}, u32[]{:S(2)}, u32[]{:S(2)}) collective-permute-start(bf16[128,896]{1,0:T(8,128)(2,1)S(1)} %get-tuple-element.70), channel_id=1, source_target_pairs={{0,12},{4,8},{8,4},{12,0},{16,28},{20,24},{24,20},{28,16},{1,13},{... | collective-permute-start | bytes 688136 | tf_op jit(solution)/shard_map/ppermute | solution.py:432
  13.3 1.6 %collective-permute-start.26 = (s32[8,128]{1,0:T(8,128)S(1)}, s32[8,128]{1,0:T(8,128)S(1)}, u32[]{:S(2)}, u32[]{:S(2)}) collective-permute-start(s32[8,128]{1,0:T(8,128)S(1)} %pad_add_fusion.upward), channel_id=1, source_target_pairs={{0,4},{4,0},{8,12},{12,8},{16,20},{20,16},{24,28},{28,24},{1,5},{5... | collective-permute-start | bytes 12296 | tf_op jit(solution)/shard_map/ppermute | solution.py:448
  14.9 2.8 %collective-permute-done.26.above = s32[8,128]{1,0:T(8,128)S(1)} collective-permute-done((s32[8,128]{1,0:T(8,128)S(1)}, s32[8,128]{1,0:T(8,128)S(1)}, u32[]{:S(2)}, u32[]{:S(2)}) %collective-permute-start.26) | collective-permute-done | bytes 4128 | tf_op jit(solution)/shard_map/ppermute | solution.py:448
  17.7 1.7 %collective-permute-done.28.refs_2_ = bf16[128,896]{1,0:T(8,128)(2,1)S(1)} collective-permute-done((bf16[128,896]{1,0:T(8,128)(2,1)S(1)}, bf16[128,896]{1,0:T(8,128)(2,1)S(1)}, u32[]{:S(2)}, u32[]{:S(2)}) %collective-permute-start.28) | collective-permute-done | bytes 229408 | tf_op jit(solution)/shard_map/ppermute | solution.py:432
  19.4 2.4 %collective-permute-done.29.refs_3_ = bf16[128,896]{1,0:T(8,128)(2,1)S(1)} collective-permute-done((bf16[128,896]{1,0:T(8,128)(2,1)S(1)}, bf16[128,896]{1,0:T(8,128)(2,1)S(1)}, u32[]{:S(2)}, u32[]{:S(2)}) %collective-permute-start.29) | collective-permute-done | bytes 229408 | tf_op jit(solution)/shard_map/ppermute | solution.py:432
  21.8 1.5 %sum_near.1.own = bf16[136,896]{1,0:T(8,128)(2,1)S(1)} custom-call(s32[8,128]{1,0:T(8,128)S(1)} %get-tuple-element.67.mine, s32[8,128]{1,0:T(8,128)S(1)} %pad_add_fusion.upward, s32[8,128]{1,0:T(8,128)S(1)} %collective-permute-done.25.aside, s32[8,128]{1,0:T(8,128)S(1)} %collective-permute-done.26.above, bf16[128,896]{1,0:T(8,128)(2,1)S(1)} %get-tuple-element.69.refs_0_, ...), custom_call_target="tpu_custom_call" | custom-call | tf_op jit(solution)/shard_map/sum_near/pallas_call | solution.py:297
  23.4 1.5 %collective-permute-done.30.beside = bf16[136,896]{1,0:T(8,128)(2,1)S(1)} collective-permute-done((bf16[136,896]{1,0:T(8,128)(2,1)S(1)}, bf16[136,896]{1,0:T(8,128)(2,1)S(1)}, u32[]{:S(2)}, u32[]{:S(2)}) %collective-permute-start.30) | collective-permute-done | bytes 243744 | tf_op jit(solution)/shard_map/ppermute | solution.py:452
  25.1 1.6 %collective-permute-start.31 = (bf16[136,896]{1,0:T(8,128)(2,1)S(1)}, bf16[136,896]{1,0:T(8,128)(2,1)S(1)}, u32[]{:S(2)}, u32[]{:S(2)}) collective-permute-start(bf16[136,896]{1,0:T(8,128)(2,1)S(1)} %choose.1), channel_id=1, source_target_pairs={{0,2},{1,3},{2,0},{3,1},{4,6},{5,7},{6,4},{7,5},{8,10},{9,11},{10,... | collective-permute-start | bytes 731144 | tf_op jit(solution)/shard_map/ppermute | solution.py:453
  26.7 2.0 %collective-permute-start.34 = (bf16[128,896]{1,0:T(8,128)(2,1)S(1)}, bf16[128,896]{1,0:T(8,128)(2,1)S(1)}, u32[]{:S(2)}, u32[]{:S(2)}) collective-permute-start(bf16[128,896]{1,0:T(8,128)(2,1)S(1)} %get-tuple-element.72), channel_id=1, source_target_pairs={{0,16},{4,20},{8,0},{12,4},{16,24},{20,28},{24,8},{28,12},{1,17},{... | collective-permute-start | bytes 688136 | tf_op jit(solution)/shard_map/ppermute | solution.py:439
  28.7 2.4 %collective-permute-start.35 = (bf16[128,896]{1,0:T(8,128)(2,1)S(1)}, bf16[128,896]{1,0:T(8,128)(2,1)S(1)}, u32[]{:S(2)}, u32[]{:S(2)}) collective-permute-start(bf16[128,896]{1,0:T(8,128)(2,1)S(1)} %get-tuple-element.73), channel_id=1, source_target_pairs={{0,20},{4,16},{8,4},{12,0},{16,28},{20,24},{24,12},{28,8},{1,21},{... | collective-permute-start | bytes 688136 | tf_op jit(solution)/shard_map/ppermute | solution.py:440
  31.1 1.9 %collective-permute-start.32 = (bf16[128,896]{1,0:T(8,128)(2,1)S(1)}, bf16[128,896]{1,0:T(8,128)(2,1)S(1)}, u32[]{:S(2)}, u32[]{:S(2)}) collective-permute-start(bf16[128,896]{1,0:T(8,128)(2,1)S(1)} %get-tuple-element.71.refs_1_), channel_id=1, source_target_pairs={{8,20},{12,16},{16,12},{20,8},{9,21},{13,17},{17,13},{21,9},{10,22... | collective-permute-start | bytes 688136 | tf_op jit(solution)/shard_map/ppermute | solution.py:441
  33.0 0.7 %select_reduce_fusion = s32[]{:T(128)} fusion(s32[4]{0:T(128)S(1)} %copy-done.3, s32[4]{0:T(128)S(1)} %copy-done.1), kind=kLoop, calls=%fused_computation.1 | loop fusion | flops 79 | bytes 36 | tf_op jit(solution)/shard_map/reduce_sum | solution.py:426
  34.4 1.0 %noise.1.refs_0_ = bf16[4,128,896]{2,1,0:T(8,128)(2,1)S(1)} custom-call(s32[8,128]{1,0:T(8,128)S(1)} %get-tuple-element.67.mine, s32[8,128]{1,0:T(8,128)S(1)} %collective-permute-done.25.aside, s32[8,128]{1,0:T(8,128)S(1)} %collective-permute-done.26.above), custom_call_target="tpu_custom_call" | custom-call | tf_op jit(solution)/shard_map/noise/pallas_call | solution.py:242
  35.4 9.5 %collective-permute-done.33.refs_3_ = bf16[128,896]{1,0:T(8,128)(2,1)S(1)} collective-permute-done((bf16[128,896]{1,0:T(8,128)(2,1)S(1)}, bf16[128,896]{1,0:T(8,128)(2,1)S(1)}, u32[]{:S(2)}, u32[]{:S(2)}) %collective-permute-start.33) | collective-permute-done | bytes 229408 | tf_op jit(solution)/shard_map/ppermute | solution.py:438
  44.9 9.7 %collective-permute-done.32.refs_2_ = bf16[128,896]{1,0:T(8,128)(2,1)S(1)} collective-permute-done((bf16[128,896]{1,0:T(8,128)(2,1)S(1)}, bf16[128,896]{1,0:T(8,128)(2,1)S(1)}, u32[]{:S(2)}, u32[]{:S(2)}) %collective-permute-start.32) | collective-permute-done | bytes 229408 | tf_op jit(solution)/shard_map/ppermute | solution.py:441
  55.3 8.1 %conditional.1 = (bf16[128,896]{1,0:T(8,128)(2,1)}) conditional(s32[]{:T(128)} %clamp.3, bf16[128,896]{1,0:T(8,128)(2,1)S(1)} %sum_far.1, bf16[128,896]{1,0:T(8,128)(2,1)S(1)} %sum_far.1, bf16[128,896]{1,0:T(8,128)(2,1)S(1)} %sum_far.1, bf16[128,896]{1,0:T(8,128)(2,1)S(1)} %sum_far.1, ...), branch_computations={%region_1.2_spmd, %region_2.3_spmd, %region_3.4_spmd, %region_4.5_... | conditional | bytes 917552 | solution.py:466
  55.3 1.9 %collective-permute-start.20 = (bf16[128,896]{1,0:T(8,128)(2,1)S(1)}, bf16[128,896]{1,0:T(8,128)(2,1)}, u32[]{:S(2)}, u32[]{:S(2)}) collective-permute-start(bf16[128,896]{1,0:T(8,128)(2,1)S(1)} %param.20), channel_id=1, source_target_pairs={{0,27},{1,25},{2,24},{3,26},{4,31},{5,29},{6,28},{7,30},{8,11},{9,... | collective-permute-start | bytes 688136 | tf_op jit(solution)/shard_map/cond/branch_20_fun/ppermute | solution.py:463
  57.3 6.1 %collective-permute-done.20 = bf16[128,896]{1,0:T(8,128)(2,1)} collective-permute-done((bf16[128,896]{1,0:T(8,128)(2,1)S(1)}, bf16[128,896]{1,0:T(8,128)(2,1)}, u32[]{:S(2)}, u32[]{:S(2)}) %collective-permute-start.20) | collective-permute-done | bytes 229408 | tf_op jit(solution)/shard_map/cond/branch_20_fun/ppermute | solution.py:463
  63.4 1.9 %update.1 = (f32[1,128,896]{2,1,0:T(8,128)}, f32[1,128,896]{2,1,0:T(8,128)}, f32[1,1]{1,0:T(1,128)}) custom-call(s32[1,4]{1,0:T(1,128)S(1)} %bitcast.3, bf16[136,896]{1,0:T(8,128)(2,1)S(1)} %sum_near.1.own, bf16[136,896]{1,0:T(8,128)(2,1)S(1)} %collective-permute-done.30.beside, bf16[136,896]{1,0:T(8,128)(2,1)S(1)} %collective-permute-done.31.across, ...), custom_call_target="tpu_custom_call" | custom-call | tf_op jit(solution)/shard_map/update/pallas_call | solution.py:398
  (24 shorter events, 1.6 us)
Async XLA Ops:
  0.6 1.2 %copy-start.2 = (s32[1,1,1024]{2,1,0:T(1,128)S(1)}, s32[1,1,1024]{2,1,0:T(1,128)}, u32[]{:S(2)}) copy-start(s32[1,1,1024]{2,1,0:T(1,128)} %param.30) | copy-start | bytes 12292
  1.9 23.0 %copy-start.1 = (s32[4]{0:T(128)S(1)}, s32[4]{0:T(128)}, u32[]{:S(2)}) copy-start(s32[4]{0:T(128)} %param.31) | copy-start | bytes 52
  1.9 31.1 %copy-start.3 = (s32[4]{0:T(128)S(1)}, s32[4]{0:T(128)}, u32[]{:S(2)}) copy-start(s32[4]{0:T(128)} %constant.6.clone) | copy-start | bytes 52
  3.5 4.6 %collective-permute-start.24 = (s32[16,128]{1,0:T(8,128)S(1)}, s32[16,128]{1,0:T(8,128)S(1)}, u32[]{:S(2)}, u32[]{:S(2)}) collective-permute-start(s32[16,128]{1,0:T(8,128)S(1)} %get-tuple-element.66.posted), channel_id=1, source_target_pairs={{0,16},{4,20},{8,24},{12,28},{16,0},{20,4},{24,8},{28,12},{1,17},{... | collective-permute-start | bytes 24584 | tf_op jit(solution)/shard_map/ppermute | solution.py:443
  8.1 5.1 %collective-permute-start.25 = (s32[8,128]{1,0:T(8,128)S(1)}, s32[8,128]{1,0:T(8,128)S(1)}, u32[]{:S(2)}, u32[]{:S(2)}) collective-permute-start(s32[8,128]{1,0:T(8,128)S(1)} %get-tuple-element.68), channel_id=1, source_target_pairs={{0,8},{4,12},{8,0},{12,4},{16,24},{20,28},{24,16},{28,20},{1,9},{5... | collective-permute-start | bytes 12296 | tf_op jit(solution)/shard_map/ppermute | solution.py:445
  9.8 7.9 %collective-permute-start.27 = (bf16[128,896]{1,0:T(8,128)(2,1)S(1)}, bf16[128,896]{1,0:T(8,128)(2,1)S(1)}, u32[]{:S(2)}, u32[]{:S(2)}) collective-permute-start(bf16[128,896]{1,0:T(8,128)(2,1)S(1)} %get-tuple-element.63.refs_0_), channel_id=1, source_target_pairs={{0,4},{4,0},{8,12},{12,8},{16,20},{20,16},{24,28},{28,24},{1,5},{5... | collective-permute-start | bytes 688136 | tf_op jit(solution)/shard_map/ppermute | solution.py:432
  11.3 8.1 %collective-permute-start.28 = (bf16[128,896]{1,0:T(8,128)(2,1)S(1)}, bf16[128,896]{1,0:T(8,128)(2,1)S(1)}, u32[]{:S(2)}, u32[]{:S(2)}) collective-permute-start(bf16[128,896]{1,0:T(8,128)(2,1)S(1)} %get-tuple-element.64.refs_1_), channel_id=1, source_target_pairs={{0,8},{4,12},{8,0},{12,4},{16,24},{20,28},{24,16},{28,20},{1,9},{5... | collective-permute-start | bytes 688136 | tf_op jit(solution)/shard_map/ppermute | solution.py:432
  11.8 10.1 %collective-permute-start.29 = (bf16[128,896]{1,0:T(8,128)(2,1)S(1)}, bf16[128,896]{1,0:T(8,128)(2,1)S(1)}, u32[]{:S(2)}, u32[]{:S(2)}) collective-permute-start(bf16[128,896]{1,0:T(8,128)(2,1)S(1)} %get-tuple-element.70), channel_id=1, source_target_pairs={{0,12},{4,8},{8,4},{12,0},{16,28},{20,24},{24,20},{28,16},{1,13},{... | collective-permute-start | bytes 688136 | tf_op jit(solution)/shard_map/ppermute | solution.py:432
  13.3 4.3 %collective-permute-start.26 = (s32[8,128]{1,0:T(8,128)S(1)}, s32[8,128]{1,0:T(8,128)S(1)}, u32[]{:S(2)}, u32[]{:S(2)}) collective-permute-start(s32[8,128]{1,0:T(8,128)S(1)} %pad_add_fusion.upward), channel_id=1, source_target_pairs={{0,4},{4,0},{8,12},{12,8},{16,20},{20,16},{24,28},{28,24},{1,5},{5... | collective-permute-start | bytes 12296 | tf_op jit(solution)/shard_map/ppermute | solution.py:448
  23.3 1.6 %collective-permute-start.30 = (bf16[136,896]{1,0:T(8,128)(2,1)S(1)}, bf16[136,896]{1,0:T(8,128)(2,1)S(1)}, u32[]{:S(2)}, u32[]{:S(2)}) collective-permute-start(bf16[136,896]{1,0:T(8,128)(2,1)S(1)} %sum_near.1.own), channel_id=1, source_target_pairs={{0,1},{1,0},{2,3},{3,2},{4,5},{5,4},{6,7},{7,6},{8,9},{9,8},{10,11... | collective-permute-start | bytes 731144 | tf_op jit(solution)/shard_map/ppermute | solution.py:452
  24.9 38.5 %copy-start = (f32[1,128,896]{2,1,0:T(8,128)S(1)}, f32[1,128,896]{2,1,0:T(8,128)}, u32[]{:S(2)}) copy-start(f32[1,128,896]{2,1,0:T(8,128)} %weight.1) | copy-start | bytes 1376260
  25.1 38.2 %collective-permute-start.31 = (bf16[136,896]{1,0:T(8,128)(2,1)S(1)}, bf16[136,896]{1,0:T(8,128)(2,1)S(1)}, u32[]{:S(2)}, u32[]{:S(2)}) collective-permute-start(bf16[136,896]{1,0:T(8,128)(2,1)S(1)} %choose.1), channel_id=1, source_target_pairs={{0,2},{1,3},{2,0},{3,1},{4,6},{5,7},{6,4},{7,5},{8,10},{9,11},{10,... | collective-permute-start | bytes 731144 | tf_op jit(solution)/shard_map/ppermute | solution.py:453
  26.7 18.2 %collective-permute-start.33 = (bf16[128,896]{1,0:T(8,128)(2,1)S(1)}, bf16[128,896]{1,0:T(8,128)(2,1)S(1)}, u32[]{:S(2)}, u32[]{:S(2)}) collective-permute-start(bf16[128,896]{1,0:T(8,128)(2,1)S(1)} %get-tuple-element.65.refs_2_), channel_id=1, source_target_pairs={{0,4},{4,0},{8,16},{12,20},{16,8},{20,12},{24,28},{28,24},{1,5},{5... | collective-permute-start | bytes 688136 | tf_op jit(solution)/shard_map/ppermute | solution.py:438
  26.7 18.2 %collective-permute-start.34 = (bf16[128,896]{1,0:T(8,128)(2,1)S(1)}, bf16[128,896]{1,0:T(8,128)(2,1)S(1)}, u32[]{:S(2)}, u32[]{:S(2)}) collective-permute-start(bf16[128,896]{1,0:T(8,128)(2,1)S(1)} %get-tuple-element.72), channel_id=1, source_target_pairs={{0,16},{4,20},{8,0},{12,4},{16,24},{20,28},{24,8},{28,12},{1,17},{... | collective-permute-start | bytes 688136 | tf_op jit(solution)/shard_map/ppermute | solution.py:439
  28.7 16.2 %collective-permute-start.35 = (bf16[128,896]{1,0:T(8,128)(2,1)S(1)}, bf16[128,896]{1,0:T(8,128)(2,1)S(1)}, u32[]{:S(2)}, u32[]{:S(2)}) collective-permute-start(bf16[128,896]{1,0:T(8,128)(2,1)S(1)} %get-tuple-element.73), channel_id=1, source_target_pairs={{0,20},{4,16},{8,4},{12,0},{16,28},{20,24},{24,12},{28,8},{1,21},{... | collective-permute-start | bytes 688136 | tf_op jit(solution)/shard_map/ppermute | solution.py:440
  31.1 23.5 %collective-permute-start.32 = (bf16[128,896]{1,0:T(8,128)(2,1)S(1)}, bf16[128,896]{1,0:T(8,128)(2,1)S(1)}, u32[]{:S(2)}, u32[]{:S(2)}) collective-permute-start(bf16[128,896]{1,0:T(8,128)(2,1)S(1)} %get-tuple-element.71.refs_1_), channel_id=1, source_target_pairs={{8,20},{12,16},{16,12},{20,8},{9,21},{13,17},{17,13},{21,9},{10,22... | collective-permute-start | bytes 688136 | tf_op jit(solution)/shard_map/ppermute | solution.py:441
  55.3 8.0 %collective-permute-start.20 = (bf16[128,896]{1,0:T(8,128)(2,1)S(1)}, bf16[128,896]{1,0:T(8,128)(2,1)}, u32[]{:S(2)}, u32[]{:S(2)}) collective-permute-start(bf16[128,896]{1,0:T(8,128)(2,1)S(1)} %param.20), channel_id=1, source_target_pairs={{0,27},{1,25},{2,24},{3,26},{4,31},{5,29},{6,28},{7,30},{8,11},{9,... | collective-permute-start | bytes 688136 | tf_op jit(solution)/shard_map/cond/branch_20_fun/ppermute | solution.py:463

commit v8 on v7

--- a/solution.py
+++ b/solution.py
@@ -212,36 +212,31 @@
     return jnp.bitwise_and(jnp.right_shift(mixed, 12), 255).astype(jnp.float32) * (1.0 / 256.0)
 
 
-def fill_codes(far, mine, aside, above, codes):
-    rows = [mine[far : far + 1, :], above[far : far + 1, :]]
-    rows += [aside[far : far + 1, :], above[far + 2 : far + 3, :]]
-    if far:
-        inner = is_inner(lax.axis_index("dp")) == 1
-        here, y, z, diagonal = rows
-        rows = [jnp.where(inner, diagonal, here), jnp.where(inner, z, y)]
-        rows += [jnp.where(inner, here, z), jnp.where(inner, y, diagonal)]
-    codes[...] = jnp.transpose(jnp.concatenate(rows * 2)) * 747796405 + 1013904223
-
-
-def noise_kernel(mine, aside, above, out, codes):
-    fill_codes(1, mine, aside, above, codes)
+def fill_codes(rows, codes):
+    spare = [rows[0]] * (codes.shape[1] - len(rows))
+    codes[...] = jnp.transpose(jnp.concatenate(rows + spare)) * 747796405 + 1013904223
+
+
+def noise_kernel(picks, *refs):
+    notes, out, codes = refs[:-2], refs[-2], refs[-1]
+    fill_codes([notes[note][row : row + 1, :] for note, row in picks], codes)
     height, width = 32, out.shape[2]
     columns = lax.broadcasted_iota(jnp.int32, (1, width), 1) * 747796405
 
     def step(index, carry):
         span = pl.ds(pl.multiple_of(index * height, height), height)
-        for near in range(square):
-            out[near, span, :] = noise_of(codes[span, near : near + 1], columns).astype(jnp.bfloat16)
+        for slab in range(len(picks)):
+            out[slab, span, :] = noise_of(codes[span, slab : slab + 1], columns).astype(jnp.bfloat16)
         return carry
 
     lax.fori_loop(0, out.shape[1] // height, step, 0)
 
 
-def far_noise(notes, rows, width):
-    vmem = pl.BlockSpec(memory_space=pltpu.VMEM)
-    return pl.pallas_call(
-        noise_kernel,
-        out_shape=jax.ShapeDtypeStruct((square, rows, width), jnp.bfloat16),
+def draw_noise(picks, notes, rows, width):
+    vmem = pl.BlockSpec(memory_space=pltpu.VMEM)
+    return pl.pallas_call(
+        functools.partial(noise_kernel, picks),
+        out_shape=jax.ShapeDtypeStruct((len(picks), rows, width), jnp.bfloat16),
         in_specs=[vmem] * len(notes),
         out_specs=vmem,
         scratch_shapes=[pltpu.VMEM((rows, 2 * square), jnp.int32)],
@@ -250,32 +245,38 @@
     )(*notes)
 
 
-def sum_kernel(far, rows, mine, upward, aside, above, *refs):
+def sum_kernel(far, rows, upward, above, early, *refs):
     me = lax.axis_index("dp")
     inner = is_inner(me) == 1
     if far:
-        noise, stays, *raws, out = refs
+        late, stays, *raws, out = refs
         target = jnp.where(inner, me, me ^ 6)
     else:
         *raws, out, codes = refs
         target = me
-        fill_codes(0, mine, aside, above, codes)
+        fill_codes([above[0:1, :], above[2:3, :]], codes)
     counts = jnp.maximum(upward[square : square + 1, :], above[square : square + 1, :])
     lanes = lax.broadcasted_iota(jnp.int32, counts.shape, 1)
     reached = jnp.where(lanes == target, counts, 0).astype(jnp.float32)
     exponent = jnp.max(reached, axis=1, keepdims=True).astype(jnp.int32) + (low_power - level_bits)
     inverse_step = power_of_two(-exponent)
+    slabs = [early.at[2], early.at[3], late.at[0], late.at[1]] if far else []
     height, width = 32, raws[0].shape[1]
     columns = lax.broadcasted_iota(jnp.int32, (1, width), 1) * 747796405
 
     def step(index, carry):
         span = pl.ds(pl.multiple_of(index * height, height), height)
         total = jnp.zeros((height, width), jnp.float32)
+        if far:
+            here, z, y, diagonal = (slab[span, :].astype(jnp.float32) for slab in slabs)
+            chosen = ((diagonal, here), (z, y), (here, z), (y, diagonal))
+            noises = [jnp.where(inner, *pair) for pair in chosen]
+        else:
+            here, z = (early[slab, span, :].astype(jnp.float32) for slab in range(2))
+            y, diagonal = (noise_of(codes[span, column : column + 1], columns) for column in range(2))
+            noises = [here, y, z, diagonal]
         for near in range(square):
-            if far:
-                drawn = noise[near, span, :].astype(jnp.float32)
-            else:
-                drawn = noise_of(codes[span, near : near + 1], columns)
+            drawn = noises[near]
             values = raws[near][span, :].astype(jnp.float32)
             if far and near == 0:
                 values = jnp.where(inner, values, stays[span, :].astype(jnp.float32))
@@ -446,13 +447,15 @@
     levels = jnp.maximum(mine[square:], aside[square:])
     upward = jnp.concatenate([mine[2:square], aside[2:square], levels])
     above = lax.ppermute(upward, "dp", flips(dp_count, 1))
-    noise = far_noise((mine, aside, above), block_rows, hidden)
-
-    own = sum_counts(0, (mine, upward, aside, above), raw, 8)
+    picks = ((0, 0), (1, 0), (0, 1), (1, 1))
+    early = draw_noise(picks, (mine, aside), block_rows, hidden)
+    late = draw_noise(((0, 1), (0, 3)), (above,), block_rows, hidden)
+
+    own = sum_counts(0, (upward, above, early), raw, 8)
     beside = lax.ppermute(own, "expert", flips(expert_count, 1))
     across = lax.ppermute(choose(slot_expert, own, beside), "expert", flips(expert_count, 2))
-    raws = (noise, last, crossed, fa, four, five)
-    message = sum_counts(1, (mine, upward, aside, above), raws, 0)
+    raws = (late, last, crossed, fa, four, five)
+    message = sum_counts(1, (upward, above, early), raws, 0)
 
     def route(order):
         pairs = [

time: 65.5 us -> 62.1 us (0.948)
  the two profiles are of different devices: /device:TPU:16 before, /device:TPU:0 now
where the time goes in v8:
time: 62.1 us; the launch traced here: 61 us
  waiting for transfers between devices  25.8 us (42%)
  starting transfers between devices  22.7 us (37%)
  Pallas kernels  10.3 us (17%)
  between operations  1.42 us (2%)
  other arithmetic  0.72 us (1%)
    ppermute x1, waiting for transfers between devices, route(): return lambda parts: lax.ppermute(parts, ('dp', 'expert'), pairs)  9.32 us
    ppermute x1, starting transfers between devices, staged_body(): four = lax.ppermute(four, 'dp', mixed(2, 4))  5.34 us
    ppermute x3, waiting for transfers between devices, staged_body(): raw[near] = lax.ppermute(raw[near], 'dp', flips(dp_count, near))  4.18 us
    ppermute x1, waiting for transfers between devices, staged_body(): four = lax.ppermute(four, 'dp', mixed(2, 4))  4.16 us
    ppermute x1, starting transfers between devices, staged_body(): twin = lax.ppermute(posted, 'dp', flips(dp_count, square))  4.13 us
    ppermute x3, starting transfers between devices, staged_body(): raw[near] = lax.ppermute(raw[near], 'dp', flips(dp_count, near))  3.49 us
    ppermute x1, waiting for transfers between devices, staged_body(): five = lax.ppermute(five, 'dp', mixed(3, 5))  3.29 us
    pallas_call x2, Pallas kernels, sum_counts(): pl.pallas_call(functools.partial(sum_kernel, far, rows), out_shape=jax.Sh...  2.99 us
  transfers between devices with their start and end apart: 13, of which 8 were waited for; matrix products, arithmetic and copies ran while one was open for 1% of the time, Pallas kernels for 6%

profile of v8, /device:TPU:0, one launch (start us, length us, event | category | flops | bytes accessed | tf_op | source)
XLA Modules:
  0.0 61.0 jit_solution(8124007227624684053)
XLA Ops:
  0.6 1.2 %pack_first.1 = (bf16[128,896]{1,0:T(8,128)(2,1)S(1)}, bf16[128,896]{1,0:T(8,128)(2,1)S(1)}, bf16[128,896]{1,0:T(8,128)(2,1)S(1)}) custom-call(bf16[1,1,1024,896]{3,2,1,0:T(8,128)(2,1)} %grads.3), custom_call_target="tpu_custom_call" | custom-call | tf_op jit(solution)/shard_map/pack_first/pallas_call | solution.py:179
  1.9 2.3 %pack_second.1 = (bf16[128,896]{1,0:T(8,128)(2,1)S(1)}, bf16[128,896]{1,0:T(8,128)(2,1)S(1)}, bf16[128,896]{1,0:T(8,128)(2,1)}, bf16[128,896]{1,0:T(8,128)(2,1)}...) custom-call(bf16[1,1,1024,896]{3,2,1,0:T(8,128)(2,1)} %grads.3, s32[8,128]{1,0:T(8,128)S(1)} %bitcast.4, ...), custom_call_target="tpu_custom_call" | custom-call | tf_op jit(solution)/shard_map/pack_second/pallas_call | solution.py:196
  4.2 4.1 %collective-permute-start.24 = (s32[16,128]{1,0:T(8,128)S(1)}, s32[16,128]{1,0:T(8,128)S(1)}, u32[]{:S(2)}, u32[]{:S(2)}) collective-permute-start(s32[16,128]{1,0:T(8,128)S(1)} %get-tuple-element.66.posted), channel_id=1, source_target_pairs={{0,16},{4,20},{8,24},{12,28},{16,0},{20,4},{24,8},{28,12},{1,17},{... | collective-permute-start | bytes 24584 | tf_op jit(solution)/shard_map/ppermute | solution.py:444
  8.3 1.6 %collective-permute-done.24.twin = s32[16,128]{1,0:T(8,128)S(1)} collective-permute-done((s32[16,128]{1,0:T(8,128)S(1)}, s32[16,128]{1,0:T(8,128)S(1)}, u32[]{:S(2)}, u32[]{:S(2)}) %collective-permute-start.24) | collective-permute-done | bytes 8224 | tf_op jit(solution)/shard_map/ppermute | solution.py:444
  9.9 2.0 %collective-permute-start.25 = (s32[8,128]{1,0:T(8,128)S(1)}, s32[8,128]{1,0:T(8,128)S(1)}, u32[]{:S(2)}, u32[]{:S(2)}) collective-permute-start(s32[8,128]{1,0:T(8,128)S(1)} %get-tuple-element.68), channel_id=1, source_target_pairs={{0,8},{4,12},{8,0},{12,4},{16,24},{20,28},{24,16},{28,20},{1,9},{5... | collective-permute-start | bytes 12296 | tf_op jit(solution)/shard_map/ppermute | solution.py:446
  11.9 1.5 %collective-permute-start.27 = (bf16[128,896]{1,0:T(8,128)(2,1)S(1)}, bf16[128,896]{1,0:T(8,128)(2,1)S(1)}, u32[]{:S(2)}, u32[]{:S(2)}) collective-permute-start(bf16[128,896]{1,0:T(8,128)(2,1)S(1)} %get-tuple-element.63.refs_0_), channel_id=1, source_target_pairs={{0,4},{4,0},{8,12},{12,8},{16,20},{20,16},{24,28},{28,24},{1,5},{5... | collective-permute-start | bytes 688136 | tf_op jit(solution)/shard_map/ppermute | solution.py:433
  13.9 1.5 %collective-permute-start.29 = (bf16[128,896]{1,0:T(8,128)(2,1)S(1)}, bf16[128,896]{1,0:T(8,128)(2,1)S(1)}, u32[]{:S(2)}, u32[]{:S(2)}) collective-permute-start(bf16[128,896]{1,0:T(8,128)(2,1)S(1)} %get-tuple-element.70), channel_id=1, source_target_pairs={{0,12},{4,8},{8,4},{12,0},{16,28},{20,24},{24,20},{28,16},{1,13},{... | collective-permute-start | bytes 688136 | tf_op jit(solution)/shard_map/ppermute | solution.py:433
  15.4 1.6 %collective-permute-start.26 = (s32[8,128]{1,0:T(8,128)S(1)}, s32[8,128]{1,0:T(8,128)S(1)}, u32[]{:S(2)}, u32[]{:S(2)}) collective-permute-start(s32[8,128]{1,0:T(8,128)S(1)} %pad_add_fusion.upward), channel_id=1, source_target_pairs={{0,4},{4,0},{8,12},{12,8},{16,20},{20,16},{24,28},{28,24},{1,5},{5... | collective-permute-start | bytes 12296 | tf_op jit(solution)/shard_map/ppermute | solution.py:449
  17.0 1.0 %noise.2.early = bf16[4,128,896]{2,1,0:T(8,128)(2,1)S(1)} custom-call(s32[8,128]{1,0:T(8,128)S(1)} %get-tuple-element.67.refs_0_, s32[8,128]{1,0:T(8,128)S(1)} %collective-permute-done.25.refs_1_), custom_call_target="tpu_custom_call" | custom-call | tf_op jit(solution)/shard_map/noise/pallas_call | solution.py:237
  18.1 1.7 %collective-permute-done.26.above.refs_0_ = s32[8,128]{1,0:T(8,128)S(1)} collective-permute-done((s32[8,128]{1,0:T(8,128)S(1)}, s32[8,128]{1,0:T(8,128)S(1)}, u32[]{:S(2)}, u32[]{:S(2)}) %collective-permute-start.26) | collective-permute-done | bytes 4128 | tf_op jit(solution)/shard_map/ppermute | solution.py:449
  19.8 1.7 %collective-permute-done.28.refs_2_ = bf16[128,896]{1,0:T(8,128)(2,1)S(1)} collective-permute-done((bf16[128,896]{1,0:T(8,128)(2,1)S(1)}, bf16[128,896]{1,0:T(8,128)(2,1)S(1)}, u32[]{:S(2)}, u32[]{:S(2)}) %collective-permute-start.28) | collective-permute-done | bytes 229408 | tf_op jit(solution)/shard_map/ppermute | solution.py:433
  21.5 2.4 %collective-permute-done.29.refs_3_ = bf16[128,896]{1,0:T(8,128)(2,1)S(1)} collective-permute-done((bf16[128,896]{1,0:T(8,128)(2,1)S(1)}, bf16[128,896]{1,0:T(8,128)(2,1)S(1)}, u32[]{:S(2)}, u32[]{:S(2)}) %collective-permute-start.29) | collective-permute-done | bytes 229408 | tf_op jit(solution)/shard_map/ppermute | solution.py:433
  24.0 1.3 %sum_near.1.own = bf16[136,896]{1,0:T(8,128)(2,1)S(1)} custom-call(s32[8,128]{1,0:T(8,128)S(1)} %pad_add_fusion.upward, s32[8,128]{1,0:T(8,128)S(1)} %collective-permute-done.26.above.refs_0_, bf16[4,128,896]{2,1,0:T(8,128)(2,1)S(1)} %noise.2.early, bf16[128,896]{1,0:T(8,128)(2,1)S(1)} %get-tuple-element.69.refs_0_, ...), custom_call_target="tpu_custom_call" | custom-call | tf_op jit(solution)/shard_map/sum_near/pallas_call | solution.py:298
  25.3 1.5 %collective-permute-done.30.beside = bf16[136,896]{1,0:T(8,128)(2,1)S(1)} collective-permute-done((bf16[136,896]{1,0:T(8,128)(2,1)S(1)}, bf16[136,896]{1,0:T(8,128)(2,1)S(1)}, u32[]{:S(2)}, u32[]{:S(2)}) %collective-permute-start.30) | collective-permute-done | bytes 243744 | tf_op jit(solution)/shard_map/ppermute | solution.py:455
  27.1 1.6 %collective-permute-start.31 = (bf16[136,896]{1,0:T(8,128)(2,1)S(1)}, bf16[136,896]{1,0:T(8,128)(2,1)S(1)}, u32[]{:S(2)}, u32[]{:S(2)}) collective-permute-start(bf16[136,896]{1,0:T(8,128)(2,1)S(1)} %choose.1), channel_id=1, source_target_pairs={{0,2},{1,3},{2,0},{3,1},{4,6},{5,7},{6,4},{7,5},{8,10},{9,11},{10,... | collective-permute-start | bytes 731144 | tf_op jit(solution)/shard_map/ppermute | solution.py:456
  28.6 1.5 %collective-permute-start.33 = (bf16[128,896]{1,0:T(8,128)(2,1)S(1)}, bf16[128,896]{1,0:T(8,128)(2,1)S(1)}, u32[]{:S(2)}, u32[]{:S(2)}) collective-permute-start(bf16[128,896]{1,0:T(8,128)(2,1)S(1)} %get-tuple-element.65.refs_2_), channel_id=1, source_target_pairs={{0,4},{4,0},{8,16},{12,20},{16,8},{20,12},{24,28},{28,24},{1,5},{5... | collective-permute-start | bytes 688136 | tf_op jit(solution)/shard_map/ppermute | solution.py:439
  30.8 5.3 %collective-permute-start.34 = (bf16[128,896]{1,0:T(8,128)(2,1)}, bf16[128,896]{1,0:T(8,128)(2,1)S(1)}, u32[]{:S(2)}, u32[]{:S(2)}) collective-permute-start(bf16[128,896]{1,0:T(8,128)(2,1)} %get-tuple-element.72), channel_id=1, source_target_pairs={{0,16},{4,20},{8,0},{12,4},{16,24},{20,28},{24,8},{28,12},{1,17},{... | collective-permute-start | bytes 688136 | tf_op jit(solution)/shard_map/ppermute | solution.py:440
  38.3 4.2 %collective-permute-done.34.refs_4_ = bf16[128,896]{1,0:T(8,128)(2,1)S(1)} collective-permute-done((bf16[128,896]{1,0:T(8,128)(2,1)}, bf16[128,896]{1,0:T(8,128)(2,1)S(1)}, u32[]{:S(2)}, u32[]{:S(2)}) %collective-permute-start.34) | collective-permute-done | bytes 229408 | tf_op jit(solution)/shard_map/ppermute | solution.py:440
  42.4 3.3 %collective-permute-done.35.refs_5_ = bf16[128,896]{1,0:T(8,128)(2,1)} collective-permute-done((bf16[128,896]{1,0:T(8,128)(2,1)}, bf16[128,896]{1,0:T(8,128)(2,1)}, u32[]{:S(2)}, u32[]{:S(2)}) %collective-permute-start.35) | collective-permute-done | bytes 229408 | tf_op jit(solution)/shard_map/ppermute | solution.py:441
  45.7 1.7 %sum_far.1 = bf16[128,896]{1,0:T(8,128)(2,1)S(1)} custom-call(s32[8,128]{1,0:T(8,128)S(1)} %pad_add_fusion.upward, s32[8,128]{1,0:T(8,128)S(1)} %collective-permute-done.26.above.refs_0_, bf16[4,128,896]{2,1,0:T(8,128)(2,1)S(1)} %noise.2.early, bf16[2,128,896]{2,1,0:T(8,128)(2,1)S(1)} %noise.3.refs_0_, bf16[128,896]{1,0:T(8,128)(2,1)S(1)} %get-tuple-element.71.refs_1_, ...), custom_call_target="tpu_custom_call" | custom-call | tf_op jit(solution)/shard_map/sum_far/pallas_call | solution.py:298
  47.4 11.7 %conditional.1 = (bf16[128,896]{1,0:T(8,128)(2,1)}) conditional(s32[]{:T(128)} %clamp.3, bf16[128,896]{1,0:T(8,128)(2,1)S(1)} %sum_far.1, bf16[128,896]{1,0:T(8,128)(2,1)S(1)} %sum_far.1, bf16[128,896]{1,0:T(8,128)(2,1)S(1)} %sum_far.1, bf16[128,896]{1,0:T(8,128)(2,1)S(1)} %sum_far.1, ...), branch_computations={%region_1.2_spmd, %region_2.3_spmd, %region_3.4_spmd, %region_4.5_... | conditional | bytes 917552 | solution.py:469
  47.4 2.3 %collective-permute-start.20 = (bf16[128,896]{1,0:T(8,128)(2,1)S(1)}, bf16[128,896]{1,0:T(8,128)(2,1)}, u32[]{:S(2)}, u32[]{:S(2)}) collective-permute-start(bf16[128,896]{1,0:T(8,128)(2,1)S(1)} %param.20), channel_id=1, source_target_pairs={{0,27},{1,25},{2,24},{3,26},{4,31},{5,29},{6,28},{7,30},{8,11},{9,... | collective-permute-start | bytes 688136 | tf_op jit(solution)/shard_map/cond/branch_20_fun/ppermute | solution.py:466
  49.8 9.3 %collective-permute-done.20 = bf16[128,896]{1,0:T(8,128)(2,1)} collective-permute-done((bf16[128,896]{1,0:T(8,128)(2,1)S(1)}, bf16[128,896]{1,0:T(8,128)(2,1)}, u32[]{:S(2)}, u32[]{:S(2)}) %collective-permute-start.20) | collective-permute-done | bytes 229408 | tf_op jit(solution)/shard_map/cond/branch_20_fun/ppermute | solution.py:466
  59.1 1.9 %update.1 = (f32[1,128,896]{2,1,0:T(8,128)}, f32[1,128,896]{2,1,0:T(8,128)}, f32[1,1]{1,0:T(1,128)}) custom-call(s32[1,4]{1,0:T(1,128)S(1)} %bitcast.3, bf16[136,896]{1,0:T(8,128)(2,1)S(1)} %sum_near.1.own, bf16[136,896]{1,0:T(8,128)(2,1)S(1)} %collective-permute-done.30.beside, bf16[136,896]{1,0:T(8,128)(2,1)S(1)} %collective-permute-done.31.across, ...), custom_call_target="tpu_custom_call" | custom-call | tf_op jit(solution)/shard_map/update/pallas_call | solution.py:399
  (25 shorter events, 2.9 us)
Async XLA Ops:
  0.6 1.2 %copy-start.2 = (s32[1,1,1024]{2,1,0:T(1,128)S(1)}, s32[1,1,1024]{2,1,0:T(1,128)}, u32[]{:S(2)}) copy-start(s32[1,1,1024]{2,1,0:T(1,128)} %param.30) | copy-start | bytes 12292
  4.1 22.7 %copy-start.1 = (s32[4]{0:T(128)S(1)}, s32[4]{0:T(128)}, u32[]{:S(2)}) copy-start(s32[4]{0:T(128)} %param.31) | copy-start | bytes 52
  4.2 5.8 %collective-permute-start.24 = (s32[16,128]{1,0:T(8,128)S(1)}, s32[16,128]{1,0:T(8,128)S(1)}, u32[]{:S(2)}, u32[]{:S(2)}) collective-permute-start(s32[16,128]{1,0:T(8,128)S(1)} %get-tuple-element.66.posted), channel_id=1, source_target_pairs={{0,16},{4,20},{8,24},{12,28},{16,0},{20,4},{24,8},{28,12},{1,17},{... | collective-permute-start | bytes 24584 | tf_op jit(solution)/shard_map/ppermute | solution.py:444
  9.9 5.5 %collective-permute-start.25 = (s32[8,128]{1,0:T(8,128)S(1)}, s32[8,128]{1,0:T(8,128)S(1)}, u32[]{:S(2)}, u32[]{:S(2)}) collective-permute-start(s32[8,128]{1,0:T(8,128)S(1)} %get-tuple-element.68), channel_id=1, source_target_pairs={{0,8},{4,12},{8,0},{12,4},{16,24},{20,28},{24,16},{28,20},{1,9},{5... | collective-permute-start | bytes 12296 | tf_op jit(solution)/shard_map/ppermute | solution.py:446
  11.9 7.9 %collective-permute-start.27 = (bf16[128,896]{1,0:T(8,128)(2,1)S(1)}, bf16[128,896]{1,0:T(8,128)(2,1)S(1)}, u32[]{:S(2)}, u32[]{:S(2)}) collective-permute-start(bf16[128,896]{1,0:T(8,128)(2,1)S(1)} %get-tuple-element.63.refs_0_), channel_id=1, source_target_pairs={{0,4},{4,0},{8,12},{12,8},{16,20},{20,16},{24,28},{28,24},{1,5},{5... | collective-permute-start | bytes 688136 | tf_op jit(solution)/shard_map/ppermute | solution.py:433
  13.4 8.1 %collective-permute-start.28 = (bf16[128,896]{1,0:T(8,128)(2,1)S(1)}, bf16[128,896]{1,0:T(8,128)(2,1)S(1)}, u32[]{:S(2)}, u32[]{:S(2)}) collective-permute-start(bf16[128,896]{1,0:T(8,128)(2,1)S(1)} %get-tuple-element.64.refs_1_), channel_id=1, source_target_pairs={{0,8},{4,12},{8,0},{12,4},{16,24},{20,28},{24,16},{28,20},{1,9},{5... | collective-permute-start | bytes 688136 | tf_op jit(solution)/shard_map/ppermute | solution.py:433
  13.9 10.1 %collective-permute-start.29 = (bf16[128,896]{1,0:T(8,128)(2,1)S(1)}, bf16[128,896]{1,0:T(8,128)(2,1)S(1)}, u32[]{:S(2)}, u32[]{:S(2)}) collective-permute-start(bf16[128,896]{1,0:T(8,128)(2,1)S(1)} %get-tuple-element.70), channel_id=1, source_target_pairs={{0,12},{4,8},{8,4},{12,0},{16,28},{20,24},{24,20},{28,16},{1,13},{... | collective-permute-start | bytes 688136 | tf_op jit(solution)/shard_map/ppermute | solution.py:433
  15.4 20.7 %copy-start.3 = (s32[4]{0:T(128)S(1)}, s32[4]{0:T(128)}, u32[]{:S(2)}) copy-start(s32[4]{0:T(128)} %constant.6.clone) | copy-start | bytes 52
  15.4 4.3 %collective-permute-start.26 = (s32[8,128]{1,0:T(8,128)S(1)}, s32[8,128]{1,0:T(8,128)S(1)}, u32[]{:S(2)}, u32[]{:S(2)}) collective-permute-start(s32[8,128]{1,0:T(8,128)S(1)} %pad_add_fusion.upward), channel_id=1, source_target_pairs={{0,4},{4,0},{8,12},{12,8},{16,20},{20,16},{24,28},{28,24},{1,5},{5... | collective-permute-start | bytes 12296 | tf_op jit(solution)/shard_map/ppermute | solution.py:449
  25.3 1.6 %collective-permute-start.30 = (bf16[136,896]{1,0:T(8,128)(2,1)S(1)}, bf16[136,896]{1,0:T(8,128)(2,1)S(1)}, u32[]{:S(2)}, u32[]{:S(2)}) collective-permute-start(bf16[136,896]{1,0:T(8,128)(2,1)S(1)} %sum_near.1.own), channel_id=1, source_target_pairs={{0,1},{1,0},{2,3},{3,2},{4,5},{5,4},{6,7},{7,6},{8,9},{9,8},{10,11... | collective-permute-start | bytes 731144 | tf_op jit(solution)/shard_map/ppermute | solution.py:455
  26.8 32.3 %copy-start = (f32[1,128,896]{2,1,0:T(8,128)S(1)}, f32[1,128,896]{2,1,0:T(8,128)}, u32[]{:S(2)}) copy-start(f32[1,128,896]{2,1,0:T(8,128)} %weight.1) | copy-start | bytes 1376260
  27.1 32.0 %collective-permute-start.31 = (bf16[136,896]{1,0:T(8,128)(2,1)S(1)}, bf16[136,896]{1,0:T(8,128)(2,1)S(1)}, u32[]{:S(2)}, u32[]{:S(2)}) collective-permute-start(bf16[136,896]{1,0:T(8,128)(2,1)S(1)} %choose.1), channel_id=1, source_target_pairs={{0,2},{1,3},{2,0},{3,1},{4,6},{5,7},{6,4},{7,5},{8,10},{9,11},{10,... | collective-permute-start | bytes 731144 | tf_op jit(solution)/shard_map/ppermute | solution.py:456
  28.6 9.6 %collective-permute-start.33 = (bf16[128,896]{1,0:T(8,128)(2,1)S(1)}, bf16[128,896]{1,0:T(8,128)(2,1)S(1)}, u32[]{:S(2)}, u32[]{:S(2)}) collective-permute-start(bf16[128,896]{1,0:T(8,128)(2,1)S(1)} %get-tuple-element.65.refs_2_), channel_id=1, source_target_pairs={{0,4},{4,0},{8,16},{12,20},{16,8},{20,12},{24,28},{28,24},{1,5},{5... | collective-permute-start | bytes 688136 | tf_op jit(solution)/shard_map/ppermute | solution.py:439
  30.1 8.1 %collective-permute-start.32 = (bf16[128,896]{1,0:T(8,128)(2,1)S(1)}, bf16[128,896]{1,0:T(8,128)(2,1)S(1)}, u32[]{:S(2)}, u32[]{:S(2)}) collective-permute-start(bf16[128,896]{1,0:T(8,128)(2,1)S(1)} %get-tuple-element.71.refs_1_), channel_id=1, source_target_pairs={{8,20},{12,16},{16,12},{20,8},{9,21},{13,17},{17,13},{21,9},{10,22... | collective-permute-start | bytes 688136 | tf_op jit(solution)/shard_map/ppermute | solution.py:442
  30.8 11.6 %collective-permute-start.34 = (bf16[128,896]{1,0:T(8,128)(2,1)}, bf16[128,896]{1,0:T(8,128)(2,1)S(1)}, u32[]{:S(2)}, u32[]{:S(2)}) collective-permute-start(bf16[128,896]{1,0:T(8,128)(2,1)} %get-tuple-element.72), channel_id=1, source_target_pairs={{0,16},{4,20},{8,0},{12,4},{16,24},{20,28},{24,8},{28,12},{1,17},{... | collective-permute-start | bytes 688136 | tf_op jit(solution)/shard_map/ppermute | solution.py:440
  36.1 9.6 %collective-permute-start.35 = (bf16[128,896]{1,0:T(8,128)(2,1)}, bf16[128,896]{1,0:T(8,128)(2,1)}, u32[]{:S(2)}, u32[]{:S(2)}) collective-permute-start(bf16[128,896]{1,0:T(8,128)(2,1)} %get-tuple-element.73), channel_id=1, source_target_pairs={{0,20},{4,16},{8,4},{12,0},{16,28},{20,24},{24,12},{28,8},{1,21},{... | collective-permute-start | bytes 688136 | tf_op jit(solution)/shard_map/ppermute | solution.py:441
  47.4 11.7 %collective-permute-start.20 = (bf16[128,896]{1,0:T(8,128)(2,1)S(1)}, bf16[128,896]{1,0:T(8,128)(2,1)}, u32[]{:S(2)}, u32[]{:S(2)}) collective-permute-start(bf16[128,896]{1,0:T(8,128)(2,1)S(1)} %param.20), channel_id=1, source_target_pairs={{0,27},{1,25},{2,24},{3,26},{4,31},{5,29},{6,28},{7,30},{8,11},{9,... | collective-permute-start | bytes 688136 | tf_op jit(solution)/shard_map/cond/branch_20_fun/ppermute | solution.py:466
